TPU v7x, 64 devices: a 2x2x8 block of a 4x4x8 slice. The times are simulated.
64 devices in a mesh: req: 4 (over x, y), dap: 16 (over z, core).
Axes of the slice: x: 2, y: 2, z: 8, core: 2. Of those that a mesh axis runs over, the one named last changes fastest.
The devices are a block of a 4x4x8 slice.
Arguments:
- single: bfloat16 [1024, 384], P(('req', 'dap')), parts along dimension 0
- pair: bfloat16 [1024, 256, 128], P(('req', 'dap')), parts along dimension 0
- token_mask: int32 [1024], P(('req', 'dap')), parts along dimension 0
- tmo_proj: bfloat16 [2, 128, 512], replicated
- tmo_gate: bfloat16 [2, 128, 128], replicated
- tmo_out: bfloat16 [2, 128, 128], replicated
- tmi_proj: bfloat16 [2, 128, 512], replicated
- tmi_gate: bfloat16 [2, 128, 128], replicated
- tmi_out: bfloat16 [2, 128, 128], replicated
- tas_qkvg: bfloat16 [2, 128, 512], replicated
- tas_bias: bfloat16 [2, 128, 4], replicated
- tas_out: bfloat16 [2, 128, 128], replicated
- tae_qkvg: bfloat16 [2, 128, 512], replicated
- tae_bias: bfloat16 [2, 128, 4], replicated
- tae_out: bfloat16 [2, 128, 128], replicated
- pt_in: bfloat16 [2, 128, 1024], replicated
- pt_out: bfloat16 [2, 512, 128], replicated
- ap_qkvg: bfloat16 [2, 384, 1536], replicated
- ap_bias: bfloat16 [2, 128, 16], replicated
- ap_out: bfloat16 [2, 384, 384], replicated
- st_in: bfloat16 [2, 384, 3072], replicated
- st_out: bfloat16 [2, 1536, 384], replicated
Outputs:
- output 1: bfloat16 [1024, 384], P(('req', 'dap')), parts along dimension 0
- output 2: bfloat16 [1024, 256, 128], P(('req', 'dap')), parts along dimension 0
There are 4 independent parts. A program takes and returns all parts, laid end to end along the dimension named above; an argument that names none is the same for every part.
All inputs are finite; a program needn't handle non-finite values.
Results may differ from a plain program's by a relative error of at most 0.02.
Values are sent between devices in bfloat16 or wider.
A program may use at most 768 MiB of HBM per device.

v0:
```python
import jax
import jax.numpy as jnp
from jax import lax
from jax.sharding import PartitionSpec as P

EPS = 1e-5
NEG_BIG = 1e9
WEIGHT_NAMES = ('tmo_proj', 'tmo_gate', 'tmo_out', 'tmi_proj', 'tmi_gate', 'tmi_out', 'tas_qkvg', 'tas_bias', 'tas_out', 'tae_qkvg', 'tae_bias', 'tae_out', 'pt_in', 'pt_out', 'ap_qkvg', 'ap_bias', 'ap_out', 'st_in', 'st_out')


def layer_norm(values):
    values = values.astype(jnp.float32)
    centred = values - jnp.mean(values, axis=-1, keepdims=True)
    variance = jnp.mean(centred * centred, axis=-1, keepdims=True)
    return (centred * lax.rsqrt(variance + EPS)).astype(jnp.bfloat16)


def tri_mult_inputs(z_rows, row_mask, col_mask, w_proj, w_gate):
    normed = layer_norm(z_rows)
    projected = jnp.dot(normed, w_proj, preferred_element_type=jnp.float32)
    hidden = w_proj.shape[1] // 4
    pair_mask = (row_mask[:, None] * col_mask[None, :]).astype(jnp.float32)[:, :, None]
    left = (jax.nn.sigmoid(projected[..., hidden:2 * hidden]) * projected[..., :hidden] * pair_mask).astype(jnp.bfloat16)
    right = (jax.nn.sigmoid(projected[..., 3 * hidden:]) * projected[..., 2 * hidden:3 * hidden] * pair_mask).astype(jnp.bfloat16)
    gate = jax.nn.sigmoid(jnp.dot(normed, w_gate, preferred_element_type=jnp.float32))
    return left, right, gate


def tri_mult_finish(z_rows, product, gate, w_out):
    update = jnp.dot(layer_norm(product), w_out, preferred_element_type=jnp.float32)
    return (z_rows.astype(jnp.float32) + gate * update).astype(jnp.bfloat16)


def pair_bias_of(normed, w_bias):
    return jnp.dot(normed, w_bias, preferred_element_type=jnp.float32).astype(jnp.bfloat16)


def tri_attention(z_rows, normed, bias_full, key_mask, w_qkvg, w_out):
    heads = bias_full.shape[-1]
    rows = z_rows.shape[0]
    width = z_rows.shape[1]
    head_dim = w_qkvg.shape[1] // (4 * heads)
    projected = jnp.dot(normed, w_qkvg, preferred_element_type=jnp.float32).reshape(rows, width, 4, heads, head_dim)
    query_all = projected[:, :, 0].astype(jnp.bfloat16)
    key_all = projected[:, :, 1].astype(jnp.bfloat16)
    value_all = projected[:, :, 2].astype(jnp.bfloat16)
    gate = jax.nn.sigmoid(projected[:, :, 3])
    bias_hjk = jnp.moveaxis(bias_full, -1, 0).astype(jnp.float32) + (key_mask.astype(jnp.float32) - 1.0) * NEG_BIG
    scale = head_dim ** -0.5

    def one_row(row_in):
        q_row, k_row, v_row = row_in
        logits = jnp.einsum('jhd,khd->hjk', q_row, k_row, preferred_element_type=jnp.float32) * scale + bias_hjk
        soft_scores = jax.nn.softmax(logits, axis=-1).astype(jnp.bfloat16)
        return jnp.einsum('hjk,khd->jhd', soft_scores, v_row, preferred_element_type=jnp.float32)

    attended = lax.map(one_row, (query_all, key_all, value_all))
    merged = (attended * gate).astype(jnp.bfloat16).reshape(rows, width, heads * head_dim)
    update = jnp.dot(merged, w_out, preferred_element_type=jnp.float32)
    return (z_rows.astype(jnp.float32) + update).astype(jnp.bfloat16)


def transition(act_in, w_in, w_out):
    hidden = w_out.shape[0]
    projected = jnp.dot(layer_norm(act_in), w_in, preferred_element_type=jnp.float32)
    inner = (jax.nn.silu(projected[..., :hidden]) * projected[..., hidden:]).astype(jnp.bfloat16)
    return (act_in.astype(jnp.float32) + jnp.dot(inner, w_out, preferred_element_type=jnp.float32)).astype(jnp.bfloat16)


def single_inputs(s_rows, w_qkvg, heads):
    rows = s_rows.shape[0]
    head_dim = w_qkvg.shape[1] // (4 * heads)
    projected = jnp.dot(layer_norm(s_rows), w_qkvg, preferred_element_type=jnp.float32).reshape(rows, 4, heads, head_dim)
    return projected[:, 0].astype(jnp.bfloat16), projected[:, 1].astype(jnp.bfloat16), projected[:, 2].astype(jnp.bfloat16), jax.nn.sigmoid(projected[:, 3])


def single_attention(s_rows, query, gate, key_all, value_all, pair_bias, key_mask, w_out):
    scale = query.shape[-1] ** -0.5
    logits = jnp.einsum('ihd,jhd->ihj', query, key_all, preferred_element_type=jnp.float32) * scale + pair_bias.astype(jnp.float32) + (key_mask.astype(jnp.float32) - 1.0) * NEG_BIG
    soft_scores = jax.nn.softmax(logits, axis=-1).astype(jnp.bfloat16)
    attended = jnp.einsum('ihj,jhd->ihd', soft_scores, value_all, preferred_element_type=jnp.float32)
    merged = (attended * gate).astype(jnp.bfloat16).reshape(s_rows.shape[0], -1)
    update = jnp.dot(merged, w_out, preferred_element_type=jnp.float32)
    return (s_rows.astype(jnp.float32) + update).astype(jnp.bfloat16)


def transpose_pairs(block_rows):
    moved = lax.all_to_all(block_rows, 'dap', 1, 0, tiled=True)
    return jnp.swapaxes(moved, 0, 1)


def run_block(single, pair, mask_rows, mask_all, layer):
    left, right, gate = tri_mult_inputs(pair, mask_rows, mask_all, layer['tmo_proj'], layer['tmo_gate'])
    right_all = lax.all_gather(right, 'dap', tiled=True)
    product = jnp.einsum('ikc,jkc->ijc', left, right_all, preferred_element_type=jnp.float32)
    pair = tri_mult_finish(pair, product, gate, layer['tmo_out'])
    left, right, gate = tri_mult_inputs(pair, mask_rows, mask_all, layer['tmi_proj'], layer['tmi_gate'])
    left_cols = transpose_pairs(left)
    right_all = lax.all_gather(right, 'dap', tiled=True)
    product = jnp.einsum('ikc,kjc->ijc', left_cols, right_all, preferred_element_type=jnp.float32)
    pair = tri_mult_finish(pair, product, gate, layer['tmi_out'])
    normed = layer_norm(pair)
    bias_all = lax.all_gather(pair_bias_of(normed, layer['tas_bias']), 'dap', tiled=True)
    pair = tri_attention(pair, normed, bias_all, mask_all, layer['tas_qkvg'], layer['tas_out'])
    pair_cols = transpose_pairs(pair)
    normed = layer_norm(pair_cols)
    bias_all = lax.all_gather(pair_bias_of(normed, layer['tae_bias']), 'dap', tiled=True)
    pair_cols = tri_attention(pair_cols, normed, bias_all, mask_all, layer['tae_qkvg'], layer['tae_out'])
    pair = transpose_pairs(pair_cols)
    pair = transition(pair, layer['pt_in'], layer['pt_out'])
    heads = layer['ap_bias'].shape[1]
    query, key_rows, value_rows, gate = single_inputs(single, layer['ap_qkvg'], heads)
    key_all = lax.all_gather(key_rows, 'dap', tiled=True)
    value_all = lax.all_gather(value_rows, 'dap', tiled=True)
    pair_bias = jnp.einsum('ijc,ch->ihj', layer_norm(pair), layer['ap_bias'], preferred_element_type=jnp.float32).astype(jnp.bfloat16)
    single = single_attention(single, query, gate, key_all, value_all, pair_bias, mask_all, layer['ap_out'])
    single = transition(single, layer['st_in'], layer['st_out'])
    return single, pair


def solution(mesh):
    row_spec = P(('req', 'dap'))
    single_spec = P(('req', 'dap'), None)
    pair_spec = P(('req', 'dap'), None, None)

    def local_program(single, pair, token_mask, *weights):
        mask_all = lax.all_gather(token_mask, 'dap', tiled=True)
        for layer_idx in range(weights[0].shape[0]):
            layer = {name: stack[layer_idx] for name, stack in zip(WEIGHT_NAMES, weights)}
            single, pair = run_block(single, pair, token_mask, mask_all, layer)
        return single, pair

    return jax.shard_map(local_program, mesh=mesh, in_specs=(single_spec, pair_spec, row_spec) + (P(),) * len(WEIGHT_NAMES), out_specs=(single_spec, pair_spec), check_vma=False)
```

profile of v0, /device:TPU:21, one launch (start us, length us, event | category | flops | bytes accessed | tf_op | source)
XLA Modules:
  0.0 1311.4 jit_solution(3365644654845977003)
XLA Ops:
  10.9 16.1 %all-reduce = s32[256]{0:T(256)S(1)} all-reduce(s32[256]{0:T(256)S(1)} %dynamic-update-slice), channel_id=1, replica_groups=mesh['req'=4,'dap'=16] {'dap'}, use_global_device_ids=true, to_apply=%add | all-reduce | flops 256 | bytes 2048
  31.5 91.8 %all-gather.9.cloned.1.call-done = bf16[256,256,128]{2,1,0:T(8,128)(2,1)} async-done(((bf16[16,256,128]{2,1,0:T(8,128)(2,1)}), bf16[256,256,128]{2,1,0:T(8,128)(2,1)}) %all-gather.9.cloned.1.call-update) | async-done | bytes 16777232 | tf_op jit(solution)/shard_map/all_gather | solution.py:94
  123.3 22.1 %copy.325 = bf16[256,256,128]{1,0,2:T(8,128)(2,1)} copy(bf16[256,256,128]{2,1,0:T(8,128)(2,1)} %all-gather.9.cloned.1.call-done) | data formatting | bytes 33554432 | tf_op jit(solution)/shard_map/all_gather | solution.py:94
  145.4 8.1 bitcast_reduce_fusion.7
  163.6 5.6 all-to-all-start
  169.4 36.9 %all-to-all-done = bf16[16,256,128]{2,0,1:T(8,128)(2,1)S(1)} async-done(((bf16[16,256,128]{2,0,1:T(8,128)(2,1)}), bf16[16,256,128]{2,0,1:T(8,128)(2,1)S(1)}, u32[]{:S(2)}, u32[]{:S(2)}) %all-to-all-start) | async-done | bytes 1048608 | tf_op jit(solution)/shard_map/all_to_all | solution.py:88
  207.8 66.9 %all-gather.11.cloned.1.call-done = bf16[256,256,128]{2,1,0:T(8,128)(2,1)} async-done(((bf16[16,256,128]{2,1,0:T(8,128)(2,1)}), bf16[256,256,128]{2,1,0:T(8,128)(2,1)}) %all-gather.11.cloned.1.call-update) | async-done | bytes 16777232 | tf_op jit(solution)/shard_map/all_gather | solution.py:99
  274.7 22.1 %copy.340 = bf16[256,256,128]{1,0,2:T(8,128)(2,1)} copy(bf16[256,256,128]{2,1,0:T(8,128)(2,1)} %all-gather.11.cloned.1.call-done) | data formatting | bytes 33554432 | tf_op jit(solution)/shard_map/all_gather | solution.py:99
  296.8 8.1 bitcast_reduce_fusion.6
  308.7 17.1 %all_gather.44 = bf16[256,256,4]{1,2,0:T(4,128)(2,1)S(1)} all-gather(bf16[16,256,4]{1,2,0:T(4,128)(2,1)S(1)} %convolution_convert_fusion.3), channel_id=1, replica_groups=mesh['req'=4,'dap'=16] {'dap'}, dimensions={0}, use_global_device_ids=true | all-gather | bytes 557056 | tf_op jit(solution)/shard_map/all_gather | solution.py:103
  326.4 4.5 fusion.419
  334.3 71.3 %while.40 = (s32[]{:T(128)}, f32[16,256,4,32]{1,3,2,0:T(8,128)}, bf16[16,256,4,32]{1,3,2,0:T(8,128)(2,1)}, bf16[16,256,4,32]{1,3,2,0:T(8,128)(2,1)}, bf16[16,256...) while((s32[]{:T(128)}, f32[16,256,4,32]{1,3,2,0:T(8,128)}, ...), condition=%wide.region_15.16_spmd, body=%wide.region_12.15_spmd.sunk | while | flops 52692480 | bytes 5712973 | solution.py:57
  405.7 2.8 fusion.192
  410.8 5.8 all-to-all-start.1
  417.7 26.8 %all-to-all-done.1 = bf16[16,256,128]{2,0,1:T(8,128)(2,1)S(1)} async-done(((bf16[16,256,128]{2,0,1:T(8,128)(2,1)}), bf16[16,256,128]{2,0,1:T(8,128)(2,1)S(1)}, u32[]{:S(2)}, u32[]{:S(2)}) %all-to-all-start.1) | async-done | bytes 1048608 | tf_op jit(solution)/shard_map/all_to_all | solution.py:88
  449.7 4.5 fusion.420
  456.3 16.0 %all_gather.45 = bf16[256,256,4]{1,2,0:T(4,128)(2,1)S(1)} all-gather(bf16[16,256,4]{1,2,0:T(4,128)(2,1)S(1)} %convolution_convert_fusion.2), channel_id=1, replica_groups=mesh['req'=4,'dap'=16] {'dap'}, dimensions={0}, use_global_device_ids=true | all-gather | bytes 557056 | tf_op jit(solution)/shard_map/all_gather | solution.py:107
  476.8 101.7 %while.41 = (s32[]{:T(128)}, f32[16,256,4,32]{1,3,2,0:T(8,128)}, bf16[16,256,4,32]{1,3,2,0:T(8,128)(2,1)}, bf16[16,256,4,32]{1,3,2,0:T(8,128)(2,1)}, bf16[16,256...) while((s32[]{:T(128)}, f32[16,256,4,32]{1,3,2,0:T(8,128)}, ...), condition=%wide.region_21.22_spmd, body=%wide.region_18.21_spmd.sunk | while | flops 52692480 | bytes 5712973 | solution.py:57
  578.5 2.8 fusion.193
  582.5 32.7 %all_to_all.72 = bf16[16,256,128]{2,0,1:T(8,128)(2,1)S(1)} all-to-all(bf16[16,256,128]{2,0,1:T(8,128)(2,1)S(1)} %copy.356), channel_id=1, replica_groups=mesh['req'=4,'dap'=16] {'dap'}, dimensions={1} | all-to-all | bytes 2097152 | tf_op jit(solution)/shard_map/all_to_all | solution.py:88
  622.7 2.9 convert_reduce_fusion.2
  631.6 89.5 %all-gather.13.cloned.1.call-done = bf16[256,256,128]{2,1,0:T(8,128)(2,1)} async-done(((bf16[16,256,128]{2,1,0:T(8,128)(2,1)}), bf16[256,256,128]{2,1,0:T(8,128)(2,1)}) %all-gather.13.cloned.1.call-update) | async-done | bytes 16777232 | tf_op jit(solution)/shard_map/all_gather | solution.py:94
  721.1 22.1 %copy.376 = bf16[256,256,128]{1,0,2:T(8,128)(2,1)} copy(bf16[256,256,128]{2,1,0:T(8,128)(2,1)} %all-gather.13.cloned.1.call-done) | data formatting | bytes 33554432 | tf_op jit(solution)/shard_map/all_gather | solution.py:94
  743.2 8.1 bitcast_reduce_fusion.3
  761.8 5.2 all-to-all-start.3
  767.2 2.8 slice_bitcast_fusion
  771.7 32.5 %all-to-all-done.3 = bf16[16,256,128]{2,0,1:T(8,128)(2,1)S(1)} async-done(((bf16[16,256,128]{2,0,1:T(8,128)(2,1)}), bf16[16,256,128]{2,0,1:T(8,128)(2,1)S(1)}, u32[]{:S(2)}, u32[]{:S(2)}) %all-to-all-start.3) | async-done | bytes 1048608 | tf_op jit(solution)/shard_map/all_to_all | solution.py:88
  805.7 67.2 %all-gather.15.cloned.1.call-done = bf16[256,256,128]{2,1,0:T(8,128)(2,1)} async-done(((bf16[16,256,128]{2,1,0:T(8,128)(2,1)}), bf16[256,256,128]{2,1,0:T(8,128)(2,1)}) %all-gather.15.cloned.1.call-update) | async-done | bytes 16777232 | tf_op jit(solution)/shard_map/all_gather | solution.py:99
  873.0 22.1 %copy.391 = bf16[256,256,128]{1,0,2:T(8,128)(2,1)} copy(bf16[256,256,128]{2,1,0:T(8,128)(2,1)} %all-gather.15.cloned.1.call-done) | data formatting | bytes 33554432 | tf_op jit(solution)/shard_map/all_gather | solution.py:99
  895.1 8.1 bitcast_reduce_fusion.2
  907.3 17.2 %all_gather.50 = bf16[256,256,4]{1,2,0:T(4,128)(2,1)S(1)} all-gather(bf16[16,256,4]{1,2,0:T(4,128)(2,1)S(1)} %convolution_convert_fusion.1), channel_id=1, replica_groups=mesh['req'=4,'dap'=16] {'dap'}, dimensions={0}, use_global_device_ids=true | all-gather | bytes 557056 | tf_op jit(solution)/shard_map/all_gather | solution.py:103
  925.0 4.5 fusion.425
  933.0 71.3 %while.42 = (s32[]{:T(128)}, f32[16,256,4,32]{1,3,2,0:T(8,128)}, bf16[16,256,4,32]{1,3,2,0:T(8,128)(2,1)}, bf16[16,256,4,32]{1,3,2,0:T(8,128)(2,1)}, bf16[16,256...) while((s32[]{:T(128)}, f32[16,256,4,32]{1,3,2,0:T(8,128)}, ...), condition=%wide.region_43.44_spmd, body=%wide.region_40.43_spmd.sunk | while | flops 52692480 | bytes 5712973 | solution.py:57
  1004.3 2.8 fusion.194
  1011.5 5.9 all-to-all-start.4
  1023.1 34.7 %all-gather.1 = bf16[256,1,16,24]{3,0,2,1:T(8,128)(2,1)S(1)} all-gather(bf16[16,1,16,24]{3,0,2,1:T(8,128)(2,1)S(1)} %get-tuple-element.314), channel_id=3, replica_groups=mesh['req'=4,'dap'=16] {'dap'}, dimensions={0}, use_global_device_ids=true | all-gather | bytes 208896 | tf_op jit(solution)/shard_map/all_gather | solution.py:113
  1057.8 17.5 %all-gather = bf16[256,1,16,24]{3,0,2,1:T(8,128)(2,1)} all-gather(bf16[16,1,16,24]{3,0,2,1:T(8,128)(2,1)S(1)} %get-tuple-element.315), channel_id=2, replica_groups=mesh['req'=4,'dap'=16] {'dap'}, dimensions={0}, use_global_device_ids=true | all-gather | bytes 208896 | tf_op jit(solution)/shard_map/all_gather | solution.py:114
  1085.7 4.5 fusion.426
  1092.0 18.2 %all_gather.51 = bf16[256,256,4]{1,2,0:T(4,128)(2,1)S(1)} all-gather(bf16[16,256,4]{1,2,0:T(4,128)(2,1)S(1)} %convolution_convert_fusion), channel_id=1, replica_groups=mesh['req'=4,'dap'=16] {'dap'}, dimensions={0}, use_global_device_ids=true | all-gather | bytes 557056 | tf_op jit(solution)/shard_map/all_gather | solution.py:107
  1114.7 101.5 %while.43 = (s32[]{:T(128)}, f32[16,256,4,32]{1,3,2,0:T(8,128)}, bf16[16,256,4,32]{1,3,2,0:T(8,128)(2,1)}, bf16[16,256,4,32]{1,3,2,0:T(8,128)(2,1)}, bf16[16,256...) while((s32[]{:T(128)}, f32[16,256,4,32]{1,3,2,0:T(8,128)}, ...), condition=%wide.region_49.50_spmd, body=%wide.region_46.49_spmd.sunk | while | flops 52692480 | bytes 5712973 | solution.py:57
  1118.3 2.8 fusion.528
  1181.7 2.8 fusion.528
  1188.0 2.8 fusion.528
  1216.2 2.8 fusion.195
  1221.2 5.1 all-to-all-start.5
  1231.5 35.2 %all-gather.3 = bf16[256,1,16,24]{3,0,2,1:T(8,128)(2,1)S(1)} all-gather(bf16[16,1,16,24]{3,0,2,1:T(8,128)(2,1)S(1)} %get-tuple-element.312), channel_id=5, replica_groups=mesh['req'=4,'dap'=16] {'dap'}, dimensions={0}, use_global_device_ids=true | all-gather | bytes 208896 | tf_op jit(solution)/shard_map/all_gather | solution.py:113
  1266.6 17.8 %all-gather.2 = bf16[256,1,16,24]{3,0,2,1:T(8,128)(2,1)} all-gather(bf16[16,1,16,24]{3,0,2,1:T(8,128)(2,1)S(1)} %get-tuple-element.313), channel_id=4, replica_groups=mesh['req'=4,'dap'=16] {'dap'}, dimensions={0}, use_global_device_ids=true | all-gather | bytes 208896 | tf_op jit(solution)/shard_map/all_gather | solution.py:114
  1291.9 3.7 convert_reduce_fusion.6
  (505 shorter events, 465.2 us)
Async XLA Ops:
  7.2 116.1 %all-gather.9.cloned.1.call-start = ((), (), s32[]{:S(2)}) async-start(), calls=%async_computation.6 | async-start | bytes 17825792 | tf_op jit(solution)/shard_map/all_gather | solution.py:94
  7.3 2.1 copy-start.64
  7.3 3.3 copy-start.50
  7.3 19.8 %copy-start.13 = (bf16[2,128,512]{2,1,0:T(8,128)(2,1)S(1)}, bf16[2,128,512]{2,1,0:T(8,128)(2,1)}, u32[]{:S(2)}) copy-start(bf16[2,128,512]{2,1,0:T(8,128)(2,1)} %param.33) | copy-start | bytes 786436
  27.0 1.4 copy-start.46
  31.1 243.6 %all-gather.11.cloned.1.call-start = ((), (), s32[]{:S(2)}) async-start(), calls=%async_computation.7 | async-start | bytes 17825792 | tf_op jit(solution)/shard_map/all_gather | solution.py:99
  155.4 2.2 copy-start.15
  161.8 7.4 copy-start.17
  161.8 7.5 copy-start.47
  163.6 42.7 %all-to-all-start = ((bf16[16,256,128]{2,0,1:T(8,128)(2,1)}), bf16[16,256,128]{2,0,1:T(8,128)(2,1)S(1)}, u32[]{:S(2)}, u32[]{:S(2)}) async-start(bf16[16,256,128]{2,0,1:T(8,128)(2,1)} %copy.337), calls=%async_computation | async-start | bytes 2097152 | tf_op jit(solution)/shard_map/all_to_all | solution.py:88
  169.3 303.0 %copy-start.44 = (f32[256]{0:T(256)}, f32[256]{0:T(256)S(1)}, u32[]{:S(2)}) copy-start(f32[256]{0:T(256)S(1)} %add_multiply_fusion) | copy-start | bytes 3076
  306.9 1.4 copy-start.62
  405.7 2.8 copy-start.33
  409.0 7.8 copy-start.18
  410.8 33.7 %all-to-all-start.1 = ((bf16[16,256,128]{2,0,1:T(8,128)(2,1)}), bf16[16,256,128]{2,0,1:T(8,128)(2,1)S(1)}, u32[]{:S(2)}, u32[]{:S(2)}) async-start(bf16[16,256,128]{2,0,1:T(8,128)(2,1)} %copy.350), calls=%async_computation.1 | async-start | bytes 2097152 | tf_op jit(solution)/shard_map/all_to_all | solution.py:88
  416.6 304.5 %all-gather.13.cloned.1.call-start = ((), (), s32[]{:S(2)}) async-start(), calls=%async_computation.8 | async-start | bytes 17825792 | tf_op jit(solution)/shard_map/all_gather | solution.py:94
  454.2 1.8 copy-start.48
  578.5 2.8 copy-start.35
  620.3 2.4 copy-start.54
  622.7 4.3 copy-start.14
  625.6 127.3 %copy-start.3 = (bf16[16,256,128]{1,2,0:T(8,128)(2,1)}, bf16[16,256,128]{1,2,0:T(8,128)(2,1)S(1)}, u32[]{:S(2)}) copy-start(bf16[16,256,128]{1,2,0:T(8,128)(2,1)S(1)} %get-tuple-element.331) | copy-start | bytes 3145732
  631.1 241.9 %all-gather.15.cloned.1.call-start = ((), (), s32[]{:S(2)}) async-start(), calls=%async_computation.9 | async-start | bytes 17825792 | tf_op jit(solution)/shard_map/all_gather | solution.py:99
  753.3 2.6 copy-start.16
  761.8 42.3 %all-to-all-start.3 = ((bf16[16,256,128]{2,0,1:T(8,128)(2,1)}), bf16[16,256,128]{2,0,1:T(8,128)(2,1)S(1)}, u32[]{:S(2)}, u32[]{:S(2)}) async-start(bf16[16,256,128]{2,0,1:T(8,128)(2,1)} %copy.388), calls=%async_computation.3 | async-start | bytes 2097152 | tf_op jit(solution)/shard_map/all_to_all | solution.py:88
  770.0 1.4 copy-start.21
  905.5 1.4 copy-start.63
  906.5 17.9 %copy-start.45 = (f32[256]{0:T(256)S(1)}, f32[256]{0:T(256)}, u32[]{:S(2)}) copy-start(f32[256]{0:T(256)} %copy-done.44) | copy-start | bytes 3076
  1004.3 2.8 copy-start.34
  1008.7 8.7 copy-start.1
  1011.5 9.3 copy-start.2
  1011.5 68.6 %all-to-all-start.4 = ((bf16[16,256,128]{2,0,1:T(8,128)(2,1)}), bf16[16,256,128]{2,0,1:T(8,128)(2,1)S(1)}, u32[]{:S(2)}, u32[]{:S(2)}) async-start(bf16[16,256,128]{2,0,1:T(8,128)(2,1)} %copy.401), calls=%async_computation.4 | async-start | bytes 2097152 | tf_op jit(solution)/shard_map/all_to_all | solution.py:88
  1020.8 54.5 %copy-start.4 = (bf16[16,256,128]{1,2,0:T(8,128)(2,1)S(1)}, bf16[16,256,128]{1,2,0:T(8,128)(2,1)}, u32[]{:S(2)}) copy-start(bf16[16,256,128]{1,2,0:T(8,128)(2,1)} %copy-done.3) | copy-start | bytes 3145732
  1022.2 53.1 %copy-start.24 = (f32[16,256]{1,0:T(8,128)S(1)}, f32[16,256]{1,0:T(8,128)}, u32[]{:S(2)}) copy-start(f32[16,256]{1,0:T(8,128)} %copy-done.22) | copy-start | bytes 49156
  1022.2 53.1 %copy-start.39 = (f32[16,256]{1,0:T(8,128)S(1)}, f32[16,256]{1,0:T(8,128)}, u32[]{:S(2)}) copy-start(f32[16,256]{1,0:T(8,128)} %copy-done.37) | copy-start | bytes 49156
  1022.2 53.1 %copy-start.60 = (bf16[2,128,16]{1,2,0:T(8,128)(2,1)S(1)}, bf16[2,128,16]{1,2,0:T(8,128)(2,1)}, u32[]{:S(2)}) copy-start(bf16[2,128,16]{1,2,0:T(8,128)(2,1)} %param.48) | copy-start | bytes 24580
  1075.7 3.4 copy-start.9
  1083.9 1.4 copy-start.49
  1216.2 2.8 copy-start.36
  1219.5 6.7 copy-start.51
  1219.5 6.7 copy-start.20
  1221.2 63.3 %all-to-all-start.5 = ((bf16[16,256,128]{2,0,1:T(8,128)(2,1)}), bf16[16,256,128]{2,0,1:T(8,128)(2,1)S(1)}, u32[]{:S(2)}, u32[]{:S(2)}) async-start(bf16[16,256,128]{2,0,1:T(8,128)(2,1)} %copy.407), calls=%async_computation.5 | async-start | bytes 2097152 | tf_op jit(solution)/shard_map/all_to_all | solution.py:88
  1226.2 2.4 copy-start.52
  1226.3 3.0 copy-start
  1289.5 2.4 copy-start.55
  1295.6 2.4 copy-start.7
  1295.6 2.7 copy-start.61
  1298.7 2.2 copy-start.10
  1300.7 2.8 copy-start.53
  (26 other events, 23.2 us)
Sparse Core Ops, SparseCore 0:
  31.2 91.9 all-gather.8
  161.9 112.8 all-gather.10
  631.2 89.8 all-gather.12
  760.1 112.7 all-gather.14
where the time goes:
time: 1330 us; the launch traced here: 1310 us
  matrix products  439 us (33%)
  waiting for transfers between devices  412 us (31%)
  blocking collectives  223 us (17%)
  local copies, waits for them, and re-layouts  157 us (12%)
  other arithmetic  35 us (3%)
  starting transfers between devices  28.6 us (2%)
  between operations  16.3 us (1%)
    all_gather x4, waiting for transfers between devices, run_block(): right_all = lax.all_gather(right, 'dap', tiled=True)  315 us
    dot_general x64, matrix products, one_row(): jnp.einsum('hjk,khd->jhd', soft_scores, v_row, preferred_element_type=jnp...  146 us
    dot_general x64, matrix products, one_row(): jnp.einsum('jhd,khd->hjk', q_row, k_row, preferred_element_type=jnp.float32)  110 us
    all_to_all x5, waiting for transfers between devices, transpose_pairs(): moved = lax.all_to_all(block_rows, 'dap', 1, 0, tiled=True)  96.2 us
    sub x64, matrix products, one_row(): soft_scores = jax.nn.softmax(logits, axis=-1).astype(jnp.bfloat16)  88.6 us
    all_gather x4, local copies, waits for them, and re-layouts, run_block(): right_all = lax.all_gather(right, 'dap', tiled=True)  88.4 us
    all_gather x2, blocking collectives, run_block(): key_all = lax.all_gather(key_rows, 'dap', tiled=True)  69.8 us
    all_gather x2, blocking collectives, run_block(): value_all = lax.all_gather(value_rows, 'dap', tiled=True)  35.3 us
  transfers between devices with their start and end apart: 9, of which 7 were waited for; matrix products, arithmetic and copies ran while one was open for 2% of the time, Pallas kernels for 0%

commit v1 on v0

v1 whole, which is shorter than its diff:
```python
import functools

import jax
import jax.numpy as jnp
from jax import lax
from jax.experimental import pallas as pl
from jax.experimental.pallas import tpu as pltpu
from jax.sharding import PartitionSpec as P

EPS = 1e-5
NEG_BIG = 1e9
LOG2E = 1.4426950408889634
F32 = jnp.float32
BF16 = jnp.bfloat16
MESH = pl.DeviceIdType.MESH
WEIGHT_NAMES = ('tmo_proj', 'tmo_gate', 'tmo_out', 'tmi_proj', 'tmi_gate', 'tmi_out', 'tas_qkvg', 'tas_bias', 'tas_out', 'tae_qkvg', 'tae_bias', 'tae_out', 'pt_in', 'pt_out', 'ap_qkvg', 'ap_bias', 'ap_out', 'st_in', 'st_out')
LANES = 128
VMEM_LIMIT = 60 * 1024 * 1024


def dot_nn(lhs, rhs):
    return lax.dot_general(lhs, rhs, (((1,), (0,)), ((), ())), preferred_element_type=F32)


def dot_nt(lhs, rhs):
    return lax.dot_general(lhs, rhs, (((1,), (1,)), ((), ())), preferred_element_type=F32)


def dot_tn(lhs, rhs):
    return lax.dot_general(lhs, rhs, (((0,), (0,)), ((), ())), preferred_element_type=F32)


def sigmoid(values):
    return 0.5 * jnp.tanh(0.5 * values) + 0.5


def layer_norm(values):
    values = values.astype(F32)
    centred = values - jnp.mean(values, axis=-1, keepdims=True)
    variance = jnp.mean(centred * centred, axis=-1, keepdims=True)
    return (centred * lax.rsqrt(variance + EPS)).astype(BF16)


def tri_mult_kernel(kind, layer, n_dev, z_hbm, mask_s, mask_v, w_proj, w_gate, w_out, *rest):
    if kind == 'colx':
        out_ref, zrow_ref = rest[:2]
        rest = rest[2:]
    else:
        out_ref, zrow_ref = rest[0], None
        rest = rest[1:]
    (zfull, b_full, a_full, z_t, stage, w_t, x_buf, x_in, in_sem, right_send, right_recv, left_send, left_recv, pair_send, pair_recv, x_send, x_recv) = rest
    chips = n_dev // 2
    rows = zfull.shape[2]
    half_c = b_full.shape[0]
    channels = 2 * half_c
    pad = half_c + 8
    me = lax.axis_index('dap')
    chip, core = me // 2, lax.rem(me, 2)
    partner = chip * 2 + 1 - core
    right = lax.rem(chip + 1, chips) * 2 + core
    left = lax.rem(chip + chips - 1, chips) * 2 + core

    loads = [pltpu.make_async_copy(z_hbm.at[:, pl.ds(h * LANES, LANES), :], zfull.at[me, h], in_sem.at[h]) for h in range(2)]
    for load in loads:
        load.start()
    barrier = pltpu.get_barrier_semaphore()
    for peer in (left, right, partner):
        pl.semaphore_signal(barrier, inc=1, device_id={'dap': peer}, device_id_type=MESH)
    w_t[...] = w_proj[layer].astype(F32).T.astype(BF16)
    for load in loads:
        load.wait()
    pl.semaphore_wait(barrier, 3)

    def send(block, half, send_sem, recv_sem, target):
        return pltpu.make_async_remote_copy(src_ref=zfull.at[block, half], dst_ref=zfull.at[block, half], send_sem=send_sem, recv_sem=recv_sem, device_id={'dap': target}, device_id_type=MESH)

    send(me, 0, right_send.at[0], right_recv.at[0], right).start()
    send(me, 1, left_send.at[0], left_recv.at[0], left).start()
    send(me, 1, right_send.at[1], right_recv.at[1], right).start()
    send(me, 0, left_send.at[1], left_recv.at[1], left).start()
    send(me, 0, pair_send.at[0], pair_recv.at[0], partner).start()
    send(me, 1, pair_send.at[1], pair_recv.at[1], partner).start()

    def weights(first):
        lo = pl.multiple_of(core * half_c, half_c)
        return jnp.concatenate([w_t[pl.ds(first * channels + lo, half_c), :], w_t[pl.ds((first + 1) * channels + lo, half_c), :]], axis=0)

    def project(load, row_mask, tok_mask, first, store):
        w_half = weights(first)

        @pl.loop(0, rows // 2)
        def _(pair):
            normed = layer_norm(load(pair))
            slab = dot_nt(w_half, normed)
            gated = sigmoid(slab[half_c:]) * slab[:half_c]
            for t in range(2):
                row = 2 * pair + t
                stage[pl.ds(pl.multiple_of(row * pad, 8), half_c), :] = gated[:, t * LANES:(t + 1) * LANES] * (tok_mask * row_mask(row))

        @pl.loop(0, half_c // 8)
        def _(group):
            for t in range(8):
                c = group * 8 + t
                store(c, stage[pl.ds(c, rows, stride=pad), :].astype(BF16))

    my_half = chip // (chips // 2)
    my_off = pl.multiple_of(lax.rem(chip, chips // 2) * 2 * rows, 2 * rows)

    def process(block, half):
        def load(pair):
            return zfull[block, half, pl.ds(2 * pair, 2)].reshape(2 * LANES, LANES)

        def store(c, values):
            b_full[c, half, pl.ds(pl.multiple_of(block * rows, rows), rows), :] = values

        project(load, lambda row: mask_s[block * rows + row], mask_v[half], 2, store)
        if kind != 'row':
            @pl.when(half == my_half)
            def _():
                @pl.loop(0, rows)
                def _(row):
                    stage[pl.ds(pl.multiple_of(row * pad, 8), 2 * rows), :] = zfull[block, half, row, pl.ds(my_off, 2 * rows), :].astype(F32)

                @pl.loop(0, rows // 4)
                def _(group):
                    for t in range(8):
                        i = group * 8 + t
                        z_t[i, pl.ds(pl.multiple_of(block * rows, rows), rows), :] = stage[pl.ds(i, rows, stride=pad), :].astype(BF16)

    def process_left_operand(who, half):
        spot = pl.multiple_of(who * rows, rows)

        def store(c, values):
            a_full[c, half, pl.ds(spot, rows), :] = values

        def load(pair):
            if kind == 'row':
                return zfull[chip * 2 + who, half, pl.ds(2 * pair, 2)].reshape(2 * LANES, LANES)
            return z_t[pl.ds(spot + 2 * pair, 2), pl.ds(pl.multiple_of(half * LANES, LANES), LANES), :].reshape(2 * LANES, LANES)

        project(load, lambda row: mask_s[(chip * 2 + who) * rows + row], mask_v[half], 0, store)

    @pl.loop(0, 4)
    def _(t):
        who, half = t // 2, lax.rem(t, 2)
        block = jnp.where(who == 0, me, partner)

        @pl.when(who == 1)
        def _():
            send(partner, half, pair_send.at[half], pair_recv.at[half], partner).wait_recv()

        process(block, half)

    if kind == 'row':
        @pl.loop(0, 4)
        def _(t):
            process_left_operand(t // 2, lax.rem(t, 2))

    events = chips - 1

    @pl.loop(0, events)
    def _(e):
        dist = e // 2 + 1
        half_r = lax.rem(e, 2)
        half_l = 1 - half_r
        from_left = lax.rem(chip - dist + chips, chips)
        from_right = lax.rem(chip + dist, chips)
        block_r, block_l = from_left * 2 + core, from_right * 2 + core
        send(block_r, half_r, right_send.at[e], right_recv.at[e], right).wait_recv()

        @pl.when(e + 2 < events)
        def _():
            send(block_r, half_r, right_send.at[e + 2], right_recv.at[e + 2], right).start()

        send(block_r, half_r, pair_send.at[2 * e + 2], pair_recv.at[2 * e + 2], partner).start()
        send(block_l, half_l, left_send.at[e], left_recv.at[e], left).wait_recv()

        @pl.when(e + 2 < events)
        def _():
            send(block_l, half_l, left_send.at[e + 2], left_recv.at[e + 2], left).start()

        send(block_l, half_l, pair_send.at[2 * e + 3], pair_recv.at[2 * e + 3], partner).start()

        @pl.loop(0, 4)
        def _(t):
            side, other = lax.rem(t, 2), t // 2
            owner = jnp.where(other == 0, core, 1 - core)
            block = jnp.where(side == 0, from_left, from_right) * 2 + owner
            half = jnp.where(side == 0, half_r, half_l)

            @pl.when(other == 1)
            def _():
                send(block, half, pair_send.at[2 * e + 2 + side], pair_recv.at[2 * e + 2 + side], partner).wait_recv()

            process(block, half)

    if kind != 'row':
        @pl.loop(0, 4)
        def _(t):
            process_left_operand(t // 2, lax.rem(t, 2))

    @pl.loop(0, half_c)
    def _(c):
        lhs = jnp.concatenate([a_full[c, 0], a_full[c, 1]], axis=1)
        rhs = jnp.concatenate([b_full[c, 0], b_full[c, 1]], axis=1)
        product = dot_nt(lhs, rhs) if kind == 'row' else dot_nn(lhs, rhs)
        for who in range(2):
            for half in range(2):
                x_buf[who, half, pl.ds(c, rows, stride=pad), :] = product[who * rows:(who + 1) * rows, half * LANES:(half + 1) * LANES]

    for e in range(events):
        send(me, 0, right_send.at[e], right_recv.at[e], right).wait_send()
        send(me, 0, left_send.at[e], left_recv.at[e], left).wait_send()
    for e in range(2 * events + 2):
        send(me, 0, pair_send.at[e], pair_recv.at[e], partner).wait_send()

    exchange = pltpu.make_async_remote_copy(src_ref=x_buf.at[1 - core], dst_ref=x_in, send_sem=x_send, recv_sem=x_recv, device_id={'dap': partner}, device_id_type=MESH)
    exchange.start()
    w_o = jnp.concatenate([w_out[layer, pl.ds(pl.multiple_of(core * half_c, half_c), half_c), :], w_out[layer, pl.ds(pl.multiple_of((1 - core) * half_c, half_c), half_c), :]], axis=0)
    exchange.wait()

    @pl.loop(0, rows)
    def _(i):
        for half in range(2):
            x = jnp.concatenate([x_buf[core, half, pl.ds(pl.multiple_of(i * pad, 8), half_c), :], x_in[half, pl.ds(pl.multiple_of(i * pad, 8), half_c), :]], axis=0)
            centred = x - jnp.mean(x, axis=0, keepdims=True)
            variance = jnp.mean(centred * centred, axis=0, keepdims=True)
            x_norm = (centred * lax.rsqrt(variance + EPS)).astype(BF16)
            update = dot_tn(x_norm, w_o)
            if kind == 'colx':
                z_row = z_t[core * rows + i, half * LANES:(half + 1) * LANES, :]
                zrow_ref[i, half * LANES:(half + 1) * LANES, :] = z_row
            else:
                z_row = zfull[me, half, i]
            gate = sigmoid(dot_nn(layer_norm(z_row), w_gate[layer]))
            out_ref[i, half * LANES:(half + 1) * LANES, :] = (z_row.astype(F32) + gate * update).astype(BF16)


def tri_mult(kind, layer, n_dev, cid, z, mask_s, mask_v, w_proj, w_gate, w_out):
    rows, tokens, channels = z.shape
    assert tokens == 2 * LANES and channels == LANES and rows * n_dev == tokens
    half_c = channels // 2
    pad = half_c + 8
    events = n_dev // 2 - 1
    vmem = pl.BlockSpec(memory_space=pltpu.VMEM)
    shape = jax.ShapeDtypeStruct(z.shape, BF16)
    dma = pltpu.SemaphoreType.DMA
    return pl.pallas_call(
        functools.partial(tri_mult_kernel, kind, layer, n_dev),
        out_shape=(shape, shape) if kind == 'colx' else shape,
        in_specs=[pl.BlockSpec(memory_space=pl.ANY), pl.BlockSpec(memory_space=pltpu.SMEM), vmem, vmem, vmem, vmem],
        out_specs=(vmem, vmem) if kind == 'colx' else vmem,
        scratch_shapes=[
            pltpu.VMEM((n_dev, 2, rows, LANES, channels), BF16),
            pltpu.VMEM((half_c, 2, tokens, LANES), BF16),
            pltpu.VMEM((half_c, 2, 2 * rows, LANES), BF16),
            pltpu.VMEM((2 * rows, tokens, channels), BF16),
            pltpu.VMEM((rows * pad, LANES), F32),
            pltpu.VMEM((4 * channels, channels), BF16),
            pltpu.VMEM((2, 2, rows * pad, LANES), F32),
            pltpu.VMEM((2, rows * pad, LANES), F32),
            dma((2,)), dma((events,)), dma((events,)), dma((events,)), dma((events,)), dma((2 * events + 2,)), dma((2 * events + 2,)), dma, dma,
        ],
        compiler_params=pltpu.CompilerParams(collective_id=cid, has_side_effects=True, vmem_limit_bytes=VMEM_LIMIT),
        name=f'tri_mult_{kind}_{cid}',
    )(z, mask_s, mask_v, w_proj, w_gate, w_out)


def tri_att_kernel(layer, n_dev, heads, turn, trans, z_ref, mask_c, w_qkvg, bias_t, w_out, *rest):
    if trans:
        pt_in, pt_out = rest[:2]
        rest = rest[2:]
    if turn:
        (out_ref, normed_s, bias_s, bias_all, logit_bias, w_t, k_s, q_s, v_s, g_s, z_new, r_buf, stage, b_send, b_recv, t_send, t_recv, own_sem) = rest
    else:
        (out_ref, normed_s, bias_s, bias_all, logit_bias, w_t, k_s, q_s, v_s, g_s, b_send, b_recv) = rest
        z_new = out_ref
    rows, tokens, channels = z_ref.shape
    width = channels // heads
    me = lax.axis_index('dap')
    barrier = pltpu.get_barrier_semaphore()
    peers = [lax.rem(me + p, n_dev) for p in range(1, n_dev)]
    for peer in peers:
        pl.semaphore_signal(barrier, inc=1, device_id={'dap': peer}, device_id_type=MESH)

    @pl.loop(0, rows)
    def _(i):
        normed = layer_norm(z_ref[i])
        normed_s[i] = normed
        slab = dot_nt(bias_t[layer], normed)
        for half in range(2):
            bias_s[half, pl.ds(pl.multiple_of(i * 8, 8), 8), :] = slab[:, half * LANES:(half + 1) * LANES]

    spot = pl.multiple_of(me * rows, rows)
    for h in range(heads):
        for half in range(2):
            bias_all[h, pl.ds(spot, rows), half * LANES:(half + 1) * LANES] = bias_s[half, pl.ds(h, rows, stride=8), :].astype(BF16)
    w_t[...] = w_qkvg[layer].astype(F32).T.astype(BF16)
    pl.semaphore_wait(barrier, n_dev - 1)

    def bias_copy(owner, p, target):
        ref = bias_all.at[:, pl.ds(pl.multiple_of(owner * rows, rows), rows), :]
        return pltpu.make_async_remote_copy(src_ref=ref, dst_ref=ref, send_sem=b_send.at[p - 1], recv_sem=b_recv.at[p - 1], device_id={'dap': target}, device_id_type=MESH)

    for p in range(1, n_dev):
        bias_copy(me, p, peers[p - 1]).start()

    @pl.loop(0, rows)
    def _(i):
        normed = normed_s[i]
        q_s[i] = dot_nt(w_t[:channels], normed).astype(BF16)
        k_s[i] = dot_nn(normed, w_qkvg[layer, :, channels:2 * channels]).astype(BF16)
        v_s[i] = dot_nt(w_t[2 * channels:3 * channels], normed).astype(BF16)
        g_s[i] = sigmoid(dot_nt(w_t[3 * channels:], normed))

    for p in range(1, n_dev):
        bias_copy(lax.rem(me + n_dev - p, n_dev), p, peers[p - 1]).wait_recv()
    for h in range(heads):
        for qh in range(2):
            for kh in range(2):
                tile = bias_all[h, qh * LANES:(qh + 1) * LANES, kh * LANES:(kh + 1) * LANES].astype(F32).T
                logit_bias[h, qh, kh * LANES:(kh + 1) * LANES, :] = (tile + mask_c[kh * LANES:(kh + 1) * LANES, :]) * LOG2E
    scale = width ** -0.5 * LOG2E

    def turn_copy(source, t, p, target, to):
        return pltpu.make_async_remote_copy(
            src_ref=z_new.at[pl.ds(4 * t, 4), pl.ds(pl.multiple_of(to * rows, rows), rows), :], dst_ref=r_buf.at[source, pl.ds(4 * t, 4)],
            send_sem=t_send.at[p - 1], recv_sem=t_recv.at[p - 1], device_id={'dap': target}, device_id_type=MESH)

    @pl.loop(0, rows)
    def _(i):
        keys = k_s[i]
        for qh in range(2):
            lanes = slice(qh * LANES, (qh + 1) * LANES)
            parts = []
            for h in range(heads):
                q_head = q_s[i, h * width:(h + 1) * width, lanes]
                pieces = [q_head]
                if h:
                    pieces = [jnp.zeros((h * width, LANES), BF16)] + pieces
                if h < heads - 1:
                    pieces = pieces + [jnp.zeros(((heads - 1 - h) * width, LANES), BF16)]
                logits = dot_nn(keys, jnp.concatenate(pieces, axis=0)) * scale + logit_bias[h, qh]
                weights = jnp.exp2(logits - jnp.max(logits, axis=0, keepdims=True))
                total = jnp.sum(weights, axis=0, keepdims=True)
                soft = (weights * (1.0 / total)).astype(BF16)
                parts.append(dot_nn(v_s[i, h * width:(h + 1) * width, :], soft))
            merged = (jnp.concatenate(parts, axis=0) * g_s[i, :, lanes]).astype(BF16)
            z_row = (z_ref[i, lanes, :].astype(F32) + dot_tn(merged, w_out[layer])).astype(BF16)
            if trans:
                normed = layer_norm(z_row)
                hidden = pt_out.shape[1]
                first = dot_nn(normed, pt_in[layer, :, :hidden])
                second = dot_nn(normed, pt_in[layer, :, hidden:])
                inner = (first * sigmoid(first) * second).astype(BF16)
                z_row = (z_row.astype(F32) + dot_nn(inner, pt_out[layer])).astype(BF16)
            z_new[i, lanes, :] = z_row
        if turn:
            @pl.when((lax.rem(i, 4) == 0) & (i > 0))
            def _():
                for p in range(1, n_dev):
                    turn_copy(me, i // 4 - 1, p, peers[p - 1], peers[p - 1]).start()

    if turn:
        own = pltpu.make_async_copy(z_new.at[:, pl.ds(spot, rows), :], r_buf.at[me], own_sem)
        own.start()
        for p in range(1, n_dev):
            turn_copy(me, rows // 4 - 1, p, peers[p - 1], peers[p - 1]).start()
        own.wait()

        def whole(source, p, target):
            return pltpu.make_async_remote_copy(src_ref=r_buf.at[source], dst_ref=r_buf.at[source], send_sem=t_send.at[p - 1], recv_sem=t_recv.at[p - 1], device_id={'dap': target}, device_id_type=MESH)

        def place(source):
            pad = rows + 8
            for i in range(rows):
                stage[i * pad:i * pad + rows, :] = r_buf[source, i].astype(F32)
            for j in range(rows):
                out_ref[j, pl.ds(pl.multiple_of(source * rows, rows), rows), :] = stage[pl.ds(j, rows, stride=pad), :].astype(BF16)

        place(me)

        @pl.loop(1, n_dev)
        def _(p):
            source = lax.rem(me + n_dev - p, n_dev)
            whole(source, p, lax.rem(me + p, n_dev)).wait_recv()
            place(source)

        for p in range(1, n_dev):
            whole(me, p, peers[p - 1]).wait_send()
    for p in range(1, n_dev):
        bias_copy(me, p, peers[p - 1]).wait_send()


def tri_att(layer, n_dev, cid, turn, z, mask_c, w_qkvg, bias_t, heads, w_out, pt=()):
    rows, tokens, channels = z.shape
    vmem = pl.BlockSpec(memory_space=pltpu.VMEM)
    dma = pltpu.SemaphoreType.DMA
    scratch = [
        pltpu.VMEM((rows, tokens, channels), BF16),
        pltpu.VMEM((2, rows * 8, LANES), F32),
        pltpu.VMEM((heads, tokens, tokens), BF16),
        pltpu.VMEM((heads, 2, tokens, LANES), F32),
        pltpu.VMEM((4 * channels, channels), BF16),
        pltpu.VMEM((rows, tokens, channels), BF16),
        pltpu.VMEM((rows, channels, tokens), BF16),
        pltpu.VMEM((rows, channels, tokens), BF16),
        pltpu.VMEM((rows, channels, tokens), F32),
    ]
    if turn:
        scratch += [pltpu.VMEM((rows, tokens, channels), BF16), pltpu.VMEM((n_dev, rows, rows, channels), BF16), pltpu.VMEM((rows * (rows + 8), LANES), F32)]
    scratch += [dma((n_dev - 1,)), dma((n_dev - 1,))]
    if turn:
        scratch += [dma((n_dev - 1,)), dma((n_dev - 1,)), dma]
    return pl.pallas_call(
        functools.partial(tri_att_kernel, layer, n_dev, heads, turn, bool(pt)),
        out_shape=jax.ShapeDtypeStruct(z.shape, BF16),
        in_specs=[vmem] * (5 + len(pt)),
        out_specs=vmem,
        scratch_shapes=scratch,
        compiler_params=pltpu.CompilerParams(collective_id=cid, has_side_effects=True, vmem_limit_bytes=VMEM_LIMIT),
        name=f'tri_att_{cid}',
    )(z, mask_c, w_qkvg, bias_t, w_out, *pt)


def transition(act_in, w_in, w_out):
    hidden = w_out.shape[0]
    projected = jnp.dot(layer_norm(act_in), w_in, preferred_element_type=F32)
    inner = (jax.nn.silu(projected[..., :hidden]) * projected[..., hidden:]).astype(BF16)
    return (act_in.astype(F32) + jnp.dot(inner, w_out, preferred_element_type=F32)).astype(BF16)


def single_step(single, pair, mask_all, w_qkvg, w_bias, w_out, st_in, st_out):
    rows = single.shape[0]
    heads = w_bias.shape[1]
    head_dim = w_qkvg.shape[1] // (4 * heads)
    projected = jnp.dot(layer_norm(single), w_qkvg, preferred_element_type=F32).reshape(rows, 4, heads, head_dim)
    query, gate = projected[:, 0].astype(BF16), jax.nn.sigmoid(projected[:, 3])
    kv_all = lax.all_gather(projected[:, 1:3].astype(BF16), 'dap', tiled=True)
    key_all, value_all = kv_all[:, 0], kv_all[:, 1]
    pair_bias = jnp.einsum('ijc,ch->ihj', layer_norm(pair), w_bias, preferred_element_type=F32).astype(BF16)
    logits = jnp.einsum('ihd,jhd->ihj', query, key_all, preferred_element_type=F32) * head_dim ** -0.5 + pair_bias.astype(F32) + (mask_all.astype(F32) - 1.0) * NEG_BIG
    soft_scores = jax.nn.softmax(logits, axis=-1).astype(BF16)
    attended = jnp.einsum('ihj,jhd->ihd', soft_scores, value_all, preferred_element_type=F32)
    merged = (attended * gate).astype(BF16).reshape(rows, -1)
    single = (single.astype(F32) + jnp.dot(merged, w_out, preferred_element_type=F32)).astype(BF16)
    return transition(single, st_in, st_out)


def solution(mesh):
    row_spec = P(('req', 'dap'))
    single_spec = P(('req', 'dap'), None)
    pair_spec = P(('req', 'dap'), None, None)
    n_dev = mesh.shape['dap']

    def local_program(single, pair, token_mask, *weights):
        w = dict(zip(WEIGHT_NAMES, weights))
        blocks = weights[0].shape[0]
        mask_all = lax.all_gather(token_mask, 'dap', tiled=True)
        tokens = mask_all.shape[0]
        mask_f = mask_all.astype(F32)
        mask_v = mask_f.reshape(2, 1, tokens // 2)
        mask_c = jnp.broadcast_to(((mask_f - 1.0) * NEG_BIG)[:, None], (tokens, LANES))
        heads = w['tas_bias'].shape[2]

        def bias_rows(name):
            turned = jnp.swapaxes(w[name], 1, 2)
            return jnp.pad(turned, ((0, 0), (0, 8 - heads), (0, 0)))

        tas_bias, tae_bias = bias_rows('tas_bias'), bias_rows('tae_bias')

        def single_block(b, single, pair_rows):
            return single_step(single, pair_rows, mask_all, *(w[name][b] for name in ('ap_qkvg', 'ap_bias', 'ap_out', 'st_in', 'st_out')))

        for b in range(blocks):
            cid = 4 * b
            out = (w['tmo_proj'], w['tmo_gate'], w['tmo_out'])
            if b == 0:
                pair = tri_mult('row', b, n_dev, cid, pair, mask_f, mask_v, *out)
            else:
                pair, pair_rows = tri_mult('colx', b, n_dev, cid, pair, mask_f, mask_v, *out)
                single = single_block(b - 1, single, pair_rows)
            pair = tri_mult('col', b, n_dev, cid + 1, pair, mask_f, mask_v, w['tmi_proj'], w['tmi_gate'], w['tmi_out'])
            pair = tri_att(b, n_dev, cid + 2, True, pair, mask_c, w['tas_qkvg'], tas_bias, heads, w['tas_out'])
            pair = tri_att(b, n_dev, cid + 3, b == blocks - 1, pair, mask_c, w['tae_qkvg'], tae_bias, heads, w['tae_out'], (w['pt_in'], w['pt_out']))
        single = single_block(blocks - 1, single, pair)
        return single, pair

    return jax.shard_map(local_program, mesh=mesh, in_specs=(single_spec, pair_spec, row_spec) + (P(),) * len(WEIGHT_NAMES), out_specs=(single_spec, pair_spec), check_vma=False)
```

time: 1330 us -> 934 us (0.70); the launches traced: 1310 us -> 934 us
  Pallas kernels: 0 us -> 831 us
  matrix products: 439 us -> 19.9 us
  waiting for transfers between devices: 412 us -> 0 us
  blocking collectives: 223 us -> 60.1 us
  local copies, waits for them, and re-layouts: 157 us -> 11.7 us
  starting transfers between devices: 28.6 us -> 0 us
  other arithmetic: 35 us -> 8.89 us
  between operations: 16.3 us -> 1.62 us
    pallas_call x0 -> x8, Pallas kernels: none -> 831 us  [the longest x4 534 us: tri_mult(): pl.pallas_call(functools.partial(tri_mult_kernel, kind, layer, n_dev), ou...]
    dot_general x174 -> x14, matrix products: 351 us -> 19.9 us  [the longest x2 4.48 us: single_step(): jnp.dot(layer_norm(single), w_qkvg, preferred_element_type=F32)]
    all_gather x4 -> x0, waiting for transfers between devices: 315 us -> none  [run_block(): right_all = lax.all_gather(right, 'dap', tiled=True)]
    all_gather x8 -> x2, blocking collectives: 174 us -> 44 us  [single_step(): kv_all = lax.all_gather(projected[:, 1:3].astype(BF16), 'dap', tiled=True)]
    all_to_all x5 -> x0, waiting for transfers between devices: 96.2 us -> none  [transpose_pairs(): moved = lax.all_to_all(block_rows, 'dap', 1, 0, tiled=True)]
    sub x64 -> x0, matrix products: 88.6 us -> none  [one_row(): soft_scores = jax.nn.softmax(logits, axis=-1).astype(jnp.bfloat16)]
    all_gather x4 -> x0, local copies, waits for them, and re-layouts: 88.4 us -> none  [run_block(): right_all = lax.all_gather(right, 'dap', tiled=True)]
    all_to_all x1 -> x0, blocking collectives: 32.7 us -> none  [transpose_pairs(): moved = lax.all_to_all(block_rows, 'dap', 1, 0, tiled=True)]
  transfers between devices with their start and end apart: 9 -> 0, of which waited for: 7 -> 0; matrix products, arithmetic and copies ran while one was open for 2% -> 0% of each run, Pallas kernels for 0% -> 0%
where the time goes in v1:
time: 934 us
  Pallas kernels  831 us (89%)
  blocking collectives  60.1 us (6%)
  matrix products  19.9 us (2%)
  local copies, waits for them, and re-layouts  11.7 us (1%)
    pallas_call x4, Pallas kernels, tri_mult(): pl.pallas_call(functools.partial(tri_mult_kernel, kind, layer, n_dev), ou...  534 us
    pallas_call x4, Pallas kernels, tri_att(): pl.pallas_call(functools.partial(tri_att_kernel, layer, n_dev, heads, tur...  298 us
    all_gather x2, blocking collectives, single_step(): kv_all = lax.all_gather(projected[:, 1:3].astype(BF16), 'dap', tiled=True)  44 us

profile of v1, /device:TPU:21, one launch (start us, length us, event | category | flops | bytes accessed | tf_op | source)
XLA Modules:
  0.0 933.6 jit_solution(1139329986051937975)
XLA Ops:
  0.6 1.2 dynamic-slice
  2.5 0.8 convert_reduce_fusion.2
  3.4 0.9 fusion.85
  4.3 0.9 dynamic-update-slice
  5.1 16.1 %all-reduce.2 = s32[256]{0:T(256)S(1)} all-reduce(s32[256]{0:T(256)S(1)} %dynamic-update-slice), channel_id=1, replica_groups=mesh['req'=4,'dap'=16] {'dap'}, use_global_device_ids=true, to_apply=%add.2 | all-reduce | flops 256 | bytes 2048
  21.2 0.6 convert_element_type.111.mask_s
  21.8 1.3 pad.7.bias_t
  23.1 1.3 pad.8.bias_t
  24.4 0.8 broadcast_in_dim.2.mask_c
  25.1 132.0 %tri_mult_row_0.1.z_hbm = bf16[16,256,128]{2,1,0:T(8,128)(2,1)} custom-call(bf16[16,256,128]{2,1,0:T(8,128)(2,1)} %z_hbm.1, f32[256]{0:T(256)} %convert_element_type.111.mask_s, f32[2,1,128]{2,1,0:T(1,128)} %bitcast.134, bf16[2,128,512]{2,1,0:T(8,128)(2,1)} %w_proj.6, bf16[2,128,128]{2,1,0:T(8,128)(2,1)} %w_gate.6, bf16[2,128,128]{2,1,0:T(8,128)(2,1)} %w_out.12), custom_call_target="tpu_custom_call" | custom-call | tf_op jit(solution)/shard_map/tri_mult_row_0/pallas_call | solution.py:248
  157.1 133.1 %tri_mult_col_1.1.z_ref = bf16[16,256,128]{2,1,0:T(8,128)(2,1)} custom-call(bf16[16,256,128]{2,1,0:T(8,128)(2,1)} %tri_mult_row_0.1.z_hbm, f32[256]{0:T(256)} %convert_element_type.111.mask_s, f32[2,1,128]{2,1,0:T(1,128)} %bitcast.135, bf16[2,128,512]{2,1,0:T(8,128)(2,1)} %w_proj.7, bf16[2,128,128]{2,1,0:T(8,128)(2,1)} %w_gate.7, bf16[2,128,128]{2,1,0:T(8,128)(2,1)} %w_out.13), custom_call_target="tpu_custom_call" | custom-call | tf_op jit(solution)/shard_map/tri_mult_col_1/pallas_call | solution.py:248
  290.2 65.6 %tri_att_2.1.z_ref = bf16[16,256,128]{2,1,0:T(8,128)(2,1)} custom-call(bf16[16,256,128]{2,1,0:T(8,128)(2,1)} %tri_mult_col_1.1.z_ref, f32[256,128]{1,0:T(8,128)} %broadcast_in_dim.2.mask_c, bf16[2,128,512]{2,1,0:T(8,128)(2,1)} %w_qkvg.6, bf16[2,8,128]{2,1,0:T(8,128)(2,1)} %pad.7.bias_t, bf16[2,128,128]{2,1,0:T(8,128)(2,1)} %w_out.14), custom_call_target="tpu_custom_call" | custom-call | tf_op jit(solution)/shard_map/tri_att_2/pallas_call | solution.py:415
  355.8 75.3 %tri_att_3.1.z_hbm = bf16[16,256,128]{2,1,0:T(8,128)(2,1)} custom-call(bf16[16,256,128]{2,1,0:T(8,128)(2,1)} %tri_att_2.1.z_ref, f32[256,128]{1,0:T(8,128)} %broadcast_in_dim.2.mask_c, bf16[2,128,512]{2,1,0:T(8,128)(2,1)} %w_qkvg.7, bf16[2,8,128]{2,1,0:T(8,128)(2,1)} %pad.8.bias_t, bf16[2,128,128]{2,1,0:T(8,128)(2,1)} %w_out.15, ...), custom_call_target="tpu_custom_call" | custom-call | tf_op jit(solution)/shard_map/tri_att_3/pallas_call | solution.py:415
  431.2 135.6 %tri_mult_colx_4.1 = (bf16[16,256,128]{2,1,0:T(8,128)(2,1)}, bf16[16,256,128]{2,1,0:T(8,128)(2,1)}) custom-call(bf16[16,256,128]{2,1,0:T(8,128)(2,1)} %tri_att_3.1.z_hbm, f32[256]{0:T(256)} %convert_element_type.111.mask_s, f32[2,1,128]{2,1,0:T(1,128)} %bitcast.136, bf16[2,128,512]{2,1,0:T(8,128)(2,1)} %w_proj.6, bf16[2,128,128]{2,1,0:T(8,128)(2,1)} %w_gate.6, ...), custom_call_target="tpu_custom_call" | custom-call | tf_op jit(solution)/shard_map/tri_mult_colx_4/pallas_call | solution.py:248
  566.8 133.1 %tri_mult_col_5.1.z_ref = bf16[16,256,128]{2,1,0:T(8,128)(2,1)} custom-call(bf16[16,256,128]{2,1,0:T(8,128)(2,1)} %get-tuple-element.5.z_hbm, f32[256]{0:T(256)} %convert_element_type.111.mask_s, f32[2,1,128]{2,1,0:T(1,128)} %bitcast.137, bf16[2,128,512]{2,1,0:T(8,128)(2,1)} %w_proj.7, bf16[2,128,128]{2,1,0:T(8,128)(2,1)} %w_gate.7, bf16[2,128,128]{2,1,0:T(8,128)(2,1)} %w_out.13), custom_call_target="tpu_custom_call" | custom-call | tf_op jit(solution)/shard_map/tri_mult_col_5/pallas_call | solution.py:248
  699.9 68.5 %tri_att_6.1.z_ref = bf16[16,256,128]{2,1,0:T(8,128)(2,1)} custom-call(bf16[16,256,128]{2,1,0:T(8,128)(2,1)} %tri_mult_col_5.1.z_ref, f32[256,128]{1,0:T(8,128)} %broadcast_in_dim.2.mask_c, bf16[2,128,512]{2,1,0:T(8,128)(2,1)} %w_qkvg.6, bf16[2,8,128]{2,1,0:T(8,128)(2,1)} %pad.7.bias_t, bf16[2,128,128]{2,1,0:T(8,128)(2,1)} %w_out.14), custom_call_target="tpu_custom_call" | custom-call | tf_op jit(solution)/shard_map/tri_att_6/pallas_call | solution.py:415
  768.3 88.2 %tri_att_7.1 = bf16[16,256,128]{2,1,0:T(8,128)(2,1)} custom-call(bf16[16,256,128]{2,1,0:T(8,128)(2,1)} %tri_att_6.1.z_ref, f32[256,128]{1,0:T(8,128)} %broadcast_in_dim.2.mask_c, bf16[2,128,512]{2,1,0:T(8,128)(2,1)} %w_qkvg.7, bf16[2,8,128]{2,1,0:T(8,128)(2,1)} %pad.8.bias_t, bf16[2,128,128]{2,1,0:T(8,128)(2,1)} %w_out.15, bf16[2,128,1024]{2,1,0:T(8,128)(2,1)} %rest_0_.3, ...), custom_call_target="tpu_custom_call" | custom-call | tf_op jit(solution)/shard_map/tri_att_7/pallas_call | solution.py:415
  856.6 1.6 convert_reduce_fusion
  858.2 2.3 fusion.12
  860.5 0.3 convert_reduce_fusion.1
  860.9 1.3 fusion.14
  862.2 2.1 fusion.55
  864.3 2.1 fusion.57
  866.4 1.2 slice_bitcast_fusion
  867.6 0.7 copy.37
  868.3 1.7 copy.32
  870.0 2.2 fusion.109
  872.3 22.3 %all_gather.9 = bf16[256,2,16,24]{3,0,2,1:T(8,128)(2,1)S(1)} all-gather(bf16[16,2,16,24]{3,0,2,1:T(8,128)(2,1)S(1)} %slice.100), channel_id=1, replica_groups=mesh['req'=4,'dap'=16] {'dap'}, dimensions={0}, use_global_device_ids=true | all-gather | bytes 417792 | tf_op jit(solution)/shard_map/all_gather | solution.py:439
  894.6 1.3 copy-done.3
  895.9 0.4 fusion.31
  896.3 0.2 fusion.110
  896.5 1.7 fusion.34
  898.2 0.1 reshape.110
  898.4 0.3 fusion.111
  898.7 0.2 multiply_reduce_fusion.2
  898.9 2.3 fusion.8
  901.2 0.4 fusion.112
  901.6 0.2 multiply_reduce_fusion.1
  901.8 2.2 fusion.113
  904.1 21.7 %all_gather.11 = bf16[256,2,16,24]{3,0,2,1:T(8,128)(2,1)S(1)} all-gather(bf16[16,2,16,24]{3,0,2,1:T(8,128)(2,1)S(1)} %slice.107), channel_id=1, replica_groups=mesh['req'=4,'dap'=16] {'dap'}, dimensions={0}, use_global_device_ids=true | all-gather | bytes 417792 | tf_op jit(solution)/shard_map/all_gather | solution.py:439
  925.8 0.4 fusion.28
  926.2 0.2 fusion.114
  926.4 1.4 fusion.35
  928.0 1.4 fusion.115
  929.4 0.2 multiply_reduce_fusion
  929.6 2.1 fusion.6
  931.7 0.9 fusion.46
  932.6 1.0 copy.56
  (40 shorter events, 0.3 us)
Async XLA Ops:
  768.3 92.2 %copy-start.1 = (bf16[16,256,128]{2,1,0:T(8,128)(2,1)S(1)}, bf16[16,256,128]{2,1,0:T(8,128)(2,1)}, u32[]{:S(2)}) copy-start(bf16[16,256,128]{2,1,0:T(8,128)(2,1)} %get-tuple-element.4) | copy-start | bytes 3145732
  856.6 5.7 copy-start.8
  860.5 3.8 copy-start
  862.2 4.2 copy-start.2
  867.6 2.5 copy-start.5
  870.0 25.9 %copy-start.10 = (bf16[16,256,16]{1,2,0:T(8,128)(2,1)S(1)}, bf16[16,256,16]{1,2,0:T(8,128)(2,1)}, u32[]{:S(2)}) copy-start(bf16[16,256,16]{1,2,0:T(8,128)(2,1)} %fusion.55) | copy-start | bytes 393220
  894.6 1.4 copy-start.3
  896.3 2.1 copy-start.4
  898.4 2.8 copy-start.6
  901.8 24.0 %copy-start.9 = (bf16[16,256,16]{1,2,0:T(8,128)(2,1)S(1)}, bf16[16,256,16]{1,2,0:T(8,128)(2,1)}, u32[]{:S(2)}) copy-start(bf16[16,256,16]{1,2,0:T(8,128)(2,1)} %fusion.57) | copy-start | bytes 393220
  928.0 3.7 copy-start.7

commit v2 on v1

v2 whole, which is shorter than its diff:
```python
import functools

import jax
import jax.numpy as jnp
from jax import lax
from jax.experimental import pallas as pl
from jax.experimental.pallas import tpu as pltpu
from jax.sharding import PartitionSpec as P

EPS = 1e-5
NEG_BIG = 1e9
LOG2E = 1.4426950408889634
F32 = jnp.float32
BF16 = jnp.bfloat16
MESH = pl.DeviceIdType.MESH
WEIGHT_NAMES = ('tmo_proj', 'tmo_gate', 'tmo_out', 'tmi_proj', 'tmi_gate', 'tmi_out', 'tas_qkvg', 'tas_bias', 'tas_out', 'tae_qkvg', 'tae_bias', 'tae_out', 'pt_in', 'pt_out', 'ap_qkvg', 'ap_bias', 'ap_out', 'st_in', 'st_out')
LANES = 128
VMEM_LIMIT = 60 * 1024 * 1024


def dot_nn(lhs, rhs):
    return lax.dot_general(lhs, rhs, (((1,), (0,)), ((), ())), preferred_element_type=F32)


def turned(values):
    return values.astype(F32).T.astype(BF16)


def dot_nt(lhs, rhs):
    return lax.dot_general(lhs, rhs, (((1,), (1,)), ((), ())), preferred_element_type=F32)


def dot_tn(lhs, rhs):
    return lax.dot_general(lhs, rhs, (((0,), (0,)), ((), ())), preferred_element_type=F32)


def sigmoid(values):
    return 0.5 * jnp.tanh(0.5 * values) + 0.5


def layer_norm_t(values):
    values = values.astype(F32)
    centred = values - jnp.mean(values, axis=0, keepdims=True)
    variance = jnp.mean(centred * centred, axis=0, keepdims=True)
    return (centred * lax.rsqrt(variance + EPS)).astype(BF16)


def layer_norm(values):
    values = values.astype(F32)
    centred = values - jnp.mean(values, axis=-1, keepdims=True)
    variance = jnp.mean(centred * centred, axis=-1, keepdims=True)
    return (centred * lax.rsqrt(variance + EPS)).astype(BF16)


def tri_mult_kernel(kind, layer, n_dev, z_hbm, mask_s, mask_v, w_proj, w_gate, w_out, out_ref, *rest):
    if kind == 'row':
        (zfull, b_full, a_full, stage, w_t, x_buf, x_in, in_sem, right_send, right_recv, left_send, left_recv, pair_send, pair_recv, x_send, x_recv) = rest
    else:
        (zfull, b_full, a_full, a_turn, stage, w_t, x_buf, x_in, in_sem, right_send, right_recv, left_send, left_recv, pair_send, pair_recv, x_send, x_recv) = rest
    chips = n_dev // 2
    rows = zfull.shape[2]
    half_c = b_full.shape[0]
    channels = 2 * half_c
    pad = half_c + 8
    me = lax.axis_index('dap')
    chip, core = me // 2, lax.rem(me, 2)
    partner = chip * 2 + 1 - core
    right = lax.rem(chip + 1, chips) * 2 + core
    left = lax.rem(chip + chips - 1, chips) * 2 + core

    loads = [pltpu.make_async_copy(z_hbm.at[:, :, pl.ds(h * LANES, LANES)], zfull.at[me, h], in_sem.at[h]) for h in range(2)]
    for load in loads:
        load.start()
    barrier = pltpu.get_barrier_semaphore()
    for peer in (left, right, partner):
        pl.semaphore_signal(barrier, inc=1, device_id={'dap': peer}, device_id_type=MESH)
    for load in loads:
        load.wait()
    pl.semaphore_wait(barrier, 3)

    def send(block, half, send_sem, recv_sem, target):
        return pltpu.make_async_remote_copy(src_ref=zfull.at[block, half], dst_ref=zfull.at[block, half], send_sem=send_sem, recv_sem=recv_sem, device_id={'dap': target}, device_id_type=MESH)

    send(me, 0, right_send.at[0], right_recv.at[0], right).start()
    send(me, 1, left_send.at[0], left_recv.at[0], left).start()
    send(me, 1, right_send.at[1], right_recv.at[1], right).start()
    send(me, 0, left_send.at[1], left_recv.at[1], left).start()
    send(me, 0, pair_send.at[0], pair_recv.at[0], partner).start()
    send(me, 1, pair_send.at[1], pair_recv.at[1], partner).start()

    x_buf[0, 0, :4 * channels, :] = w_proj[layer].astype(F32).T
    for spot, part in enumerate((2, 3, 0, 1)):
        w_t[spot * half_c:(spot + 1) * half_c, :] = x_buf[0, 0, pl.ds(pl.multiple_of(part * channels + core * half_c, half_c), half_c), :].astype(BF16)

    my_half = chip // (chips // 2)
    my_off = pl.multiple_of(lax.rem(chip, chips // 2) * 2 * rows, 2 * rows)

    def project(block, half, operands):
        tok_mask = mask_v[half]
        weights = w_t[:operands * channels, :]

        @pl.loop(0, rows // 2)
        def _(pair):
            normed = jnp.concatenate([layer_norm_t(zfull[block, half, 2 * pair + t]) for t in range(2)], axis=1)
            slab = dot_nn(weights, normed)
            for o in range(operands):
                gated = sigmoid(slab[o * channels + half_c:(o + 1) * channels]) * slab[o * channels:o * channels + half_c]
                for t in range(2):
                    row = 2 * pair + t
                    stage[o, pl.ds(pl.multiple_of(row * pad, 8), half_c), :] = gated[:, t * LANES:(t + 1) * LANES] * (tok_mask * mask_s[block * rows + row])

        spot = pl.multiple_of(block * rows, rows)

        @pl.loop(0, half_c // 16)
        def _(group):
            for t in range(16):
                c = group * 16 + t
                b_full[c, half, pl.ds(spot, rows), :] = stage[0, pl.ds(c, rows, stride=pad), :].astype(BF16)
                if operands == 2:
                    left_operand = stage[1, pl.ds(c, rows, stride=pad), :].astype(BF16)
                    if kind == 'row':
                        a_full[c, half, pl.ds(pl.multiple_of(lax.rem(block, 2) * rows, rows), rows), :] = left_operand
                    else:
                        a_full[c, pl.ds(spot, rows), :] = left_operand

    def process(block, half, mine):
        if kind == 'row':
            project(block, half, 2 if mine else 1)
        else:
            @pl.when(half == my_half)
            def _():
                project(block, half, 2)

            @pl.when(half != my_half)
            def _():
                project(block, half, 1)

    @pl.loop(0, 4)
    def _(t):
        who, half = t // 2, lax.rem(t, 2)
        block = jnp.where(who == 0, me, partner)

        @pl.when(who == 1)
        def _():
            send(partner, half, pair_send.at[half], pair_recv.at[half], partner).wait_recv()

        process(block, half, True)

    events = chips - 1

    @pl.loop(0, events)
    def _(e):
        dist = e // 2 + 1
        half_r = lax.rem(e, 2)
        half_l = 1 - half_r
        from_left = lax.rem(chip - dist + chips, chips)
        from_right = lax.rem(chip + dist, chips)
        block_r, block_l = from_left * 2 + core, from_right * 2 + core
        send(block_r, half_r, right_send.at[e], right_recv.at[e], right).wait_recv()

        @pl.when(e + 2 < events)
        def _():
            send(block_r, half_r, right_send.at[e + 2], right_recv.at[e + 2], right).start()

        send(block_r, half_r, pair_send.at[2 * e + 2], pair_recv.at[2 * e + 2], partner).start()
        send(block_l, half_l, left_send.at[e], left_recv.at[e], left).wait_recv()

        @pl.when(e + 2 < events)
        def _():
            send(block_l, half_l, left_send.at[e + 2], left_recv.at[e + 2], left).start()

        send(block_l, half_l, pair_send.at[2 * e + 3], pair_recv.at[2 * e + 3], partner).start()

        @pl.loop(0, 4)
        def _(t):
            side, other = lax.rem(t, 2), t // 2
            owner = jnp.where(other == 0, core, 1 - core)
            block = jnp.where(side == 0, from_left, from_right) * 2 + owner
            half = jnp.where(side == 0, half_r, half_l)

            @pl.when(other == 1)
            def _():
                send(block, half, pair_send.at[2 * e + 2 + side], pair_recv.at[2 * e + 2 + side], partner).wait_recv()

            process(block, half, False)

    if kind != 'row':
        @pl.loop(0, half_c // 4)
        def _(group):
            for t in range(4):
                a_turn[group * 4 + t] = a_full[group * 4 + t].T

    @pl.loop(0, half_c // 4)
    def _(group):
        for t in range(4):
            c = group * 4 + t
            rhs = jnp.concatenate([b_full[c, 0], b_full[c, 1]], axis=1)
            if kind == 'row':
                product = dot_nt(jnp.concatenate([a_full[c, 0], a_full[c, 1]], axis=1), rhs)
            else:
                product = dot_nn(a_turn[c, pl.ds(my_off, 2 * rows), :], rhs)
            for who in range(2):
                for half in range(2):
                    x_buf[who, half, pl.ds(c, rows, stride=pad), :] = product[who * rows:(who + 1) * rows, half * LANES:(half + 1) * LANES]

    exchange = pltpu.make_async_remote_copy(src_ref=x_buf.at[1 - core], dst_ref=x_in, send_sem=x_send, recv_sem=x_recv, device_id={'dap': partner}, device_id_type=MESH)
    for e in range(events):
        send(me, 0, right_send.at[e], right_recv.at[e], right).wait_send()
        send(me, 0, left_send.at[e], left_recv.at[e], left).wait_send()
    for e in range(2 * events + 2):
        send(me, 0, pair_send.at[e], pair_recv.at[e], partner).wait_send()
    exchange.start()
    w_own = w_out[layer, pl.ds(pl.multiple_of(core * half_c, half_c), half_c), :]
    w_other = w_out[layer, pl.ds(pl.multiple_of((1 - core) * half_c, half_c), half_c), :]
    w_t[:channels, :] = turned(jnp.concatenate([w_own, w_other], axis=0))
    w_t[channels:2 * channels, :] = turned(w_gate[layer])
    exchange.wait()

    @pl.loop(0, rows)
    def _(i):
        for half in range(2):
            x = jnp.concatenate([x_buf[core, half, pl.ds(pl.multiple_of(i * pad, 8), half_c), :], x_in[half, pl.ds(pl.multiple_of(i * pad, 8), half_c), :]], axis=0)
            update = dot_nn(w_t[:channels, :], layer_norm_t(x))
            z_row = zfull[me, half, i]
            gate = sigmoid(dot_nn(w_t[channels:2 * channels, :], layer_norm_t(z_row)))
            out_ref[i, :, half * LANES:(half + 1) * LANES] = (z_row.astype(F32) + gate * update).astype(BF16)


def tri_mult(kind, layer, n_dev, cid, z, mask_s, mask_v, w_proj, w_gate, w_out):
    rows, channels, tokens = z.shape
    assert tokens == 2 * LANES and channels == LANES and rows * n_dev == tokens
    half_c = channels // 2
    pad = half_c + 8
    events = n_dev // 2 - 1
    vmem = pl.BlockSpec(memory_space=pltpu.VMEM)
    dma = pltpu.SemaphoreType.DMA
    left_operand = [pltpu.VMEM((half_c, 2, 2 * rows, LANES), BF16)]
    if kind != 'row':
        left_operand = [pltpu.VMEM((half_c, tokens, LANES), BF16), pltpu.VMEM((half_c, LANES, tokens), BF16)]
    return pl.pallas_call(
        functools.partial(tri_mult_kernel, kind, layer, n_dev),
        out_shape=jax.ShapeDtypeStruct(z.shape, BF16),
        in_specs=[pl.BlockSpec(memory_space=pl.ANY), pl.BlockSpec(memory_space=pltpu.SMEM), vmem, vmem, vmem, vmem],
        out_specs=vmem,
        scratch_shapes=[
            pltpu.VMEM((n_dev, 2, rows, channels, LANES), BF16),
            pltpu.VMEM((half_c, 2, tokens, LANES), BF16),
            *left_operand,
            pltpu.VMEM((2, rows * pad, LANES), F32),
            pltpu.VMEM((2 * channels, channels), BF16),
            pltpu.VMEM((2, 2, rows * pad, LANES), F32),
            pltpu.VMEM((2, rows * pad, LANES), F32),
            dma((2,)), dma((events,)), dma((events,)), dma((events,)), dma((events,)), dma((2 * events + 2,)), dma((2 * events + 2,)), dma, dma,
        ],
        compiler_params=pltpu.CompilerParams(collective_id=cid, has_side_effects=True, vmem_limit_bytes=VMEM_LIMIT),
        name=f'tri_mult_{kind}_{cid}',
    )(z, mask_s, mask_v, w_proj, w_gate, w_out)


def tri_att_kernel(layer, n_dev, heads, last, trans, share, z_ref, mask_c, w_qkvg, bias_t, w_out, *rest):
    rest = list(rest)
    pt_in, pt_out = (rest.pop(0), rest.pop(0)) if trans else (None, None)
    kv_in = rest.pop(0) if share else None
    out_ref = rest.pop(0)
    kv_all = rest.pop(0) if share else None
    (normed_s, bias_s, bias_all, logit_bias, w_t, w_o, k_s, q_s, v_s, g_s, z_nat, r_buf, stage, b_send, b_recv, t_send, t_recv, own_sem) = rest[:18]
    rest = rest[18:]
    pt_in_t, pt_out_t = (rest.pop(0), rest.pop(0)) if trans else (None, None)
    kv_buf, kv_send, kv_recv = (rest.pop(0), rest.pop(0), rest.pop(0)) if share else (None, None, None)
    rows, channels, tokens = z_ref.shape
    width = channels // heads
    me = lax.axis_index('dap')
    barrier = pltpu.get_barrier_semaphore()
    peers = [lax.rem(me + p, n_dev) for p in range(1, n_dev)]
    for peer in peers:
        pl.semaphore_signal(barrier, inc=1, device_id={'dap': peer}, device_id_type=MESH)

    @pl.loop(0, rows)
    def _(i):
        normed = layer_norm_t(z_ref[i])
        normed_s[i] = normed
        slab = dot_nn(bias_t[layer], normed)
        for half in range(2):
            bias_s[half, pl.ds(pl.multiple_of(i * 8, 8), 8), :] = slab[:, half * LANES:(half + 1) * LANES]

    spot = pl.multiple_of(me * rows, rows)
    for h in range(heads):
        for half in range(2):
            bias_all[h, pl.ds(spot, rows), half * LANES:(half + 1) * LANES] = bias_s[half, pl.ds(h, rows, stride=8), :].astype(BF16)
    if share:
        kv_buf[pl.ds(spot, rows), :] = kv_in[...]
    w_t[...] = turned(w_qkvg[layer])
    w_o[...] = turned(w_out[layer])
    if trans:
        for part in range(0, pt_in_t.shape[0], channels):
            pt_in_t[part:part + channels, :] = turned(pt_in[layer, :, part:part + channels])
        pt_out_t[...] = turned(pt_out[layer])
    pl.semaphore_wait(barrier, n_dev - 1)

    def bias_copy(owner, p, target):
        ref = bias_all.at[:, pl.ds(pl.multiple_of(owner * rows, rows), rows), :]
        return pltpu.make_async_remote_copy(src_ref=ref, dst_ref=ref, send_sem=b_send.at[p - 1], recv_sem=b_recv.at[p - 1], device_id={'dap': target}, device_id_type=MESH)

    def kv_copy(owner, p, target):
        ref = kv_buf.at[pl.ds(pl.multiple_of(owner * rows, rows), rows), :]
        return pltpu.make_async_remote_copy(src_ref=ref, dst_ref=ref, send_sem=kv_send.at[p - 1], recv_sem=kv_recv.at[p - 1], device_id={'dap': target}, device_id_type=MESH)

    for p in range(1, n_dev):
        bias_copy(me, p, peers[p - 1]).start()
    if share:
        for p in range(1, n_dev):
            kv_copy(me, p, peers[p - 1]).start()

    @pl.loop(0, rows)
    def _(i):
        slab = dot_nn(w_t[...], normed_s[i])
        q_s[i] = slab[:channels].astype(BF16)
        k_s[i] = slab[channels:2 * channels].T.astype(BF16)
        v_s[i] = slab[2 * channels:3 * channels].astype(BF16)
        g_s[i] = sigmoid(slab[3 * channels:])

    for p in range(1, n_dev):
        bias_copy(lax.rem(me + n_dev - p, n_dev), p, peers[p - 1]).wait_recv()
    for h in range(heads):
        for qh in range(2):
            for kh in range(2):
                tile = bias_all[h, qh * LANES:(qh + 1) * LANES, kh * LANES:(kh + 1) * LANES].astype(F32).T
                logit_bias[h, kh * LANES:(kh + 1) * LANES, qh * LANES:(qh + 1) * LANES] = (tile + mask_c[kh * LANES:(kh + 1) * LANES, :]) * LOG2E
    scale = width ** -0.5 * LOG2E

    def turn_copy(source, t, p, target, to):
        return pltpu.make_async_remote_copy(
            src_ref=z_nat.at[pl.ds(4 * t, 4), pl.ds(pl.multiple_of(to * rows, rows), rows), :], dst_ref=r_buf.at[source, pl.ds(4 * t, 4)],
            send_sem=t_send.at[p - 1], recv_sem=t_recv.at[p - 1], device_id={'dap': target}, device_id_type=MESH)

    @pl.loop(0, rows)
    def _(i):
        keys = k_s[i]
        parts = []
        for h in range(heads):
            pieces = [q_s[i, h * width:(h + 1) * width, :]]
            if h:
                pieces = [jnp.zeros((h * width, tokens), BF16)] + pieces
            if h < heads - 1:
                pieces = pieces + [jnp.zeros(((heads - 1 - h) * width, tokens), BF16)]
            scores = dot_nn(keys, jnp.concatenate(pieces, axis=0))
            halves = []
            for qh in range(2):
                lanes = slice(qh * LANES, (qh + 1) * LANES)
                logits = scores[:, lanes] * scale + logit_bias[h, :, lanes]
                weights = jnp.exp2(logits - jnp.max(logits, axis=0, keepdims=True))
                total = jnp.sum(weights, axis=0, keepdims=True)
                halves.append((weights * (1.0 / total)).astype(BF16))
            parts.append(dot_nn(v_s[i, h * width:(h + 1) * width, :], jnp.concatenate(halves, axis=1)))
        merged = (jnp.concatenate(parts, axis=0) * g_s[i]).astype(BF16)
        z_row = (z_ref[i].astype(F32) + dot_nn(w_o[...], merged)).astype(BF16)
        if trans:
            normed = layer_norm_t(z_row)
            hidden = pt_out.shape[1]
            update = jnp.zeros((channels, tokens), F32)
            for part in range(0, hidden, channels):
                first = dot_nn(pt_in_t[part:part + channels, :], normed)
                second = dot_nn(pt_in_t[hidden + part:hidden + part + channels, :], normed)
                update = update + dot_nn(pt_out_t[:, part:part + channels], (first * sigmoid(first) * second).astype(BF16))
            z_row = (z_row.astype(F32) + update).astype(BF16)
        z_nat[i] = turned(z_row)

        @pl.when((lax.rem(i, 4) == 0) & (i > 0))
        def _():
            for p in range(1, n_dev):
                turn_copy(me, i // 4 - 1, p, peers[p - 1], peers[p - 1]).start()

    own = pltpu.make_async_copy(z_nat.at[:, pl.ds(spot, rows), :], r_buf.at[me], own_sem)
    own.start()
    for p in range(1, n_dev):
        turn_copy(me, rows // 4 - 1, p, peers[p - 1], peers[p - 1]).start()
    own.wait()

    def whole(source, p, target):
        return pltpu.make_async_remote_copy(src_ref=r_buf.at[source], dst_ref=r_buf.at[source], send_sem=t_send.at[p - 1], recv_sem=t_recv.at[p - 1], device_id={'dap': target}, device_id_type=MESH)

    def place(source):
        pad = rows + 8
        for i in range(rows):
            stage[i * pad:i * pad + rows, :] = r_buf[source, i].astype(F32)
        for j in range(rows):
            placed_values = stage[pl.ds(j, rows, stride=pad), :].astype(BF16)
            if last:
                out_ref[j, pl.ds(pl.multiple_of(source * rows, rows), rows), :] = placed_values
            else:
                q_all[j, pl.ds(pl.multiple_of(source * rows, rows), rows), :] = placed_values

    q_all = k_s
    place(me)

    @pl.loop(1, n_dev)
    def _(p):
        source = lax.rem(me + n_dev - p, n_dev)
        whole(source, p, lax.rem(me + p, n_dev)).wait_recv()
        place(source)

    if not last:
        @pl.loop(0, rows)
        def _(j):
            out_ref[j] = turned(q_all[j])

    for p in range(1, n_dev):
        whole(me, p, peers[p - 1]).wait_send()
        bias_copy(me, p, peers[p - 1]).wait_send()
        if share:
            kv_copy(me, p, peers[p - 1]).wait_send()
            kv_copy(lax.rem(me + n_dev - p, n_dev), p, peers[p - 1]).wait_recv()
    if share:
        kv_all[...] = kv_buf[...]


def tri_att(layer, n_dev, cid, last, z, mask_c, w_qkvg, bias_t, heads, w_out, pt=(), kv=None):
    rows, channels, tokens = z.shape
    vmem = pl.BlockSpec(memory_space=pltpu.VMEM)
    dma = pltpu.SemaphoreType.DMA
    share = kv is not None
    scratch = [
        pltpu.VMEM((rows, channels, tokens), BF16),
        pltpu.VMEM((2, rows * 8, LANES), F32),
        pltpu.VMEM((heads, tokens, tokens), BF16),
        pltpu.VMEM((heads, tokens, tokens), F32),
        pltpu.VMEM((4 * channels, channels), BF16),
        pltpu.VMEM((channels, channels), BF16),
        pltpu.VMEM((rows, tokens, channels), BF16),
        pltpu.VMEM((rows, channels, tokens), BF16),
        pltpu.VMEM((rows, channels, tokens), BF16),
        pltpu.VMEM((rows, channels, tokens), F32),
        pltpu.VMEM((rows, tokens, channels), BF16),
        pltpu.VMEM((n_dev, rows, rows, channels), BF16),
        pltpu.VMEM((rows * (rows + 8), LANES), F32),
        dma((n_dev - 1,)), dma((n_dev - 1,)), dma((n_dev - 1,)), dma((n_dev - 1,)), dma,
    ]
    if pt:
        scratch += [pltpu.VMEM(pt[0].shape[:0:-1], BF16), pltpu.VMEM(pt[1].shape[:0:-1], BF16)]
    shape = jax.ShapeDtypeStruct((rows, tokens, channels) if last else z.shape, BF16)
    if share:
        kv_shape = jax.ShapeDtypeStruct((tokens, kv.shape[1]), BF16)
        scratch += [pltpu.VMEM(kv_shape.shape, BF16), dma((n_dev - 1,)), dma((n_dev - 1,))]
    return pl.pallas_call(
        functools.partial(tri_att_kernel, layer, n_dev, heads, last, bool(pt), share),
        out_shape=(shape, kv_shape) if share else shape,
        in_specs=[vmem] * (5 + len(pt) + share),
        out_specs=(vmem, vmem) if share else vmem,
        scratch_shapes=scratch,
        compiler_params=pltpu.CompilerParams(collective_id=cid, has_side_effects=True, vmem_limit_bytes=VMEM_LIMIT),
        name=f'tri_att_{cid}',
    )(z, mask_c, w_qkvg, bias_t, w_out, *pt, *((kv,) if share else ()))


def transition(act_in, w_in, w_out):
    hidden = w_out.shape[0]
    projected = jnp.dot(layer_norm(act_in), w_in, preferred_element_type=F32)
    inner = (jax.nn.silu(projected[..., :hidden]) * projected[..., hidden:]).astype(BF16)
    return (act_in.astype(F32) + jnp.dot(inner, w_out, preferred_element_type=F32)).astype(BF16)


def single_inputs(single, w_qkvg):
    width = w_qkvg.shape[1] // 4
    projected = jnp.dot(layer_norm(single), w_qkvg, preferred_element_type=F32)
    return projected[:, :width].astype(BF16), projected[:, width:3 * width].astype(BF16), jax.nn.sigmoid(projected[:, 3 * width:])


def single_step(single, query, gate, kv_all, pair_bias, mask_all, w_out, st_in, st_out):
    rows, tokens = single.shape[0], kv_all.shape[0]
    heads = pair_bias.shape[1]
    head_dim = query.shape[1] // heads
    query, gate = query.reshape(rows, heads, head_dim), gate.reshape(rows, heads, head_dim)
    kv_all = kv_all.reshape(tokens, 2, heads, head_dim)
    logits = jnp.einsum('ihd,jhd->ihj', query, kv_all[:, 0], preferred_element_type=F32) * head_dim ** -0.5 + pair_bias.astype(F32) + (mask_all.astype(F32) - 1.0) * NEG_BIG
    soft_scores = jax.nn.softmax(logits, axis=-1).astype(BF16)
    attended = jnp.einsum('ihj,jhd->ihd', soft_scores, kv_all[:, 1], preferred_element_type=F32)
    merged = (attended * gate).astype(BF16).reshape(rows, -1)
    single = (single.astype(F32) + jnp.dot(merged, w_out, preferred_element_type=F32)).astype(BF16)
    return transition(single, st_in, st_out)


def solution(mesh):
    row_spec = P(('req', 'dap'))
    single_spec = P(('req', 'dap'), None)
    pair_spec = P(('req', 'dap'), None, None)
    n_dev = mesh.shape['dap']

    def local_program(single, pair, token_mask, *weights):
        w = dict(zip(WEIGHT_NAMES, weights))
        blocks = weights[0].shape[0]
        mask_all = lax.all_gather(token_mask, 'dap', tiled=True)
        tokens = mask_all.shape[0]
        mask_f = mask_all.astype(F32)
        mask_v = mask_f.reshape(2, 1, tokens // 2)
        mask_c = jnp.broadcast_to(((mask_f - 1.0) * NEG_BIG)[:, None], (tokens, LANES))
        heads = w['tas_bias'].shape[2]

        def bias_rows(name):
            swapped = jnp.swapaxes(w[name], 1, 2)
            return jnp.pad(swapped, ((0, 0), (0, 8 - heads), (0, 0)))

        tas_bias, tae_bias = bias_rows('tas_bias'), bias_rows('tae_bias')
        pair = jnp.swapaxes(pair, 1, 2)
        for b in range(blocks):
            cid = 4 * b
            last = b == blocks - 1
            query, kv, gate = single_inputs(single, w['ap_qkvg'][b])
            pair = tri_mult('row', b, n_dev, cid, pair, mask_f, mask_v, w['tmo_proj'], w['tmo_gate'], w['tmo_out'])
            pair = tri_mult('col', b, n_dev, cid + 1, pair, mask_f, mask_v, w['tmi_proj'], w['tmi_gate'], w['tmi_out'])
            pair, kv_all = tri_att(b, n_dev, cid + 2, False, pair, mask_c, w['tas_qkvg'], tas_bias, heads, w['tas_out'], (), kv)
            pair = tri_att(b, n_dev, cid + 3, last, pair, mask_c, w['tae_qkvg'], tae_bias, heads, w['tae_out'], (w['pt_in'], w['pt_out']))
            if last:
                pair_bias = jnp.einsum('ijc,ch->ihj', layer_norm(pair), w['ap_bias'][b], preferred_element_type=F32).astype(BF16)
            else:
                centred = pair.astype(F32) - jnp.mean(pair.astype(F32), axis=1, keepdims=True)
                normed = (centred * lax.rsqrt(jnp.mean(centred * centred, axis=1, keepdims=True) + EPS)).astype(BF16)
                pair_bias = jnp.einsum('icj,ch->ihj', normed, w['ap_bias'][b], preferred_element_type=F32).astype(BF16)
            single = single_step(single, query, gate, kv_all, pair_bias, mask_all, w['ap_out'][b], w['st_in'][b], w['st_out'][b])
        return single, pair

    return jax.shard_map(local_program, mesh=mesh, in_specs=(single_spec, pair_spec, row_spec) + (P(),) * len(WEIGHT_NAMES), out_specs=(single_spec, pair_spec), check_vma=False)
```

time: 934 us -> 729 us (0.78)
  Pallas kernels: 831 us -> 680 us
  blocking collectives: 60.1 us -> 16.1 us
    pallas_call x4, Pallas kernels: 534 us -> 421 us  [tri_mult(): pl.pallas_call(functools.partial(tri_mult_kernel, kind, layer, n_dev), ou...]
    all_gather x2 -> x0, blocking collectives: 44 us -> none  [single_step(): kv_all = lax.all_gather(projected[:, 1:3].astype(BF16), 'dap', tiled=True)]
    pallas_call x4, Pallas kernels: 298 us -> 259 us  [tri_att(): pl.pallas_call(functools.partial(tri_att_kernel, layer, n_dev, heads, las...]
where the time goes in v2:
time: 729 us; the launch traced here: 728 us
  Pallas kernels  680 us (93%)
  blocking collectives  16.1 us (2%)
  matrix products  11.2 us (2%)
  local copies, waits for them, and re-layouts  9.65 us (1%)
  other arithmetic  8.9 us (1%)
    pallas_call x4, Pallas kernels, tri_mult(): pl.pallas_call(functools.partial(tri_mult_kernel, kind, layer, n_dev), ou...  421 us
    pallas_call x4, Pallas kernels, tri_att(): pl.pallas_call(functools.partial(tri_att_kernel, layer, n_dev, heads, las...  259 us
    unnamed x1, blocking collectives  16.1 us

profile of v2, /device:TPU:21, one launch (start us, length us, event | category | flops | bytes accessed | tf_op | source)
XLA Modules:
  0.0 727.6 jit_solution(14586204711318740819)
XLA Ops:
  0.6 1.2 dynamic-slice
  2.5 0.9 dynamic-update-slice
  3.4 16.1 %all-reduce.2 = s32[256]{0:T(256)S(1)} all-reduce(s32[256]{0:T(256)S(1)} %dynamic-update-slice), channel_id=1, replica_groups=mesh['req'=4,'dap'=16] {'dap'}, use_global_device_ids=true, to_apply=%add.2 | all-reduce | flops 256 | bytes 2048
  19.5 0.5 convert_element_type.104.mask_s
  20.0 2.3 copy.35
  22.3 105.1 %tri_mult_row_0.1.z_hbm = bf16[16,128,256]{2,1,0:T(8,128)(2,1)} custom-call(bf16[16,128,256]{2,1,0:T(8,128)(2,1)} %bitcast.105, f32[256]{0:T(256)} %convert_element_type.104.mask_s, f32[2,1,128]{2,1,0:T(1,128)} %bitcast.110, bf16[2,128,512]{2,1,0:T(8,128)(2,1)} %w_proj.6, bf16[2,128,128]{2,1,0:T(8,128)(2,1)} %w_gate.6, bf16[2,128,128]{2,1,0:T(8,128)(2,1)} %w_out.12), custom_call_target="tpu_custom_call" | custom-call | tf_op jit(solution)/shard_map/tri_mult_row_0/pallas_call | solution.py:240
  127.4 106.2 %tri_mult_col_1.1.z_ref = bf16[16,128,256]{2,1,0:T(8,128)(2,1)} custom-call(bf16[16,128,256]{2,1,0:T(8,128)(2,1)} %tri_mult_row_0.1.z_hbm, f32[256]{0:T(256)} %convert_element_type.104.mask_s, f32[2,1,128]{2,1,0:T(1,128)} %bitcast.111, bf16[2,128,512]{2,1,0:T(8,128)(2,1)} %w_proj.7, bf16[2,128,128]{2,1,0:T(8,128)(2,1)} %w_gate.7, bf16[2,128,128]{2,1,0:T(8,128)(2,1)} %w_out.13), custom_call_target="tpu_custom_call" | custom-call | tf_op jit(solution)/shard_map/tri_mult_col_1/pallas_call | solution.py:240
  233.6 0.8 broadcast_in_dim.2.mask_c
  234.5 0.2 fusion.85
  234.7 0.3 fusion.110
  235.0 0.6 slice.100.rest_0_
  235.7 0.6 pad.7.bias_t
  236.2 59.8 %tri_att_2.1 = (bf16[16,128,256]{2,1,0:T(8,128)(2,1)}, bf16[256,768]{1,0:T(8,128)(2,1)}) custom-call(bf16[16,128,256]{2,1,0:T(8,128)(2,1)} %tri_mult_col_1.1.z_ref, f32[256,128]{1,0:T(8,128)} %broadcast_in_dim.2.mask_c, bf16[2,128,512]{2,1,0:T(8,128)(2,1)} %w_qkvg.6, bf16[2,8,128]{2,1,0:T(8,128)(2,1)} %pad.7.bias_t, bf16[2,128,128]{2,1,0:T(8,128)(2,1)} %w_out.14, ...), custom_call_target="tpu_custom_call" | custom-call | tf_op jit(solution)/shard_map/tri_att_2/pallas_call | solution.py:444
  296.1 0.6 pad.8.bias_t
  296.7 70.2 %tri_att_3.1.z_hbm = bf16[16,128,256]{2,1,0:T(8,128)(2,1)} custom-call(bf16[16,128,256]{2,1,0:T(8,128)(2,1)} %get-tuple-element.7.z_ref, f32[256,128]{1,0:T(8,128)} %broadcast_in_dim.2.mask_c, bf16[2,128,512]{2,1,0:T(8,128)(2,1)} %w_qkvg.7, bf16[2,8,128]{2,1,0:T(8,128)(2,1)} %pad.8.bias_t, bf16[2,128,128]{2,1,0:T(8,128)(2,1)} %w_out.15, ...), custom_call_target="tpu_custom_call" | custom-call | tf_op jit(solution)/shard_map/tri_att_3/pallas_call | solution.py:444
  366.9 1.5 convert_reduce_fusion.1
  368.5 1.5 fusion.14
  370.0 0.4 fusion.61
  370.4 0.2 copy.36
  370.6 0.1 reshape.111
  370.7 0.2 fusion.35
  370.9 0.2 fusion.111
  371.2 0.5 fusion.41
  371.8 0.1 reshape.113
  371.9 1.4 fusion.112
  373.3 0.2 multiply_reduce_fusion.2
  373.5 2.1 fusion.8
  375.6 0.4 fusion.113
  376.0 0.2 multiply_reduce_fusion.1
  376.2 0.3 fusion.114
  376.6 0.6 slice.107.rest_0_
  377.2 103.9 %tri_mult_row_4.1.z_hbm = bf16[16,128,256]{2,1,0:T(8,128)(2,1)} custom-call(bf16[16,128,256]{2,1,0:T(8,128)(2,1)} %tri_att_3.1.z_hbm, f32[256]{0:T(256)} %convert_element_type.104.mask_s, f32[2,1,128]{2,1,0:T(1,128)} %bitcast.112, bf16[2,128,512]{2,1,0:T(8,128)(2,1)} %w_proj.6, bf16[2,128,128]{2,1,0:T(8,128)(2,1)} %w_gate.6, bf16[2,128,128]{2,1,0:T(8,128)(2,1)} %w_out.12), custom_call_target="tpu_custom_call" | custom-call | tf_op jit(solution)/shard_map/tri_mult_row_4/pallas_call | solution.py:240
  481.1 105.6 %tri_mult_col_5.1.z_ref = bf16[16,128,256]{2,1,0:T(8,128)(2,1)} custom-call(bf16[16,128,256]{2,1,0:T(8,128)(2,1)} %tri_mult_row_4.1.z_hbm, f32[256]{0:T(256)} %convert_element_type.104.mask_s, f32[2,1,128]{2,1,0:T(1,128)} %bitcast.113, bf16[2,128,512]{2,1,0:T(8,128)(2,1)} %w_proj.7, bf16[2,128,128]{2,1,0:T(8,128)(2,1)} %w_gate.7, bf16[2,128,128]{2,1,0:T(8,128)(2,1)} %w_out.13), custom_call_target="tpu_custom_call" | custom-call | tf_op jit(solution)/shard_map/tri_mult_col_5/pallas_call | solution.py:240
  586.7 59.9 %tri_att_6.1 = (bf16[16,128,256]{2,1,0:T(8,128)(2,1)}, bf16[256,768]{1,0:T(8,128)(2,1)}) custom-call(bf16[16,128,256]{2,1,0:T(8,128)(2,1)} %tri_mult_col_5.1.z_ref, f32[256,128]{1,0:T(8,128)} %broadcast_in_dim.2.mask_c, bf16[2,128,512]{2,1,0:T(8,128)(2,1)} %w_qkvg.6, bf16[2,8,128]{2,1,0:T(8,128)(2,1)} %pad.7.bias_t, bf16[2,128,128]{2,1,0:T(8,128)(2,1)} %w_out.14, ...), custom_call_target="tpu_custom_call" | custom-call | tf_op jit(solution)/shard_map/tri_att_6/pallas_call | solution.py:444
  646.6 69.2 %tri_att_7.1 = bf16[16,256,128]{2,1,0:T(8,128)(2,1)} custom-call(bf16[16,128,256]{2,1,0:T(8,128)(2,1)} %get-tuple-element.9.z_ref, f32[256,128]{1,0:T(8,128)} %broadcast_in_dim.2.mask_c, bf16[2,128,512]{2,1,0:T(8,128)(2,1)} %w_qkvg.7, bf16[2,8,128]{2,1,0:T(8,128)(2,1)} %pad.8.bias_t, bf16[2,128,128]{2,1,0:T(8,128)(2,1)} %w_out.15, ...), custom_call_target="tpu_custom_call" | custom-call | tf_op jit(solution)/shard_map/tri_att_7/pallas_call | solution.py:444
  715.8 1.7 convert_reduce_fusion
  717.5 2.3 fusion.12
  719.9 1.5 fusion.63
  721.4 0.2 copy.41
  721.7 0.2 fusion.32
  721.9 0.2 fusion.115
  722.2 0.5 fusion.40
  722.7 0.1 reshape.117
  722.9 0.3 fusion.116
  723.2 0.2 multiply_reduce_fusion
  723.4 2.3 fusion.6
  725.7 0.9 fusion.52
  726.6 1.0 copy.60
  (48 shorter events, 0.7 us)
Async XLA Ops:
  22.3 212.1 %copy-start.6 = (bf16[16,384]{1,0:T(8,128)(2,1)S(1)}, bf16[16,384]{1,0:T(8,128)(2,1)}, u32[]{:S(2)}) copy-start(bf16[16,384]{1,0:T(8,128)(2,1)} %param.22) | copy-start | bytes 36868
  22.3 212.4 %copy-start.2 = (bf16[2,384,1536]{2,1,0:T(8,128)(2,1)S(1)}, bf16[2,384,1536]{2,1,0:T(8,128)(2,1)}, u32[]{:S(2)}) copy-start(bf16[2,384,1536]{2,1,0:T(8,128)(2,1)} %param.39) | copy-start | bytes 7077892
  127.4 108.3 %copy-start.7 = (bf16[2,128,4]{1,2,0:T(4,128)(2,1)S(1)}, bf16[2,128,4]{1,2,0:T(4,128)(2,1)}, u32[]{:S(2)}) copy-start(bf16[2,128,4]{1,2,0:T(4,128)(2,1)} %param.32) | copy-start | bytes 6148
  233.6 62.5 %copy-start.8 = (bf16[2,128,4]{1,2,0:T(4,128)(2,1)S(1)}, bf16[2,128,4]{1,2,0:T(4,128)(2,1)}, u32[]{:S(2)}) copy-start(bf16[2,128,4]{1,2,0:T(4,128)(2,1)} %param.35) | copy-start | bytes 6148
  296.7 73.3 %copy-start.11 = (bf16[2,128,16]{1,2,0:T(8,128)(2,1)S(1)}, bf16[2,128,16]{1,2,0:T(8,128)(2,1)}, u32[]{:S(2)}) copy-start(bf16[2,128,16]{1,2,0:T(8,128)(2,1)} %param.40) | copy-start | bytes 24580
  366.9 3.1 copy-start
  366.9 3.4 copy-start.5
  371.9 3.7 copy-start.9
  715.8 4.1 copy-start.1
  715.8 5.5 copy-start.4
  721.4 1.5 copy-start.3
  722.9 2.8 copy-start.10

commit v3 on v2

--- a/solution.py
+++ b/solution.py
@@ -15,6 +15,7 @@
 MESH = pl.DeviceIdType.MESH
 WEIGHT_NAMES = ('tmo_proj', 'tmo_gate', 'tmo_out', 'tmi_proj', 'tmi_gate', 'tmi_out', 'tas_qkvg', 'tas_bias', 'tas_out', 'tae_qkvg', 'tae_bias', 'tae_out', 'pt_in', 'pt_out', 'ap_qkvg', 'ap_bias', 'ap_out', 'st_in', 'st_out')
 LANES = 128
+TURN = 2
 VMEM_LIMIT = 60 * 1024 * 1024
 
 
@@ -52,11 +53,17 @@
     return (centred * lax.rsqrt(variance + EPS)).astype(BF16)
 
 
-def tri_mult_kernel(kind, layer, n_dev, z_hbm, mask_s, mask_v, w_proj, w_gate, w_out, out_ref, *rest):
+def tri_mult_kernel(kind, layer, n_dev, first, heads, z_hbm, mask_ref, w_proj, w_gate, w_out, *rest):
+    rest = list(rest)
+    bias_t = rest.pop(0) if heads else None
+    out_ref = rest.pop(0)
+    mask_out = rest.pop(0) if first else None
+    bias_out = rest.pop(0) if heads else None
+    mask_send, mask_recv = (rest.pop(), rest.pop()) if first else (None, None)
     if kind == 'row':
-        (zfull, b_full, a_full, stage, w_t, x_buf, x_in, in_sem, right_send, right_recv, left_send, left_recv, pair_send, pair_recv, x_send, x_recv) = rest
+        (zfull, b_full, a_full, stage, w_t, x_buf, x_in, mask_l, in_sem, right_send, right_recv, left_send, left_recv, pair_send, pair_recv, x_send, x_recv) = rest
     else:
-        (zfull, b_full, a_full, a_turn, stage, w_t, x_buf, x_in, in_sem, right_send, right_recv, left_send, left_recv, pair_send, pair_recv, x_send, x_recv) = rest
+        (zfull, b_full, a_full, a_turn, stage, w_t, x_buf, x_in, mask_l, in_sem, right_send, right_recv, left_send, left_recv, pair_send, pair_recv, x_send, x_recv) = rest
     chips = n_dev // 2
     rows = zfull.shape[2]
     half_c = b_full.shape[0]
@@ -72,11 +79,12 @@
     for load in loads:
         load.start()
     barrier = pltpu.get_barrier_semaphore()
-    for peer in (left, right, partner):
+    greeted = [lax.rem(me + p, n_dev) for p in range(1, n_dev)] if first else [left, right, partner]
+    for peer in greeted:
         pl.semaphore_signal(barrier, inc=1, device_id={'dap': peer}, device_id_type=MESH)
     for load in loads:
         load.wait()
-    pl.semaphore_wait(barrier, 3)
+    pl.semaphore_wait(barrier, len(greeted))
 
     def send(block, half, send_sem, recv_sem, target):
         return pltpu.make_async_remote_copy(src_ref=zfull.at[block, half], dst_ref=zfull.at[block, half], send_sem=send_sem, recv_sem=recv_sem, device_id={'dap': target}, device_id_type=MESH)
@@ -88,6 +96,15 @@
     send(me, 0, pair_send.at[0], pair_recv.at[0], partner).start()
     send(me, 1, pair_send.at[1], pair_recv.at[1], partner).start()
 
+    def mask_copy(owner, p, target):
+        return pltpu.make_async_remote_copy(src_ref=mask_ref, dst_ref=mask_out.at[pl.ds(pl.multiple_of(owner * rows, rows), rows), :], send_sem=mask_send.at[p - 1], recv_sem=mask_recv.at[p - 1], device_id={'dap': target}, device_id_type=MESH)
+
+    if first:
+        for p in range(1, n_dev):
+            mask_copy(me, p, greeted[p - 1]).start()
+        mask_out[pl.ds(pl.multiple_of(me * rows, rows), rows), :] = mask_ref[...]
+    masks = mask_out if first else mask_ref
+
     x_buf[0, 0, :4 * channels, :] = w_proj[layer].astype(F32).T
     for spot, part in enumerate((2, 3, 0, 1)):
         w_t[spot * half_c:(spot + 1) * half_c, :] = x_buf[0, 0, pl.ds(pl.multiple_of(part * channels + core * half_c, half_c), half_c), :].astype(BF16)
@@ -96,7 +113,6 @@
     my_off = pl.multiple_of(lax.rem(chip, chips // 2) * 2 * rows, 2 * rows)
 
     def project(block, half, operands):
-        tok_mask = mask_v[half]
         weights = w_t[:operands * channels, :]
 
         @pl.loop(0, rows // 2)
@@ -107,7 +123,7 @@
                 gated = sigmoid(slab[o * channels + half_c:(o + 1) * channels]) * slab[o * channels:o * channels + half_c]
                 for t in range(2):
                     row = 2 * pair + t
-                    stage[o, pl.ds(pl.multiple_of(row * pad, 8), half_c), :] = gated[:, t * LANES:(t + 1) * LANES] * (tok_mask * mask_s[block * rows + row])
+                    stage[o, pl.ds(pl.multiple_of(row * pad, 8), half_c), :] = gated[:, t * LANES:(t + 1) * LANES]
 
         spot = pl.multiple_of(block * rows, rows)
 
@@ -184,49 +200,75 @@
 
             process(block, half, False)
 
+    if first:
+        for p in range(1, n_dev):
+            mask_copy(lax.rem(me + n_dev - p, n_dev), p, greeted[p - 1]).wait_recv()
+    for half in range(2):
+        mask_l[half] = masks[half * LANES:(half + 1) * LANES, :].T[:8, :]
+    key_mask = jnp.concatenate([mask_l[0, :1, :], mask_l[1, :1, :]], axis=1).astype(BF16)
     if kind != 'row':
         @pl.loop(0, half_c // 4)
         def _(group):
             for t in range(4):
                 a_turn[group * 4 + t] = a_full[group * 4 + t].T
 
-    @pl.loop(0, half_c // 4)
-    def _(group):
-        for t in range(4):
-            c = group * 4 + t
-            rhs = jnp.concatenate([b_full[c, 0], b_full[c, 1]], axis=1)
-            if kind == 'row':
-                product = dot_nt(jnp.concatenate([a_full[c, 0], a_full[c, 1]], axis=1), rhs)
-            else:
-                product = dot_nn(a_turn[c, pl.ds(my_off, 2 * rows), :], rhs)
-            for who in range(2):
-                for half in range(2):
-                    x_buf[who, half, pl.ds(c, rows, stride=pad), :] = product[who * rows:(who + 1) * rows, half * LANES:(half + 1) * LANES]
-
-    exchange = pltpu.make_async_remote_copy(src_ref=x_buf.at[1 - core], dst_ref=x_in, send_sem=x_send, recv_sem=x_recv, device_id={'dap': partner}, device_id_type=MESH)
+    def exchange(half):
+        return pltpu.make_async_remote_copy(src_ref=x_buf.at[1 - core, half], dst_ref=x_in.at[half], send_sem=x_send.at[half], recv_sem=x_recv.at[half], device_id={'dap': partner}, device_id_type=MESH)
+
+    for half in range(2):
+        @pl.loop(0, half_c // 4)
+        def _(group):
+            for t in range(4):
+                c = group * 4 + t
+                if kind == 'row':
+                    lanes = slice(half * LANES, (half + 1) * LANES)
+                    product = dot_nt(jnp.concatenate([a_full[c, 0], a_full[c, 1]], axis=1) * key_mask, jnp.concatenate([b_full[c, 0, lanes, :], b_full[c, 1, lanes, :]], axis=1))
+                else:
+                    product = dot_nn(a_turn[c, pl.ds(my_off, 2 * rows), :] * key_mask, b_full[c, half])
+                for who in range(2):
+                    x_buf[who, half, pl.ds(c, rows, stride=pad), :] = product[who * rows:(who + 1) * rows, :]
+
+        if half == 0:
+            w_own = w_out[layer, pl.ds(pl.multiple_of(core * half_c, half_c), half_c), :]
+            w_other = w_out[layer, pl.ds(pl.multiple_of((1 - core) * half_c, half_c), half_c), :]
+            w_t[:channels, :] = turned(jnp.concatenate([w_own, w_other], axis=0))
+            w_t[channels:2 * channels, :] = turned(w_gate[layer])
+        exchange(half).start()
+
+    for half in range(2):
+        exchange(half).wait_recv()
+
+        @pl.loop(0, rows)
+        def _(i):
+            lanes = slice(half * LANES, (half + 1) * LANES)
+            spot = pl.ds(pl.multiple_of(i * pad, 8), half_c)
+            x_mask = mask_l[half, :1, :] * masks[pl.ds(me * rows + i, 1), :]
+            x = jnp.concatenate([x_buf[core, half, spot, :], x_in[half, spot, :]], axis=0) * x_mask
+            update = dot_nn(w_t[:channels, :], layer_norm_t(x))
+            z_row = zfull[me, half, i]
+            gate = sigmoid(dot_nn(w_t[channels:2 * channels, :], layer_norm_t(z_row)))
+            z_new = (z_row.astype(F32) + gate * update).astype(BF16)
+            out_ref[i, :, lanes] = z_new
+            if heads:
+                stage[0, pl.ds(pl.multiple_of((half * rows + i) * 8, 8), 8), :] = dot_nn(bias_t[layer], layer_norm_t(z_new))
+
+    if heads:
+        for half in range(2):
+            for h in range(heads):
+                bias_out[h, :, half * LANES:(half + 1) * LANES] = stage[0, pl.ds(half * rows * 8 + h, rows, stride=8), :].astype(BF16)
     for e in range(events):
         send(me, 0, right_send.at[e], right_recv.at[e], right).wait_send()
         send(me, 0, left_send.at[e], left_recv.at[e], left).wait_send()
     for e in range(2 * events + 2):
         send(me, 0, pair_send.at[e], pair_recv.at[e], partner).wait_send()
-    exchange.start()
-    w_own = w_out[layer, pl.ds(pl.multiple_of(core * half_c, half_c), half_c), :]
-    w_other = w_out[layer, pl.ds(pl.multiple_of((1 - core) * half_c, half_c), half_c), :]
-    w_t[:channels, :] = turned(jnp.concatenate([w_own, w_other], axis=0))
-    w_t[channels:2 * channels, :] = turned(w_gate[layer])
-    exchange.wait()
-
-    @pl.loop(0, rows)
-    def _(i):
-        for half in range(2):
-            x = jnp.concatenate([x_buf[core, half, pl.ds(pl.multiple_of(i * pad, 8), half_c), :], x_in[half, pl.ds(pl.multiple_of(i * pad, 8), half_c), :]], axis=0)
-            update = dot_nn(w_t[:channels, :], layer_norm_t(x))
-            z_row = zfull[me, half, i]
-            gate = sigmoid(dot_nn(w_t[channels:2 * channels, :], layer_norm_t(z_row)))
-            out_ref[i, :, half * LANES:(half + 1) * LANES] = (z_row.astype(F32) + gate * update).astype(BF16)
-
-
-def tri_mult(kind, layer, n_dev, cid, z, mask_s, mask_v, w_proj, w_gate, w_out):
+    for half in range(2):
+        exchange(half).wait_send()
+    if first:
+        for p in range(1, n_dev):
+            mask_copy(me, p, greeted[p - 1]).wait_send()
+
+
+def tri_mult(kind, layer, n_dev, cid, first, z, mask, w_proj, w_gate, w_out, bias_t=None, heads=0):
     rows, channels, tokens = z.shape
     assert tokens == 2 * LANES and channels == LANES and rows * n_dev == tokens
     half_c = channels // 2
@@ -235,13 +277,18 @@
     vmem = pl.BlockSpec(memory_space=pltpu.VMEM)
     dma = pltpu.SemaphoreType.DMA
     left_operand = [pltpu.VMEM((half_c, 2, 2 * rows, LANES), BF16)]
+    shapes = [jax.ShapeDtypeStruct(z.shape, BF16)]
+    if first:
+        shapes.append(jax.ShapeDtypeStruct((tokens, LANES), F32))
+    if heads:
+        shapes.append(jax.ShapeDtypeStruct((heads, rows, tokens), BF16))
     if kind != 'row':
         left_operand = [pltpu.VMEM((half_c, tokens, LANES), BF16), pltpu.VMEM((half_c, LANES, tokens), BF16)]
     return pl.pallas_call(
-        functools.partial(tri_mult_kernel, kind, layer, n_dev),
-        out_shape=jax.ShapeDtypeStruct(z.shape, BF16),
-        in_specs=[pl.BlockSpec(memory_space=pl.ANY), pl.BlockSpec(memory_space=pltpu.SMEM), vmem, vmem, vmem, vmem],
-        out_specs=vmem,
+        functools.partial(tri_mult_kernel, kind, layer, n_dev, first, heads),
+        out_shape=shapes,
+        in_specs=[pl.BlockSpec(memory_space=pl.ANY)] + [vmem] * (4 + bool(heads)),
+        out_specs=[vmem] * len(shapes),
         scratch_shapes=[
             pltpu.VMEM((n_dev, 2, rows, channels, LANES), BF16),
             pltpu.VMEM((half_c, 2, tokens, LANES), BF16),
@@ -250,23 +297,24 @@
             pltpu.VMEM((2 * channels, channels), BF16),
             pltpu.VMEM((2, 2, rows * pad, LANES), F32),
             pltpu.VMEM((2, rows * pad, LANES), F32),
-            dma((2,)), dma((events,)), dma((events,)), dma((events,)), dma((events,)), dma((2 * events + 2,)), dma((2 * events + 2,)), dma, dma,
-        ],
+            pltpu.VMEM((2, 8, LANES), F32),
+            dma((2,)), dma((events,)), dma((events,)), dma((events,)), dma((events,)), dma((2 * events + 2,)), dma((2 * events + 2,)), dma((2,)), dma((2,)),
+        ] + [dma((n_dev - 1,)), dma((n_dev - 1,))] * first,
         compiler_params=pltpu.CompilerParams(collective_id=cid, has_side_effects=True, vmem_limit_bytes=VMEM_LIMIT),
         name=f'tri_mult_{kind}_{cid}',
-    )(z, mask_s, mask_v, w_proj, w_gate, w_out)
-
-
-def tri_att_kernel(layer, n_dev, heads, last, trans, share, z_ref, mask_c, w_qkvg, bias_t, w_out, *rest):
+    )(z, mask, w_proj, w_gate, w_out, *((bias_t,) if heads else ()))
+
+
+def tri_att_kernel(layer, n_dev, heads, last, trans, share, z_ref, mask_ref, w_qkvg, bias_own, w_out, *rest):
     rest = list(rest)
     pt_in, pt_out = (rest.pop(0), rest.pop(0)) if trans else (None, None)
-    kv_in = rest.pop(0) if share else None
+    kv_in, bias_t = (rest.pop(0), rest.pop(0)) if share else (None, None)
     out_ref = rest.pop(0)
-    kv_all = rest.pop(0) if share else None
-    (normed_s, bias_s, bias_all, logit_bias, w_t, w_o, k_s, q_s, v_s, g_s, z_nat, r_buf, stage, b_send, b_recv, t_send, t_recv, own_sem) = rest[:18]
-    rest = rest[18:]
+    kv_all, bias_next = (rest.pop(0), rest.pop(0)) if share else (None, None)
+    (bias_s, bias_all, logit_bias, w_t, w_o, k_s, q_s, v_s, g_s, z_nat, r_buf, stage, b_send, b_recv, d_send, d_recv, t_send, t_recv, own_sem) = rest[:19]
+    rest = rest[19:]
     pt_in_t, pt_out_t = (rest.pop(0), rest.pop(0)) if trans else (None, None)
-    kv_buf, kv_send, kv_recv = (rest.pop(0), rest.pop(0), rest.pop(0)) if share else (None, None, None)
+    kv_send, kv_recv = (rest.pop(0), rest.pop(0)) if share else (None, None)
     rows, channels, tokens = z_ref.shape
     width = channels // heads
     me = lax.axis_index('dap')
@@ -275,62 +323,72 @@
     for peer in peers:
         pl.semaphore_signal(barrier, inc=1, device_id={'dap': peer}, device_id_type=MESH)
 
-    @pl.loop(0, rows)
-    def _(i):
-        normed = layer_norm_t(z_ref[i])
-        normed_s[i] = normed
-        slab = dot_nn(bias_t[layer], normed)
-        for half in range(2):
-            bias_s[half, pl.ds(pl.multiple_of(i * 8, 8), 8), :] = slab[:, half * LANES:(half + 1) * LANES]
-
+    chips = n_dev // 2
+    chip, core = me // 2, lax.rem(me, 2)
+    partner = chip * 2 + 1 - core
     spot = pl.multiple_of(me * rows, rows)
-    for h in range(heads):
-        for half in range(2):
-            bias_all[h, pl.ds(spot, rows), half * LANES:(half + 1) * LANES] = bias_s[half, pl.ds(h, rows, stride=8), :].astype(BF16)
+
+    def rows_of(ref, owner, lead):
+        block = pl.ds(pl.multiple_of(owner * rows, rows), rows)
+        return ref.at[:, block, :] if lead else ref.at[block, :]
+
+    def bias_copy(owner, d, target):
+        return pltpu.make_async_remote_copy(src_ref=bias_own, dst_ref=rows_of(bias_all, owner, True), send_sem=b_send.at[d], recv_sem=b_recv.at[d], device_id={'dap': target}, device_id_type=MESH)
+
+    def relay_copy(owner, d):
+        ref = rows_of(bias_all, owner, True)
+        return pltpu.make_async_remote_copy(src_ref=ref, dst_ref=ref, send_sem=d_send.at[d], recv_sem=d_recv.at[d], device_id={'dap': partner}, device_id_type=MESH)
+
+    def kv_copy(owner, p, target):
+        return pltpu.make_async_remote_copy(src_ref=kv_in, dst_ref=rows_of(kv_all, owner, False), send_sem=kv_send.at[p - 1], recv_sem=kv_recv.at[p - 1], device_id={'dap': target}, device_id_type=MESH)
+
+    def chip_core(d):
+        return lax.rem(chip + d + chips, chips) * 2 + core
+
+    pl.semaphore_wait(barrier, n_dev - 1)
+    for d in range(chips):
+        bias_copy(me, d, partner if d == 0 else chip_core(d)).start()
     if share:
-        kv_buf[pl.ds(spot, rows), :] = kv_in[...]
+        for p in range(1, n_dev):
+            kv_copy(me, p, peers[p - 1]).start()
+        kv_all[pl.ds(spot, rows), :] = kv_in[...]
+    bias_all[:, pl.ds(spot, rows), :] = bias_own[...]
     w_t[...] = turned(w_qkvg[layer])
     w_o[...] = turned(w_out[layer])
     if trans:
         for part in range(0, pt_in_t.shape[0], channels):
             pt_in_t[part:part + channels, :] = turned(pt_in[layer, :, part:part + channels])
         pt_out_t[...] = turned(pt_out[layer])
-    pl.semaphore_wait(barrier, n_dev - 1)
-
-    def bias_copy(owner, p, target):
-        ref = bias_all.at[:, pl.ds(pl.multiple_of(owner * rows, rows), rows), :]
-        return pltpu.make_async_remote_copy(src_ref=ref, dst_ref=ref, send_sem=b_send.at[p - 1], recv_sem=b_recv.at[p - 1], device_id={'dap': target}, device_id_type=MESH)
-
-    def kv_copy(owner, p, target):
-        ref = kv_buf.at[pl.ds(pl.multiple_of(owner * rows, rows), rows), :]
-        return pltpu.make_async_remote_copy(src_ref=ref, dst_ref=ref, send_sem=kv_send.at[p - 1], recv_sem=kv_recv.at[p - 1], device_id={'dap': target}, device_id_type=MESH)
-
-    for p in range(1, n_dev):
-        bias_copy(me, p, peers[p - 1]).start()
-    if share:
-        for p in range(1, n_dev):
-            kv_copy(me, p, peers[p - 1]).start()
-
-    @pl.loop(0, rows)
-    def _(i):
-        slab = dot_nn(w_t[...], normed_s[i])
+
+    def projections(i):
+        slab = dot_nn(w_t[...], layer_norm_t(z_ref[i]))
         q_s[i] = slab[:channels].astype(BF16)
         k_s[i] = slab[channels:2 * channels].T.astype(BF16)
         v_s[i] = slab[2 * channels:3 * channels].astype(BF16)
         g_s[i] = sigmoid(slab[3 * channels:])
 
-    for p in range(1, n_dev):
-        bias_copy(lax.rem(me + n_dev - p, n_dev), p, peers[p - 1]).wait_recv()
+    @pl.loop(0, rows // 2)
+    def _(pair):
+        projections(2 * pair)
+        projections(2 * pair + 1)
+
+    for d in range(1, chips):
+        bias_copy(chip_core(-d), d, partner).wait_recv()
+        relay_copy(chip_core(-d), d).start()
+    bias_copy(partner, 0, partner).wait_recv()
+    for d in range(1, chips):
+        relay_copy(lax.rem(chip - d + chips, chips) * 2 + 1 - core, d).wait_recv()
     for h in range(heads):
         for qh in range(2):
             for kh in range(2):
-                tile = bias_all[h, qh * LANES:(qh + 1) * LANES, kh * LANES:(kh + 1) * LANES].astype(F32).T
-                logit_bias[h, kh * LANES:(kh + 1) * LANES, qh * LANES:(qh + 1) * LANES] = (tile + mask_c[kh * LANES:(kh + 1) * LANES, :]) * LOG2E
+                keys, queries = slice(kh * LANES, (kh + 1) * LANES), slice(qh * LANES, (qh + 1) * LANES)
+                tile = bias_all[h, queries, keys].astype(F32).T if share else bias_all[h, keys, queries].astype(F32)
+                logit_bias[h, keys, queries] = (tile + (mask_ref[keys, :] - 1.0) * NEG_BIG) * LOG2E
     scale = width ** -0.5 * LOG2E
 
     def turn_copy(source, t, p, target, to):
         return pltpu.make_async_remote_copy(
-            src_ref=z_nat.at[pl.ds(4 * t, 4), pl.ds(pl.multiple_of(to * rows, rows), rows), :], dst_ref=r_buf.at[source, pl.ds(4 * t, 4)],
+            src_ref=z_nat.at[pl.ds(TURN * t, TURN), pl.ds(pl.multiple_of(to * rows, rows), rows), :], dst_ref=r_buf.at[source, pl.ds(TURN * t, TURN)],
             send_sem=t_send.at[p - 1], recv_sem=t_recv.at[p - 1], device_id={'dap': target}, device_id_type=MESH)
 
     @pl.loop(0, rows)
@@ -365,15 +423,18 @@
             z_row = (z_row.astype(F32) + update).astype(BF16)
         z_nat[i] = turned(z_row)
 
-        @pl.when((lax.rem(i, 4) == 0) & (i > 0))
+        if share:
+            bias_s[0, pl.ds(pl.multiple_of(i * 8, 8), 8), :], bias_s[1, pl.ds(pl.multiple_of(i * 8, 8), 8), :] = jnp.split(dot_nn(bias_t[layer], layer_norm_t(z_row)), 2, axis=1)
+
+        @pl.when((lax.rem(i, TURN) == 0) & (i > 0))
         def _():
             for p in range(1, n_dev):
-                turn_copy(me, i // 4 - 1, p, peers[p - 1], peers[p - 1]).start()
+                turn_copy(me, i // TURN - 1, p, peers[p - 1], peers[p - 1]).start()
 
     own = pltpu.make_async_copy(z_nat.at[:, pl.ds(spot, rows), :], r_buf.at[me], own_sem)
     own.start()
     for p in range(1, n_dev):
-        turn_copy(me, rows // 4 - 1, p, peers[p - 1], peers[p - 1]).start()
+        turn_copy(me, rows // TURN - 1, p, peers[p - 1], peers[p - 1]).start()
     own.wait()
 
     def whole(source, p, target):
@@ -406,21 +467,26 @@
 
     for p in range(1, n_dev):
         whole(me, p, peers[p - 1]).wait_send()
-        bias_copy(me, p, peers[p - 1]).wait_send()
         if share:
             kv_copy(me, p, peers[p - 1]).wait_send()
             kv_copy(lax.rem(me + n_dev - p, n_dev), p, peers[p - 1]).wait_recv()
+    for d in range(chips):
+        bias_copy(me, d, partner).wait_send()
+        if d:
+            relay_copy(chip_core(-d), d).wait_send()
     if share:
-        kv_all[...] = kv_buf[...]
-
-
-def tri_att(layer, n_dev, cid, last, z, mask_c, w_qkvg, bias_t, heads, w_out, pt=(), kv=None):
+        for h in range(heads):
+            for half in range(2):
+                bias_next[h, :, half * LANES:(half + 1) * LANES] = bias_s[half, pl.ds(h, rows, stride=8), :].astype(BF16)
+
+
+def tri_att(layer, n_dev, cid, last, z, mask, w_qkvg, bias_own, w_out, pt=(), kv=None, bias_t=None):
     rows, channels, tokens = z.shape
     vmem = pl.BlockSpec(memory_space=pltpu.VMEM)
     dma = pltpu.SemaphoreType.DMA
     share = kv is not None
+    heads = bias_own.shape[0]
     scratch = [
-        pltpu.VMEM((rows, channels, tokens), BF16),
         pltpu.VMEM((2, rows * 8, LANES), F32),
         pltpu.VMEM((heads, tokens, tokens), BF16),
         pltpu.VMEM((heads, tokens, tokens), F32),
@@ -433,23 +499,24 @@
         pltpu.VMEM((rows, tokens, channels), BF16),
         pltpu.VMEM((n_dev, rows, rows, channels), BF16),
         pltpu.VMEM((rows * (rows + 8), LANES), F32),
-        dma((n_dev - 1,)), dma((n_dev - 1,)), dma((n_dev - 1,)), dma((n_dev - 1,)), dma,
+        dma((n_dev // 2,)), dma((n_dev // 2,)), dma((n_dev // 2,)), dma((n_dev // 2,)), dma((n_dev - 1,)), dma((n_dev - 1,)), dma,
     ]
     if pt:
         scratch += [pltpu.VMEM(pt[0].shape[:0:-1], BF16), pltpu.VMEM(pt[1].shape[:0:-1], BF16)]
     shape = jax.ShapeDtypeStruct((rows, tokens, channels) if last else z.shape, BF16)
     if share:
         kv_shape = jax.ShapeDtypeStruct((tokens, kv.shape[1]), BF16)
-        scratch += [pltpu.VMEM(kv_shape.shape, BF16), dma((n_dev - 1,)), dma((n_dev - 1,))]
+        scratch += [dma((n_dev - 1,)), dma((n_dev - 1,))]
+        bias_shape = jax.ShapeDtypeStruct(bias_own.shape, BF16)
     return pl.pallas_call(
         functools.partial(tri_att_kernel, layer, n_dev, heads, last, bool(pt), share),
-        out_shape=(shape, kv_shape) if share else shape,
-        in_specs=[vmem] * (5 + len(pt) + share),
-        out_specs=(vmem, vmem) if share else vmem,
+        out_shape=(shape, kv_shape, bias_shape) if share else shape,
+        in_specs=[vmem] * (5 + len(pt) + 2 * share),
+        out_specs=(vmem, vmem, vmem) if share else vmem,
         scratch_shapes=scratch,
         compiler_params=pltpu.CompilerParams(collective_id=cid, has_side_effects=True, vmem_limit_bytes=VMEM_LIMIT),
         name=f'tri_att_{cid}',
-    )(z, mask_c, w_qkvg, bias_t, w_out, *pt, *((kv,) if share else ()))
+    )(z, mask, w_qkvg, bias_own, w_out, *pt, *((kv, bias_t) if share else ()))
 
 
 def transition(act_in, w_in, w_out):
@@ -471,7 +538,7 @@
     head_dim = query.shape[1] // heads
     query, gate = query.reshape(rows, heads, head_dim), gate.reshape(rows, heads, head_dim)
     kv_all = kv_all.reshape(tokens, 2, heads, head_dim)
-    logits = jnp.einsum('ihd,jhd->ihj', query, kv_all[:, 0], preferred_element_type=F32) * head_dim ** -0.5 + pair_bias.astype(F32) + (mask_all.astype(F32) - 1.0) * NEG_BIG
+    logits = jnp.einsum('ihd,jhd->ihj', query, kv_all[:, 0], preferred_element_type=F32) * head_dim ** -0.5 + pair_bias.astype(F32) + (mask_all - 1.0) * NEG_BIG
     soft_scores = jax.nn.softmax(logits, axis=-1).astype(BF16)
     attended = jnp.einsum('ihj,jhd->ihd', soft_scores, kv_all[:, 1], preferred_element_type=F32)
     merged = (attended * gate).astype(BF16).reshape(rows, -1)
@@ -488,11 +555,7 @@
     def local_program(single, pair, token_mask, *weights):
         w = dict(zip(WEIGHT_NAMES, weights))
         blocks = weights[0].shape[0]
-        mask_all = lax.all_gather(token_mask, 'dap', tiled=True)
-        tokens = mask_all.shape[0]
-        mask_f = mask_all.astype(F32)
-        mask_v = mask_f.reshape(2, 1, tokens // 2)
-        mask_c = jnp.broadcast_to(((mask_f - 1.0) * NEG_BIG)[:, None], (tokens, LANES))
+        mask = jnp.broadcast_to(token_mask.astype(F32)[:, None], (token_mask.shape[0], LANES))
         heads = w['tas_bias'].shape[2]
 
         def bias_rows(name):
@@ -505,17 +568,21 @@
             cid = 4 * b
             last = b == blocks - 1
             query, kv, gate = single_inputs(single, w['ap_qkvg'][b])
-            pair = tri_mult('row', b, n_dev, cid, pair, mask_f, mask_v, w['tmo_proj'], w['tmo_gate'], w['tmo_out'])
-            pair = tri_mult('col', b, n_dev, cid + 1, pair, mask_f, mask_v, w['tmi_proj'], w['tmi_gate'], w['tmi_out'])
-            pair, kv_all = tri_att(b, n_dev, cid + 2, False, pair, mask_c, w['tas_qkvg'], tas_bias, heads, w['tas_out'], (), kv)
-            pair = tri_att(b, n_dev, cid + 3, last, pair, mask_c, w['tae_qkvg'], tae_bias, heads, w['tae_out'], (w['pt_in'], w['pt_out']))
+            out = ('row', b, n_dev, cid, b == 0, pair, mask, w['tmo_proj'], w['tmo_gate'], w['tmo_out'])
+            if b == 0:
+                pair, mask = tri_mult(*out)
+            else:
+                pair, = tri_mult(*out)
+            pair, bias = tri_mult('col', b, n_dev, cid + 1, False, pair, mask, w['tmi_proj'], w['tmi_gate'], w['tmi_out'], tas_bias, heads)
+            pair, kv_all, bias = tri_att(b, n_dev, cid + 2, False, pair, mask, w['tas_qkvg'], bias, w['tas_out'], (), kv, tae_bias)
+            pair = tri_att(b, n_dev, cid + 3, last, pair, mask, w['tae_qkvg'], bias, w['tae_out'], (w['pt_in'], w['pt_out']))
             if last:
                 pair_bias = jnp.einsum('ijc,ch->ihj', layer_norm(pair), w['ap_bias'][b], preferred_element_type=F32).astype(BF16)
             else:
                 centred = pair.astype(F32) - jnp.mean(pair.astype(F32), axis=1, keepdims=True)
                 normed = (centred * lax.rsqrt(jnp.mean(centred * centred, axis=1, keepdims=True) + EPS)).astype(BF16)
                 pair_bias = jnp.einsum('icj,ch->ihj', normed, w['ap_bias'][b], preferred_element_type=F32).astype(BF16)
-            single = single_step(single, query, gate, kv_all, pair_bias, mask_all, w['ap_out'][b], w['st_in'][b], w['st_out'][b])
+            single = single_step(single, query, gate, kv_all, pair_bias, mask[:, 0], w['ap_out'][b], w['st_in'][b], w['st_out'][b])
         return single, pair
 
     return jax.shard_map(local_program, mesh=mesh, in_specs=(single_spec, pair_spec, row_spec) + (P(),) * len(WEIGHT_NAMES), out_specs=(single_spec, pair_spec), check_vma=False)

time: 729 us -> 716 us (0.982)
  blocking collectives: 16.1 us -> 0 us
    pallas_call x4, Pallas kernels: 421 us -> 450 us  [tri_mult(): pl.pallas_call(functools.partial(tri_mult_kernel, kind, layer, n_dev, fir...]
    pallas_call x4, Pallas kernels: 259 us -> 236 us  [tri_att(): pl.pallas_call(functools.partial(tri_att_kernel, layer, n_dev, heads, las...]
    unnamed x1 -> x0, blocking collectives: 16.1 us -> none
where the time goes in v3:
time: 716 us
  Pallas kernels  686 us (96%)
  matrix products  12.8 us (2%)
  other arithmetic  8.5 us (1%)
  local copies, waits for them, and re-layouts  7.64 us (1%)
    pallas_call x4, Pallas kernels, tri_mult(): pl.pallas_call(functools.partial(tri_mult_kernel, kind, layer, n_dev, fir...  450 us
    pallas_call x4, Pallas kernels, tri_att(): pl.pallas_call(functools.partial(tri_att_kernel, layer, n_dev, heads, las...  236 us

profile of v3, /device:TPU:21, one launch (start us, length us, event | category | flops | bytes accessed | tf_op | source)
XLA Modules:
  0.0 715.7 jit_solution(12371883217387856619)
XLA Ops:
  0.7 2.4 copy.35
  3.1 0.7 broadcast_in_dim.2.mask_ref
  3.8 116.5 %tri_mult_row_0.1 = (bf16[16,128,256]{2,1,0:T(8,128)(2,1)}, f32[256,128]{1,0:T(8,128)}) custom-call(bf16[16,128,256]{2,1,0:T(8,128)(2,1)} %bitcast.103, f32[16,128]{1,0:T(8,128)} %broadcast_in_dim.2.mask_ref, bf16[2,128,512]{2,1,0:T(8,128)(2,1)} %w_proj.6, bf16[2,128,128]{2,1,0:T(8,128)(2,1)} %w_gate.6, bf16[2,128,128]{2,1,0:T(8,128)(2,1)} %w_out.12), custom_call_target="tpu_custom_call" | custom-call | tf_op jit(solution)/shard_map/tri_mult_row_0/pallas_call | solution.py:287
  120.3 0.6 pad.7.rest_0_
  120.9 113.3 %tri_mult_col_1.1 = (bf16[16,128,256]{2,1,0:T(8,128)(2,1)}, bf16[4,16,256]{2,1,0:T(8,128)(2,1)}) custom-call(bf16[16,128,256]{2,1,0:T(8,128)(2,1)} %get-tuple-element.14.z_hbm, f32[256,128]{1,0:T(8,128)} %get-tuple-element.15.mask_ref, bf16[2,128,512]{2,1,0:T(8,128)(2,1)} %w_proj.7, bf16[2,128,128]{2,1,0:T(8,128)(2,1)} %w_gate.7, ...), custom_call_target="tpu_custom_call" | custom-call | tf_op jit(solution)/shard_map/tri_mult_col_1/pallas_call | solution.py:287
  234.1 0.1 convert_reduce_fusion.2
  234.3 0.2 fusion.85
  234.5 0.3 fusion.110
  234.8 0.6 slice.105.rest_0_
  235.4 0.6 pad.8.rest_1_
  236.0 55.5 %tri_att_2.1 = (bf16[16,128,256]{2,1,0:T(8,128)(2,1)}, bf16[256,768]{1,0:T(8,128)(2,1)}, bf16[4,16,256]{2,1,0:T(8,128)(2,1)}) custom-call(bf16[16,128,256]{2,1,0:T(8,128)(2,1)} %get-tuple-element.16.z_ref, f32[256,128]{1,0:T(8,128)} %get-tuple-element.15.mask_ref, bf16[2,128,512]{2,1,0:T(8,128)(2,1)} %w_qkvg.6, ...), custom_call_target="tpu_custom_call" | custom-call | tf_op jit(solution)/shard_map/tri_att_2/pallas_call | solution.py:511
  291.6 63.5 %tri_att_3.1.z_hbm = bf16[16,128,256]{2,1,0:T(8,128)(2,1)} custom-call(bf16[16,128,256]{2,1,0:T(8,128)(2,1)} %get-tuple-element.19.z_ref, f32[256,128]{1,0:T(8,128)} %get-tuple-element.15.mask_ref, bf16[2,128,512]{2,1,0:T(8,128)(2,1)} %w_qkvg.7, bf16[4,16,256]{2,1,0:T(8,128)(2,1)} %get-tuple-element.20.bias_own, bf16[2,128,128]{2,1,0:T(8,128)(2,1)} %w_out.15, ...), custom_call_target="tpu_custom_call" | custom-call | tf_op jit(solution)/shard_map/tri_att_3/pallas_call | solution.py:511
  355.1 1.5 convert_reduce_fusion.1
  356.6 1.5 fusion.14
  358.2 1.0 fusion.61
  359.2 0.2 copy.36
  359.4 0.1 multiply_reduce_fusion
  359.5 0.1 reshape.116
  359.6 1.1 fusion.35
  360.7 0.2 fusion.111
  360.9 0.1 reshape.117
  361.0 0.5 fusion.41
  361.6 0.1 reshape.118
  361.7 1.4 fusion.112
  363.1 0.2 multiply_reduce_fusion.3
  363.3 2.1 fusion.8
  365.4 0.4 fusion.113
  365.9 0.2 multiply_reduce_fusion.2
  366.1 0.3 fusion.114
  366.4 0.6 slice.112.rest_0_
  367.0 106.8 %tri_mult_row_4.1.z_hbm = bf16[16,128,256]{2,1,0:T(8,128)(2,1)} custom-call(bf16[16,128,256]{2,1,0:T(8,128)(2,1)} %tri_att_3.1.z_hbm, f32[256,128]{1,0:T(8,128)} %get-tuple-element.15.mask_ref, bf16[2,128,512]{2,1,0:T(8,128)(2,1)} %w_proj.6, bf16[2,128,128]{2,1,0:T(8,128)(2,1)} %w_gate.6, bf16[2,128,128]{2,1,0:T(8,128)(2,1)} %w_out.12), custom_call_target="tpu_custom_call" | custom-call | tf_op jit(solution)/shard_map/tri_mult_row_4/pallas_call | solution.py:287
  473.8 113.2 %tri_mult_col_5.1 = (bf16[16,128,256]{2,1,0:T(8,128)(2,1)}, bf16[4,16,256]{2,1,0:T(8,128)(2,1)}) custom-call(bf16[16,128,256]{2,1,0:T(8,128)(2,1)} %tri_mult_row_4.1.z_hbm, f32[256,128]{1,0:T(8,128)} %get-tuple-element.15.mask_ref, bf16[2,128,512]{2,1,0:T(8,128)(2,1)} %w_proj.7, bf16[2,128,128]{2,1,0:T(8,128)(2,1)} %w_gate.7, bf16[2,128,128]{2,1,0:T(8,128)(2,1)} %w_out.13, ...), custom_call_target="tpu_custom_call" | custom-call | tf_op jit(solution)/shard_map/tri_mult_col_5/pallas_call | solution.py:287
  587.0 54.6 %tri_att_6.1 = (bf16[16,128,256]{2,1,0:T(8,128)(2,1)}, bf16[256,768]{1,0:T(8,128)(2,1)}, bf16[4,16,256]{2,1,0:T(8,128)(2,1)}) custom-call(bf16[16,128,256]{2,1,0:T(8,128)(2,1)} %get-tuple-element.21.z_ref, f32[256,128]{1,0:T(8,128)} %get-tuple-element.15.mask_ref, bf16[2,128,512]{2,1,0:T(8,128)(2,1)} %w_qkvg.6, ...), custom_call_target="tpu_custom_call" | custom-call | tf_op jit(solution)/shard_map/tri_att_6/pallas_call | solution.py:511
  641.6 62.4 %tri_att_7.1 = bf16[16,256,128]{2,1,0:T(8,128)(2,1)} custom-call(bf16[16,128,256]{2,1,0:T(8,128)(2,1)} %get-tuple-element.24.z_ref, f32[256,128]{1,0:T(8,128)} %get-tuple-element.15.mask_ref, bf16[2,128,512]{2,1,0:T(8,128)(2,1)} %w_qkvg.7, bf16[4,16,256]{2,1,0:T(8,128)(2,1)} %get-tuple-element.25.bias_own, bf16[2,128,128]{2,1,0:T(8,128)(2,1)} %w_out.15, ...), custom_call_target="tpu_custom_call" | custom-call | tf_op jit(solution)/shard_map/tri_att_7/pallas_call | solution.py:511
  704.0 1.7 convert_reduce_fusion
  705.7 2.3 fusion.12
  708.1 1.5 fusion.63
  709.5 0.2 copy.41
  709.7 0.1 reshape.120
  709.9 0.2 fusion.32
  710.0 0.2 fusion.115
  710.4 0.5 fusion.40
  710.9 0.1 reshape.122
  711.1 0.3 fusion.116
  711.3 0.2 multiply_reduce_fusion.1
  711.5 2.3 fusion.6
  713.9 0.9 fusion.52
  714.8 1.0 copy.59
  (48 shorter events, 0.3 us)
Async XLA Ops:
  0.6 2.5 copy-start.13
  0.6 119.6 %copy-start.8 = (bf16[2,128,4]{1,2,0:T(4,128)(2,1)S(1)}, bf16[2,128,4]{1,2,0:T(4,128)(2,1)}, u32[]{:S(2)}) copy-start(bf16[2,128,4]{1,2,0:T(4,128)(2,1)} %param.32) | copy-start | bytes 6148
  0.7 233.5 %copy-start.7 = (bf16[16,384]{1,0:T(8,128)(2,1)S(1)}, bf16[16,384]{1,0:T(8,128)(2,1)}, u32[]{:S(2)}) copy-start(bf16[16,384]{1,0:T(8,128)(2,1)} %param.22) | copy-start | bytes 36868
  0.7 233.8 %copy-start.3 = (bf16[2,384,1536]{2,1,0:T(8,128)(2,1)S(1)}, bf16[2,384,1536]{2,1,0:T(8,128)(2,1)}, u32[]{:S(2)}) copy-start(bf16[2,384,1536]{2,1,0:T(8,128)(2,1)} %param.39) | copy-start | bytes 7077892
  3.8 231.6 %copy-start.9 = (bf16[2,128,4]{1,2,0:T(4,128)(2,1)S(1)}, bf16[2,128,4]{1,2,0:T(4,128)(2,1)}, u32[]{:S(2)}) copy-start(bf16[2,128,4]{1,2,0:T(4,128)(2,1)} %param.35) | copy-start | bytes 6148
  291.5 66.6 %copy-start.12 = (bf16[2,128,16]{1,2,0:T(8,128)(2,1)S(1)}, bf16[2,128,16]{1,2,0:T(8,128)(2,1)}, u32[]{:S(2)}) copy-start(bf16[2,128,16]{1,2,0:T(8,128)(2,1)} %param.40) | copy-start | bytes 24580
  355.0 3.1 copy-start
  355.1 4.1 copy-start.6
  355.1 4.3 copy-start.2
  361.7 3.7 copy-start.10
  704.0 4.1 copy-start.1
  704.0 5.5 copy-start.5
  709.5 1.5 copy-start.4
  711.0 2.8 copy-start.11

commit v4 on v3

--- a/solution.py
+++ b/solution.py
@@ -60,10 +60,7 @@
     mask_out = rest.pop(0) if first else None
     bias_out = rest.pop(0) if heads else None
     mask_send, mask_recv = (rest.pop(), rest.pop()) if first else (None, None)
-    if kind == 'row':
-        (zfull, b_full, a_full, stage, w_t, x_buf, x_in, mask_l, in_sem, right_send, right_recv, left_send, left_recv, pair_send, pair_recv, x_send, x_recv) = rest
-    else:
-        (zfull, b_full, a_full, a_turn, stage, w_t, x_buf, x_in, mask_l, in_sem, right_send, right_recv, left_send, left_recv, pair_send, pair_recv, x_send, x_recv) = rest
+    (zfull, b_full, a_full, a_turn, stage, w_t, w_o, w_g, gate_s, x_buf, x_in, mask_l, in_sem, right_send, right_recv, left_send, left_recv, pair_send, pair_recv, x_send, x_recv) = rest
     chips = n_dev // 2
     rows = zfull.shape[2]
     half_c = b_full.shape[0]
@@ -108,6 +105,11 @@
     x_buf[0, 0, :4 * channels, :] = w_proj[layer].astype(F32).T
     for spot, part in enumerate((2, 3, 0, 1)):
         w_t[spot * half_c:(spot + 1) * half_c, :] = x_buf[0, 0, pl.ds(pl.multiple_of(part * channels + core * half_c, half_c), half_c), :].astype(BF16)
+
+    w_own = w_out[layer, pl.ds(pl.multiple_of(core * half_c, half_c), half_c), :]
+    w_other = w_out[layer, pl.ds(pl.multiple_of((1 - core) * half_c, half_c), half_c), :]
+    w_o[...] = turned(jnp.concatenate([w_own, w_other], axis=0))
+    w_g[...] = turned(w_gate[layer])
 
     my_half = chip // (chips // 2)
     my_off = pl.multiple_of(lax.rem(chip, chips // 2) * 2 * rows, 2 * rows)
@@ -164,6 +166,16 @@
 
     events = chips - 1
 
+    def turn_left():
+        key_mask = jnp.concatenate([mask_l[0, :1, :], mask_l[1, :1, :]], axis=1).astype(BF16)
+
+        @pl.loop(0, half_c // 4)
+        def _(group):
+            for t in range(4):
+                c = group * 4 + t
+                left_operand = jnp.concatenate([a_full[c, 0], a_full[c, 1]], axis=1) if kind == 'row' else a_full[c].T
+                a_turn[c] = left_operand * key_mask
+
     @pl.loop(0, events)
     def _(e):
         dist = e // 2 + 1
@@ -187,6 +199,23 @@
 
         send(block_l, half_l, pair_send.at[2 * e + 3], pair_recv.at[2 * e + 3], partner).start()
 
+        @pl.when(e == 0)
+        def _():
+            @pl.loop(0, rows)
+            def _(i):
+                for half in range(2):
+                    gate_s[half, i] = sigmoid(dot_nn(w_g[...], layer_norm_t(zfull[me, half, i])))
+
+        @pl.when(e == 1)
+        def _():
+            if first:
+                for p in range(1, n_dev):
+                    mask_copy(lax.rem(me + n_dev - p, n_dev), p, greeted[p - 1]).wait_recv()
+            for half in range(2):
+                mask_l[half] = masks[half * LANES:(half + 1) * LANES, :].T[:8, :]
+            if kind == 'row':
+                turn_left()
+
         @pl.loop(0, 4)
         def _(t):
             side, other = lax.rem(t, 2), t // 2
@@ -200,65 +229,48 @@
 
             process(block, half, False)
 
-    if first:
-        for p in range(1, n_dev):
-            mask_copy(lax.rem(me + n_dev - p, n_dev), p, greeted[p - 1]).wait_recv()
-    for half in range(2):
-        mask_l[half] = masks[half * LANES:(half + 1) * LANES, :].T[:8, :]
-    key_mask = jnp.concatenate([mask_l[0, :1, :], mask_l[1, :1, :]], axis=1).astype(BF16)
     if kind != 'row':
-        @pl.loop(0, half_c // 4)
-        def _(group):
-            for t in range(4):
-                a_turn[group * 4 + t] = a_full[group * 4 + t].T
+        turn_left()
 
     def exchange(half):
         return pltpu.make_async_remote_copy(src_ref=x_buf.at[1 - core, half], dst_ref=x_in.at[half], send_sem=x_send.at[half], recv_sem=x_recv.at[half], device_id={'dap': partner}, device_id_type=MESH)
 
+    @pl.loop(0, half_c // 4)
+    def _(group):
+        for t in range(4):
+            c = group * 4 + t
+            rhs = jnp.concatenate([b_full[c, 0], b_full[c, 1]], axis=1)
+            product = dot_nt(a_turn[c], rhs) if kind == 'row' else dot_nn(a_turn[c, pl.ds(my_off, 2 * rows), :], rhs)
+            for who in range(2):
+                for half in range(2):
+                    x_buf[who, half, pl.ds(c, rows, stride=pad), :] = product[who * rows:(who + 1) * rows, half * LANES:(half + 1) * LANES]
+
+    for e in range(events):
+        send(me, 0, right_send.at[e], right_recv.at[e], right).wait_send()
+        send(me, 0, left_send.at[e], left_recv.at[e], left).wait_send()
     for half in range(2):
-        @pl.loop(0, half_c // 4)
-        def _(group):
-            for t in range(4):
-                c = group * 4 + t
-                if kind == 'row':
-                    lanes = slice(half * LANES, (half + 1) * LANES)
-                    product = dot_nt(jnp.concatenate([a_full[c, 0], a_full[c, 1]], axis=1) * key_mask, jnp.concatenate([b_full[c, 0, lanes, :], b_full[c, 1, lanes, :]], axis=1))
-                else:
-                    product = dot_nn(a_turn[c, pl.ds(my_off, 2 * rows), :] * key_mask, b_full[c, half])
-                for who in range(2):
-                    x_buf[who, half, pl.ds(c, rows, stride=pad), :] = product[who * rows:(who + 1) * rows, :]
-
-        if half == 0:
-            w_own = w_out[layer, pl.ds(pl.multiple_of(core * half_c, half_c), half_c), :]
-            w_other = w_out[layer, pl.ds(pl.multiple_of((1 - core) * half_c, half_c), half_c), :]
-            w_t[:channels, :] = turned(jnp.concatenate([w_own, w_other], axis=0))
-            w_t[channels:2 * channels, :] = turned(w_gate[layer])
         exchange(half).start()
-
     for half in range(2):
         exchange(half).wait_recv()
 
-        @pl.loop(0, rows)
-        def _(i):
+        @pl.loop(0, rows // 2)
+        def _(pair):
             lanes = slice(half * LANES, (half + 1) * LANES)
-            spot = pl.ds(pl.multiple_of(i * pad, 8), half_c)
-            x_mask = mask_l[half, :1, :] * masks[pl.ds(me * rows + i, 1), :]
-            x = jnp.concatenate([x_buf[core, half, spot, :], x_in[half, spot, :]], axis=0) * x_mask
-            update = dot_nn(w_t[:channels, :], layer_norm_t(x))
-            z_row = zfull[me, half, i]
-            gate = sigmoid(dot_nn(w_t[channels:2 * channels, :], layer_norm_t(z_row)))
-            z_new = (z_row.astype(F32) + gate * update).astype(BF16)
-            out_ref[i, :, lanes] = z_new
-            if heads:
-                stage[0, pl.ds(pl.multiple_of((half * rows + i) * 8, 8), 8), :] = dot_nn(bias_t[layer], layer_norm_t(z_new))
+            for t in range(2):
+                i = 2 * pair + t
+                spot = pl.ds(pl.multiple_of(i * pad, 8), half_c)
+                x_mask = mask_l[half, :1, :] * masks[pl.ds(me * rows + i, 1), :]
+                x = jnp.concatenate([x_buf[core, half, spot, :], x_in[half, spot, :]], axis=0) * x_mask
+                update = dot_nn(w_o[...], layer_norm_t(x))
+                z_new = (zfull[me, half, i].astype(F32) + gate_s[half, i] * update).astype(BF16)
+                out_ref[i, :, lanes] = z_new
+                if heads:
+                    stage[0, pl.ds(pl.multiple_of((half * rows + i) * 8, 8), 8), :] = dot_nn(bias_t[layer], layer_norm_t(z_new))
 
     if heads:
         for half in range(2):
             for h in range(heads):
                 bias_out[h, :, half * LANES:(half + 1) * LANES] = stage[0, pl.ds(half * rows * 8 + h, rows, stride=8), :].astype(BF16)
-    for e in range(events):
-        send(me, 0, right_send.at[e], right_recv.at[e], right).wait_send()
-        send(me, 0, left_send.at[e], left_recv.at[e], left).wait_send()
     for e in range(2 * events + 2):
         send(me, 0, pair_send.at[e], pair_recv.at[e], partner).wait_send()
     for half in range(2):
@@ -276,7 +288,7 @@
     events = n_dev // 2 - 1
     vmem = pl.BlockSpec(memory_space=pltpu.VMEM)
     dma = pltpu.SemaphoreType.DMA
-    left_operand = [pltpu.VMEM((half_c, 2, 2 * rows, LANES), BF16)]
+    left_operand = [pltpu.VMEM((half_c, 2, 2 * rows, LANES), BF16), pltpu.VMEM((half_c, 2 * rows, tokens), BF16)]
     shapes = [jax.ShapeDtypeStruct(z.shape, BF16)]
     if first:
         shapes.append(jax.ShapeDtypeStruct((tokens, LANES), F32))
@@ -295,6 +307,9 @@
             *left_operand,
             pltpu.VMEM((2, rows * pad, LANES), F32),
             pltpu.VMEM((2 * channels, channels), BF16),
+            pltpu.VMEM((channels, channels), BF16),
+            pltpu.VMEM((channels, channels), BF16),
+            pltpu.VMEM((2, rows, channels, LANES), F32),
             pltpu.VMEM((2, 2, rows * pad, LANES), F32),
             pltpu.VMEM((2, rows * pad, LANES), F32),
             pltpu.VMEM((2, 8, LANES), F32),

time: 716 us -> 696 us (0.972)
  Pallas kernels: 686 us -> 664 us
    pallas_call x4, Pallas kernels: 450 us -> 429 us  [tri_mult(): pl.pallas_call(functools.partial(tri_mult_kernel, kind, layer, n_dev, fir...]
where the time goes in v4:
time: 696 us; the launch traced here: 694 us
  Pallas kernels  664 us (95%)
  matrix products  12.8 us (2%)
  other arithmetic  8.5 us (1%)
  local copies, waits for them, and re-layouts  7.64 us (1%)
    pallas_call x4, Pallas kernels, tri_mult(): pl.pallas_call(functools.partial(tri_mult_kernel, kind, layer, n_dev, fir...  429 us
    pallas_call x4, Pallas kernels, tri_att(): pl.pallas_call(functools.partial(tri_att_kernel, layer, n_dev, heads, las...  235 us

profile of v4, /device:TPU:21, one launch (start us, length us, event | category | flops | bytes accessed | tf_op | source)
XLA Modules:
  0.0 694.4 jit_solution(12409452204760458925)
XLA Ops:
  0.7 2.4 copy.35
  3.1 0.7 broadcast_in_dim.2.mask_ref
  3.8 113.0 %tri_mult_row_0.1 = (bf16[16,128,256]{2,1,0:T(8,128)(2,1)}, f32[256,128]{1,0:T(8,128)}) custom-call(bf16[16,128,256]{2,1,0:T(8,128)(2,1)} %bitcast.103, f32[16,128]{1,0:T(8,128)} %broadcast_in_dim.2.mask_ref, bf16[2,128,512]{2,1,0:T(8,128)(2,1)} %w_proj.6, bf16[2,128,128]{2,1,0:T(8,128)(2,1)} %w_gate.6, bf16[2,128,128]{2,1,0:T(8,128)(2,1)} %w_out.12), custom_call_target="tpu_custom_call" | custom-call | tf_op jit(solution)/shard_map/tri_mult_row_0/pallas_call | solution.py:299
  116.8 0.6 pad.7.rest_0_
  117.4 107.0 %tri_mult_col_1.1 = (bf16[16,128,256]{2,1,0:T(8,128)(2,1)}, bf16[4,16,256]{2,1,0:T(8,128)(2,1)}) custom-call(bf16[16,128,256]{2,1,0:T(8,128)(2,1)} %get-tuple-element.14.z_hbm, f32[256,128]{1,0:T(8,128)} %get-tuple-element.15.mask_ref, bf16[2,128,512]{2,1,0:T(8,128)(2,1)} %w_proj.7, bf16[2,128,128]{2,1,0:T(8,128)(2,1)} %w_gate.7, ...), custom_call_target="tpu_custom_call" | custom-call | tf_op jit(solution)/shard_map/tri_mult_col_1/pallas_call | solution.py:299
  224.4 0.1 convert_reduce_fusion.2
  224.6 0.2 fusion.85
  224.8 0.3 fusion.110
  225.1 0.6 slice.105.rest_0_
  225.7 0.6 pad.8.rest_1_
  226.3 55.4 %tri_att_2.1 = (bf16[16,128,256]{2,1,0:T(8,128)(2,1)}, bf16[256,768]{1,0:T(8,128)(2,1)}, bf16[4,16,256]{2,1,0:T(8,128)(2,1)}) custom-call(bf16[16,128,256]{2,1,0:T(8,128)(2,1)} %get-tuple-element.16.z_ref, f32[256,128]{1,0:T(8,128)} %get-tuple-element.15.mask_ref, bf16[2,128,512]{2,1,0:T(8,128)(2,1)} %w_qkvg.6, ...), custom_call_target="tpu_custom_call" | custom-call | tf_op jit(solution)/shard_map/tri_att_2/pallas_call | solution.py:526
  281.7 62.2 %tri_att_3.1.z_hbm = bf16[16,128,256]{2,1,0:T(8,128)(2,1)} custom-call(bf16[16,128,256]{2,1,0:T(8,128)(2,1)} %get-tuple-element.19.z_ref, f32[256,128]{1,0:T(8,128)} %get-tuple-element.15.mask_ref, bf16[2,128,512]{2,1,0:T(8,128)(2,1)} %w_qkvg.7, bf16[4,16,256]{2,1,0:T(8,128)(2,1)} %get-tuple-element.20.bias_own, bf16[2,128,128]{2,1,0:T(8,128)(2,1)} %w_out.15, ...), custom_call_target="tpu_custom_call" | custom-call | tf_op jit(solution)/shard_map/tri_att_3/pallas_call | solution.py:526
  343.9 1.5 convert_reduce_fusion.1
  345.4 1.5 fusion.14
  347.0 1.0 fusion.61
  348.0 0.2 copy.36
  348.2 0.1 multiply_reduce_fusion
  348.3 0.1 reshape.116
  348.5 1.1 fusion.35
  349.5 0.2 fusion.111
  349.8 0.1 reshape.117
  349.9 0.5 fusion.41
  350.4 0.1 reshape.118
  350.5 1.4 fusion.112
  351.9 0.2 multiply_reduce_fusion.3
  352.1 2.1 fusion.8
  354.3 0.4 fusion.113
  354.7 0.2 multiply_reduce_fusion.2
  354.9 0.3 fusion.114
  355.2 0.6 slice.112.rest_0_
  355.8 102.4 %tri_mult_row_4.1.z_hbm = bf16[16,128,256]{2,1,0:T(8,128)(2,1)} custom-call(bf16[16,128,256]{2,1,0:T(8,128)(2,1)} %tri_att_3.1.z_hbm, f32[256,128]{1,0:T(8,128)} %get-tuple-element.15.mask_ref, bf16[2,128,512]{2,1,0:T(8,128)(2,1)} %w_proj.6, bf16[2,128,128]{2,1,0:T(8,128)(2,1)} %w_gate.6, bf16[2,128,128]{2,1,0:T(8,128)(2,1)} %w_out.12), custom_call_target="tpu_custom_call" | custom-call | tf_op jit(solution)/shard_map/tri_mult_row_4/pallas_call | solution.py:299
  458.2 106.6 %tri_mult_col_5.1 = (bf16[16,128,256]{2,1,0:T(8,128)(2,1)}, bf16[4,16,256]{2,1,0:T(8,128)(2,1)}) custom-call(bf16[16,128,256]{2,1,0:T(8,128)(2,1)} %tri_mult_row_4.1.z_hbm, f32[256,128]{1,0:T(8,128)} %get-tuple-element.15.mask_ref, bf16[2,128,512]{2,1,0:T(8,128)(2,1)} %w_proj.7, bf16[2,128,128]{2,1,0:T(8,128)(2,1)} %w_gate.7, bf16[2,128,128]{2,1,0:T(8,128)(2,1)} %w_out.13, ...), custom_call_target="tpu_custom_call" | custom-call | tf_op jit(solution)/shard_map/tri_mult_col_5/pallas_call | solution.py:299
  564.9 55.5 %tri_att_6.1 = (bf16[16,128,256]{2,1,0:T(8,128)(2,1)}, bf16[256,768]{1,0:T(8,128)(2,1)}, bf16[4,16,256]{2,1,0:T(8,128)(2,1)}) custom-call(bf16[16,128,256]{2,1,0:T(8,128)(2,1)} %get-tuple-element.21.z_ref, f32[256,128]{1,0:T(8,128)} %get-tuple-element.15.mask_ref, bf16[2,128,512]{2,1,0:T(8,128)(2,1)} %w_qkvg.6, ...), custom_call_target="tpu_custom_call" | custom-call | tf_op jit(solution)/shard_map/tri_att_6/pallas_call | solution.py:526
  620.4 62.2 %tri_att_7.1 = bf16[16,256,128]{2,1,0:T(8,128)(2,1)} custom-call(bf16[16,128,256]{2,1,0:T(8,128)(2,1)} %get-tuple-element.24.z_ref, f32[256,128]{1,0:T(8,128)} %get-tuple-element.15.mask_ref, bf16[2,128,512]{2,1,0:T(8,128)(2,1)} %w_qkvg.7, bf16[4,16,256]{2,1,0:T(8,128)(2,1)} %get-tuple-element.25.bias_own, bf16[2,128,128]{2,1,0:T(8,128)(2,1)} %w_out.15, ...), custom_call_target="tpu_custom_call" | custom-call | tf_op jit(solution)/shard_map/tri_att_7/pallas_call | solution.py:526
  682.6 1.7 convert_reduce_fusion
  684.3 2.3 fusion.12
  686.7 1.5 fusion.63
  688.2 0.2 copy.41
  688.4 0.1 reshape.120
  688.5 0.2 fusion.32
  688.7 0.2 fusion.115
  689.0 0.5 fusion.40
  689.5 0.1 reshape.122
  689.7 0.3 fusion.116
  690.0 0.2 multiply_reduce_fusion.1
  690.2 2.3 fusion.6
  692.5 0.9 fusion.52
  693.4 1.0 copy.59
  (48 shorter events, 0.3 us)
Async XLA Ops:
  0.6 2.5 copy-start.13
  0.6 116.1 %copy-start.8 = (bf16[2,128,4]{1,2,0:T(4,128)(2,1)S(1)}, bf16[2,128,4]{1,2,0:T(4,128)(2,1)}, u32[]{:S(2)}) copy-start(bf16[2,128,4]{1,2,0:T(4,128)(2,1)} %param.32) | copy-start | bytes 6148
  0.7 223.8 %copy-start.7 = (bf16[16,384]{1,0:T(8,128)(2,1)S(1)}, bf16[16,384]{1,0:T(8,128)(2,1)}, u32[]{:S(2)}) copy-start(bf16[16,384]{1,0:T(8,128)(2,1)} %param.22) | copy-start | bytes 36868
  0.7 224.1 %copy-start.3 = (bf16[2,384,1536]{2,1,0:T(8,128)(2,1)S(1)}, bf16[2,384,1536]{2,1,0:T(8,128)(2,1)}, u32[]{:S(2)}) copy-start(bf16[2,384,1536]{2,1,0:T(8,128)(2,1)} %param.39) | copy-start | bytes 7077892
  3.8 221.9 %copy-start.9 = (bf16[2,128,4]{1,2,0:T(4,128)(2,1)S(1)}, bf16[2,128,4]{1,2,0:T(4,128)(2,1)}, u32[]{:S(2)}) copy-start(bf16[2,128,4]{1,2,0:T(4,128)(2,1)} %param.35) | copy-start | bytes 6148
  281.7 65.3 %copy-start.12 = (bf16[2,128,16]{1,2,0:T(8,128)(2,1)S(1)}, bf16[2,128,16]{1,2,0:T(8,128)(2,1)}, u32[]{:S(2)}) copy-start(bf16[2,128,16]{1,2,0:T(8,128)(2,1)} %param.40) | copy-start | bytes 24580
  343.9 3.1 copy-start
  343.9 4.1 copy-start.6
  343.9 4.3 copy-start.2
  350.5 3.7 copy-start.10
  682.6 4.1 copy-start.1
  682.6 5.5 copy-start.5
  688.2 1.5 copy-start.4
  689.7 2.8 copy-start.11

commit v5 on v4

--- a/solution.py
+++ b/solution.py
@@ -378,7 +378,7 @@
     def projections(i):
         slab = dot_nn(w_t[...], layer_norm_t(z_ref[i]))
         q_s[i] = slab[:channels].astype(BF16)
-        k_s[i] = slab[channels:2 * channels].T.astype(BF16)
+        k_s[i] = slab[channels:2 * channels].astype(BF16).T
         v_s[i] = slab[2 * channels:3 * channels].astype(BF16)
         g_s[i] = sigmoid(slab[3 * channels:])
 
@@ -406,8 +406,7 @@
             src_ref=z_nat.at[pl.ds(TURN * t, TURN), pl.ds(pl.multiple_of(to * rows, rows), rows), :], dst_ref=r_buf.at[source, pl.ds(TURN * t, TURN)],
             send_sem=t_send.at[p - 1], recv_sem=t_recv.at[p - 1], device_id={'dap': target}, device_id_type=MESH)
 
-    @pl.loop(0, rows)
-    def _(i):
+    def one_row(i):
         keys = k_s[i]
         parts = []
         for h in range(heads):
@@ -436,12 +435,19 @@
                 second = dot_nn(pt_in_t[hidden + part:hidden + part + channels, :], normed)
                 update = update + dot_nn(pt_out_t[:, part:part + channels], (first * sigmoid(first) * second).astype(BF16))
             z_row = (z_row.astype(F32) + update).astype(BF16)
-        z_nat[i] = turned(z_row)
+        z_nat[i] = z_row.T
 
         if share:
             bias_s[0, pl.ds(pl.multiple_of(i * 8, 8), 8), :], bias_s[1, pl.ds(pl.multiple_of(i * 8, 8), 8), :] = jnp.split(dot_nn(bias_t[layer], layer_norm_t(z_row)), 2, axis=1)
 
-        @pl.when((lax.rem(i, TURN) == 0) & (i > 0))
+
+    @pl.loop(0, rows // 2)
+    def _(step):
+        for t in range(2):
+            one_row(2 * step + t)
+        i = 2 * step + 2 - 1
+
+        @pl.when((lax.rem(i, TURN) == TURN - 1) & (i > TURN))
         def _():
             for p in range(1, n_dev):
                 turn_copy(me, i // TURN - 1, p, peers[p - 1], peers[p - 1]).start()
@@ -478,7 +484,7 @@
     if not last:
         @pl.loop(0, rows)
         def _(j):
-            out_ref[j] = turned(q_all[j])
+            out_ref[j] = q_all[j].T
 
     for p in range(1, n_dev):
         whole(me, p, peers[p - 1]).wait_send()
@@ -534,31 +540,70 @@
     )(z, mask, w_qkvg, bias_own, w_out, *pt, *((kv, bias_t) if share else ()))
 
 
-def transition(act_in, w_in, w_out):
-    hidden = w_out.shape[0]
-    projected = jnp.dot(layer_norm(act_in), w_in, preferred_element_type=F32)
-    inner = (jax.nn.silu(projected[..., :hidden]) * projected[..., hidden:]).astype(BF16)
-    return (act_in.astype(F32) + jnp.dot(inner, w_out, preferred_element_type=F32)).astype(BF16)
-
-
 def single_inputs(single, w_qkvg):
     width = w_qkvg.shape[1] // 4
     projected = jnp.dot(layer_norm(single), w_qkvg, preferred_element_type=F32)
     return projected[:, :width].astype(BF16), projected[:, width:3 * width].astype(BF16), jax.nn.sigmoid(projected[:, 3 * width:])
 
 
-def single_step(single, query, gate, kv_all, pair_bias, mask_all, w_out, st_in, st_out):
-    rows, tokens = single.shape[0], kv_all.shape[0]
-    heads = pair_bias.shape[1]
-    head_dim = query.shape[1] // heads
-    query, gate = query.reshape(rows, heads, head_dim), gate.reshape(rows, heads, head_dim)
-    kv_all = kv_all.reshape(tokens, 2, heads, head_dim)
-    logits = jnp.einsum('ihd,jhd->ihj', query, kv_all[:, 0], preferred_element_type=F32) * head_dim ** -0.5 + pair_bias.astype(F32) + (mask_all - 1.0) * NEG_BIG
-    soft_scores = jax.nn.softmax(logits, axis=-1).astype(BF16)
-    attended = jnp.einsum('ihj,jhd->ihd', soft_scores, kv_all[:, 1], preferred_element_type=F32)
-    merged = (attended * gate).astype(BF16).reshape(rows, -1)
-    single = (single.astype(F32) + jnp.dot(merged, w_out, preferred_element_type=F32)).astype(BF16)
-    return transition(single, st_in, st_out)
+def single_kernel(layer, natural, z_ref, s_ref, q_ref, gate_ref, kv_ref, mask_ref, bias_t, w_out, w_in, w_back, out_ref, bias_s, q_s, o_s, merged_s):
+    heads = bias_t.shape[1]
+    rows, width = q_ref.shape
+    head_dim = width // heads
+    lane = lax.broadcasted_iota(jnp.int32, (heads, width), 1)
+    head = lax.broadcasted_iota(jnp.int32, (heads, width), 0)
+    own_head = ((lane >= head * head_dim) & (lane < (head + 1) * head_dim)).astype(F32)
+
+    @pl.loop(0, rows // 2)
+    def _(pair):
+        for t in range(2):
+            i = 2 * pair + t
+            spot = pl.ds(pl.multiple_of(i * heads, heads), heads)
+            slab = dot_nt(bias_t[layer], layer_norm(z_ref[i])) if natural else dot_nn(bias_t[layer], layer_norm_t(z_ref[i]))
+            bias_s[spot, :] = slab.astype(BF16)
+            q_s[spot, :] = (q_ref[pl.ds(i, 1), :] * own_head).astype(BF16)
+
+    key_bias = (jnp.concatenate([mask_ref[half * LANES:(half + 1) * LANES, :].T[:1, :] for half in range(2)], axis=1) - 1.0) * NEG_BIG
+    logits = dot_nt(q_s[...], kv_ref[:, :width]) * head_dim ** -0.5 + bias_s[...].astype(F32) + key_bias
+    weights = jnp.exp(logits - jnp.max(logits, axis=1, keepdims=True))
+    soft = (weights * (1.0 / jnp.sum(weights, axis=1, keepdims=True))).astype(BF16)
+    o_s[...] = dot_nn(soft, kv_ref[:, width:])
+
+    @pl.loop(0, rows)
+    def _(i):
+        merged_s[pl.ds(i, 1), :] = jnp.sum(o_s[pl.ds(pl.multiple_of(i * heads, heads), heads), :] * own_head, axis=0, keepdims=True)
+
+    merged = (merged_s[...] * gate_ref[...]).astype(BF16)
+    single = (s_ref[...].astype(F32) + dot_nn(merged, w_out[layer])).astype(BF16)
+    normed = layer_norm(single)
+    hidden = w_back.shape[1]
+    update = jnp.zeros(single.shape, F32)
+    part = hidden // 3
+    for lo in range(0, hidden, part):
+        first = dot_nn(normed, w_in[layer, :, lo:lo + part])
+        second = dot_nn(normed, w_in[layer, :, hidden + lo:hidden + lo + part])
+        update = update + dot_nn((first * sigmoid(first) * second).astype(BF16), w_back[layer, lo:lo + part, :])
+    out_ref[...] = (single.astype(F32) + update).astype(BF16)
+
+
+def single_step(layer, natural, single, query, gate, kv_all, pair, mask, bias_t, w_out, st_in, st_out):
+    rows, width = query.shape
+    heads = bias_t.shape[1]
+    vmem = pl.BlockSpec(memory_space=pltpu.VMEM)
+    return pl.pallas_call(
+        functools.partial(single_kernel, layer, natural),
+        out_shape=jax.ShapeDtypeStruct(single.shape, BF16),
+        in_specs=[vmem] * 10,
+        out_specs=vmem,
+        scratch_shapes=[
+            pltpu.VMEM((rows * heads, kv_all.shape[0]), BF16),
+            pltpu.VMEM((rows * heads, width), BF16),
+            pltpu.VMEM((rows * heads, width), F32),
+            pltpu.VMEM((rows, width), F32),
+        ],
+        compiler_params=pltpu.CompilerParams(vmem_limit_bytes=VMEM_LIMIT),
+        name=f'single_step_{layer}',
+    )(pair, single, query.astype(F32), gate, kv_all, mask, bias_t, w_out, st_in, st_out)
 
 
 def solution(mesh):
@@ -578,6 +623,7 @@
             return jnp.pad(swapped, ((0, 0), (0, 8 - heads), (0, 0)))
 
         tas_bias, tae_bias = bias_rows('tas_bias'), bias_rows('tae_bias')
+        ap_bias = jnp.swapaxes(w['ap_bias'], 1, 2)
         pair = jnp.swapaxes(pair, 1, 2)
         for b in range(blocks):
             cid = 4 * b
@@ -591,13 +637,7 @@
             pair, bias = tri_mult('col', b, n_dev, cid + 1, False, pair, mask, w['tmi_proj'], w['tmi_gate'], w['tmi_out'], tas_bias, heads)
             pair, kv_all, bias = tri_att(b, n_dev, cid + 2, False, pair, mask, w['tas_qkvg'], bias, w['tas_out'], (), kv, tae_bias)
             pair = tri_att(b, n_dev, cid + 3, last, pair, mask, w['tae_qkvg'], bias, w['tae_out'], (w['pt_in'], w['pt_out']))
-            if last:
-                pair_bias = jnp.einsum('ijc,ch->ihj', layer_norm(pair), w['ap_bias'][b], preferred_element_type=F32).astype(BF16)
-            else:
-                centred = pair.astype(F32) - jnp.mean(pair.astype(F32), axis=1, keepdims=True)
-                normed = (centred * lax.rsqrt(jnp.mean(centred * centred, axis=1, keepdims=True) + EPS)).astype(BF16)
-                pair_bias = jnp.einsum('icj,ch->ihj', normed, w['ap_bias'][b], preferred_element_type=F32).astype(BF16)
-            single = single_step(single, query, gate, kv_all, pair_bias, mask[:, 0], w['ap_out'][b], w['st_in'][b], w['st_out'][b])
+            single = single_step(b, last, single, query, gate, kv_all, pair, mask, ap_bias, w['ap_out'], w['st_in'], w['st_out'])
         return single, pair
 
     return jax.shard_map(local_program, mesh=mesh, in_specs=(single_spec, pair_spec, row_spec) + (P(),) * len(WEIGHT_NAMES), out_specs=(single_spec, pair_spec), check_vma=False)

time: 696 us -> 693 us (level)
  Pallas kernels: 664 us -> 677 us
  matrix products: 12.8 us -> 1.89 us
    pallas_call x0 -> x2, Pallas kernels: none -> 17.4 us  [single_step(): pl.pallas_call(functools.partial(single_kernel, layer, natural), out_shap...]
    dot_general x12 -> x0, matrix products: 12.2 us -> none  [the longest x2 4.46 us: transition(): projected = jnp.dot(layer_norm(act_in), w_in, preferred_element_type=F32)]
where the time goes in v5:
time: 693 us
  Pallas kernels  677 us (98%)
  local copies, waits for them, and re-layouts  7.68 us (1%)
    pallas_call x4, Pallas kernels, tri_mult(): pl.pallas_call(functools.partial(tri_mult_kernel, kind, layer, n_dev, fir...  429 us
    pallas_call x4, Pallas kernels, tri_att(): pl.pallas_call(functools.partial(tri_att_kernel, layer, n_dev, heads, las...  231 us
    pallas_call x2, Pallas kernels, single_step(): pl.pallas_call(functools.partial(single_kernel, layer, natural), out_shap...  17.4 us

profile of v5, /device:TPU:21, one launch (start us, length us, event | category | flops | bytes accessed | tf_op | source)
XLA Modules:
  0.0 692.8 jit_solution(12628721177611005218)
XLA Ops:
  0.6 0.7 convert_element_type.28
  1.3 0.8 convert_reduce_fusion.1
  2.1 0.9 fusion.12
  3.0 1.3 pad.7.rest_0_
  4.3 1.3 pad.8.rest_1_
  5.6 0.7 broadcast_in_dim.2.mask_ref
  6.2 1.6 fusion.26
  7.8 0.6 fusion.19.gate_ref
  8.5 0.6 slice_convert_fusion.1.q_ref
  9.1 0.6 slice.36.rest_0_
  9.7 2.3 copy.24
  11.9 113.0 %tri_mult_row_0.1 = (bf16[16,128,256]{2,1,0:T(8,128)(2,1)}, f32[256,128]{1,0:T(8,128)}) custom-call(bf16[16,128,256]{2,1,0:T(8,128)(2,1)} %bitcast.14, f32[16,128]{1,0:T(8,128)} %broadcast_in_dim.2.mask_ref, bf16[2,128,512]{2,1,0:T(8,128)(2,1)} %w_proj.6, bf16[2,128,128]{2,1,0:T(8,128)(2,1)} %w_gate.6, bf16[2,128,128]{2,1,0:T(8,128)(2,1)} %w_out.14), custom_call_target="tpu_custom_call" | custom-call | tf_op jit(solution)/shard_map/tri_mult_row_0/pallas_call | solution.py:299
  125.0 107.1 %tri_mult_col_1.1 = (bf16[16,128,256]{2,1,0:T(8,128)(2,1)}, bf16[4,16,256]{2,1,0:T(8,128)(2,1)}) custom-call(bf16[16,128,256]{2,1,0:T(8,128)(2,1)} %get-tuple-element.14.z_hbm, f32[256,128]{1,0:T(8,128)} %get-tuple-element.15.mask_ref, bf16[2,128,512]{2,1,0:T(8,128)(2,1)} %w_proj.7, bf16[2,128,128]{2,1,0:T(8,128)(2,1)} %w_gate.7, ...), custom_call_target="tpu_custom_call" | custom-call | tf_op jit(solution)/shard_map/tri_mult_col_1/pallas_call | solution.py:299
  232.0 55.6 %tri_att_2.1 = (bf16[16,128,256]{2,1,0:T(8,128)(2,1)}, bf16[256,768]{1,0:T(8,128)(2,1)}, bf16[4,16,256]{2,1,0:T(8,128)(2,1)}) custom-call(bf16[16,128,256]{2,1,0:T(8,128)(2,1)} %get-tuple-element.16.z_ref, f32[256,128]{1,0:T(8,128)} %get-tuple-element.15.mask_ref, bf16[2,128,512]{2,1,0:T(8,128)(2,1)} %w_qkvg.6, ...), custom_call_target="tpu_custom_call" | custom-call | tf_op jit(solution)/shard_map/tri_att_2/pallas_call | solution.py:532
  287.6 61.3 %tri_att_3.1.z_hbm.z_ref = bf16[16,128,256]{2,1,0:T(8,128)(2,1)} custom-call(bf16[16,128,256]{2,1,0:T(8,128)(2,1)} %get-tuple-element.18.z_ref, f32[256,128]{1,0:T(8,128)} %get-tuple-element.15.mask_ref, bf16[2,128,512]{2,1,0:T(8,128)(2,1)} %w_qkvg.7, bf16[4,16,256]{2,1,0:T(8,128)(2,1)} %get-tuple-element.19.bias_own, bf16[2,128,128]{2,1,0:T(8,128)(2,1)} %w_out.18, ...), custom_call_target="tpu_custom_call" | custom-call | tf_op jit(solution)/shard_map/tri_att_3/pallas_call | solution.py:532
  349.0 8.1 %single_step_0.1.s_ref = bf16[16,384]{1,0:T(8,128)(2,1)} custom-call(bf16[16,128,256]{2,1,0:T(8,128)(2,1)} %tri_att_3.1.z_hbm.z_ref, bf16[16,384]{1,0:T(8,128)(2,1)} %s_ref.1, f32[16,384]{1,0:T(8,128)} %slice_convert_fusion.1.q_ref, f32[16,384]{1,0:T(8,128)} %fusion.19.gate_ref, bf16[256,768]{1,0:T(8,128)(2,1)} %get-tuple-element.22.kv_ref, ...), custom_call_target="tpu_custom_call" | custom-call | tf_op jit(solution)/shard_map/single_step_0/pallas_call | solution.py:593
  357.1 0.0 copy-start.2
  357.1 0.0 copy-start.1
  357.1 102.6 %tri_mult_row_4.1.z_hbm = bf16[16,128,256]{2,1,0:T(8,128)(2,1)} custom-call(bf16[16,128,256]{2,1,0:T(8,128)(2,1)} %tri_att_3.1.z_hbm.z_ref, f32[256,128]{1,0:T(8,128)} %get-tuple-element.15.mask_ref, bf16[2,128,512]{2,1,0:T(8,128)(2,1)} %w_proj.6, bf16[2,128,128]{2,1,0:T(8,128)(2,1)} %w_gate.6, bf16[2,128,128]{2,1,0:T(8,128)(2,1)} %w_out.14), custom_call_target="tpu_custom_call" | custom-call | tf_op jit(solution)/shard_map/tri_mult_row_4/pallas_call | solution.py:299
  459.7 0.0 copy-done.2
  459.7 0.1 convert_reduce_fusion
  459.8 0.2 fusion.10
  460.0 106.7 %tri_mult_col_5.1 = (bf16[16,128,256]{2,1,0:T(8,128)(2,1)}, bf16[4,16,256]{2,1,0:T(8,128)(2,1)}) custom-call(bf16[16,128,256]{2,1,0:T(8,128)(2,1)} %tri_mult_row_4.1.z_hbm, f32[256,128]{1,0:T(8,128)} %get-tuple-element.15.mask_ref, bf16[2,128,512]{2,1,0:T(8,128)(2,1)} %w_proj.7, bf16[2,128,128]{2,1,0:T(8,128)(2,1)} %w_gate.7, bf16[2,128,128]{2,1,0:T(8,128)(2,1)} %w_out.15, ...), custom_call_target="tpu_custom_call" | custom-call | tf_op jit(solution)/shard_map/tri_mult_col_5/pallas_call | solution.py:299
  566.7 0.0 copy-done.1
  566.8 0.3 fusion.27
  567.1 0.6 fusion.16.gate_ref
  567.7 0.6 slice_convert_fusion.q_ref
  568.3 0.6 slice.39.rest_0_
  568.9 53.7 %tri_att_6.1 = (bf16[16,128,256]{2,1,0:T(8,128)(2,1)}, bf16[256,768]{1,0:T(8,128)(2,1)}, bf16[4,16,256]{2,1,0:T(8,128)(2,1)}) custom-call(bf16[16,128,256]{2,1,0:T(8,128)(2,1)} %get-tuple-element.20.z_ref, f32[256,128]{1,0:T(8,128)} %get-tuple-element.15.mask_ref, bf16[2,128,512]{2,1,0:T(8,128)(2,1)} %w_qkvg.6, ...), custom_call_target="tpu_custom_call" | custom-call | tf_op jit(solution)/shard_map/tri_att_6/pallas_call | solution.py:532
  622.6 60.0 %tri_att_7.1.z_ref = bf16[16,256,128]{2,1,0:T(8,128)(2,1)} custom-call(bf16[16,128,256]{2,1,0:T(8,128)(2,1)} %get-tuple-element.23.z_ref, f32[256,128]{1,0:T(8,128)} %get-tuple-element.15.mask_ref, bf16[2,128,512]{2,1,0:T(8,128)(2,1)} %w_qkvg.7, bf16[4,16,256]{2,1,0:T(8,128)(2,1)} %get-tuple-element.24.bias_own, bf16[2,128,128]{2,1,0:T(8,128)(2,1)} %w_out.18, ...), custom_call_target="tpu_custom_call" | custom-call | tf_op jit(solution)/shard_map/tri_att_7/pallas_call | solution.py:532
  682.6 0.0 copy-start
  682.6 9.2 %single_step_1.1 = bf16[16,384]{1,0:T(8,128)(2,1)} custom-call(bf16[16,256,128]{2,1,0:T(8,128)(2,1)} %tri_att_7.1.z_ref, bf16[16,384]{1,0:T(8,128)(2,1)} %single_step_0.1.s_ref, f32[16,384]{1,0:T(8,128)} %slice_convert_fusion.q_ref, f32[16,384]{1,0:T(8,128)} %fusion.16.gate_ref, bf16[256,768]{1,0:T(8,128)(2,1)} %get-tuple-element.25.kv_ref, ...), custom_call_target="tpu_custom_call" | custom-call | tf_op jit(solution)/shard_map/single_step_1/pallas_call | solution.py:593
  691.8 0.0 copy-done
  691.8 1.0 copy.26
  (4 shorter events, 0.0 us)
Async XLA Ops:
  357.1 102.6 %copy-start.2 = (bf16[16,384]{1,0:T(8,128)(2,1)S(1)}, bf16[16,384]{1,0:T(8,128)(2,1)}, u32[]{:S(2)}) copy-start(bf16[16,384]{1,0:T(8,128)(2,1)} %single_step_0.1.s_ref) | copy-start | bytes 36868
  357.1 209.7 %copy-start.1 = (bf16[2,384,1536]{2,1,0:T(8,128)(2,1)S(1)}, bf16[2,384,1536]{2,1,0:T(8,128)(2,1)}, u32[]{:S(2)}) copy-start(bf16[2,384,1536]{2,1,0:T(8,128)(2,1)} %param.39) | copy-start | bytes 7077892
  682.6 9.3 %copy-start = (bf16[16,256,128]{2,1,0:T(8,128)(2,1)S(1)}, bf16[16,256,128]{2,1,0:T(8,128)(2,1)}, u32[]{:S(2)}) copy-start(bf16[16,256,128]{2,1,0:T(8,128)(2,1)} %tri_att_7.1.z_ref) | copy-start | bytes 3145732

commit v6 on v5

--- a/solution.py
+++ b/solution.py
@@ -33,6 +33,12 @@
 
 def dot_tn(lhs, rhs):
     return lax.dot_general(lhs, rhs, (((0,), (0,)), ((), ())), preferred_element_type=F32)
+
+
+def bias_rows(w_bias):
+    size = w_bias.shape[0]
+    eye = lax.broadcasted_iota(jnp.int32, (size, size), 0) == lax.broadcasted_iota(jnp.int32, (size, size), 1)
+    return dot_tn(w_bias, eye.astype(F32).astype(BF16)).astype(BF16)
 
 
 def sigmoid(values):
@@ -250,6 +256,7 @@
         send(me, 0, left_send.at[e], left_recv.at[e], left).wait_send()
     for half in range(2):
         exchange(half).start()
+    bias_w = bias_rows(bias_t[layer]) if heads else None
     for half in range(2):
         exchange(half).wait_recv()
 
@@ -265,7 +272,7 @@
                 z_new = (zfull[me, half, i].astype(F32) + gate_s[half, i] * update).astype(BF16)
                 out_ref[i, :, lanes] = z_new
                 if heads:
-                    stage[0, pl.ds(pl.multiple_of((half * rows + i) * 8, 8), 8), :] = dot_nn(bias_t[layer], layer_norm_t(z_new))
+                    stage[0, pl.ds(pl.multiple_of((half * rows + i) * 8, 8), heads), :] = dot_nn(bias_w, layer_norm_t(z_new))
 
     if heads:
         for half in range(2):
@@ -406,6 +413,8 @@
             src_ref=z_nat.at[pl.ds(TURN * t, TURN), pl.ds(pl.multiple_of(to * rows, rows), rows), :], dst_ref=r_buf.at[source, pl.ds(TURN * t, TURN)],
             send_sem=t_send.at[p - 1], recv_sem=t_recv.at[p - 1], device_id={'dap': target}, device_id_type=MESH)
 
+    bias_w = bias_rows(bias_t[layer]) if share else None
+
     def one_row(i):
         keys = k_s[i]
         parts = []
@@ -435,27 +444,30 @@
                 second = dot_nn(pt_in_t[hidden + part:hidden + part + channels, :], normed)
                 update = update + dot_nn(pt_out_t[:, part:part + channels], (first * sigmoid(first) * second).astype(BF16))
             z_row = (z_row.astype(F32) + update).astype(BF16)
+
         z_nat[i] = z_row.T
-
         if share:
-            bias_s[0, pl.ds(pl.multiple_of(i * 8, 8), 8), :], bias_s[1, pl.ds(pl.multiple_of(i * 8, 8), 8), :] = jnp.split(dot_nn(bias_t[layer], layer_norm_t(z_row)), 2, axis=1)
+            slab = dot_nn(bias_w, layer_norm_t(z_row))
+            for half in range(2):
+                bias_s[half, pl.ds(pl.multiple_of(i * 8, 8), heads), :] = slab[:, half * LANES:(half + 1) * LANES]
 
 
     @pl.loop(0, rows // 2)
     def _(step):
         for t in range(2):
             one_row(2 * step + t)
-        i = 2 * step + 2 - 1
-
-        @pl.when((lax.rem(i, TURN) == TURN - 1) & (i > TURN))
+        late = 0 if share else 1
+
+        @pl.when(step >= late)
         def _():
             for p in range(1, n_dev):
-                turn_copy(me, i // TURN - 1, p, peers[p - 1], peers[p - 1]).start()
+                turn_copy(me, step - late, p, peers[p - 1], peers[p - 1]).start()
 
     own = pltpu.make_async_copy(z_nat.at[:, pl.ds(spot, rows), :], r_buf.at[me], own_sem)
     own.start()
-    for p in range(1, n_dev):
-        turn_copy(me, rows // TURN - 1, p, peers[p - 1], peers[p - 1]).start()
+    if not share:
+        for p in range(1, n_dev):
+            turn_copy(me, rows // TURN - 1, p, peers[p - 1], peers[p - 1]).start()
     own.wait()
 
     def whole(source, p, target):
@@ -482,9 +494,10 @@
         place(source)
 
     if not last:
-        @pl.loop(0, rows)
-        def _(j):
-            out_ref[j] = q_all[j].T
+        @pl.loop(0, rows // 4)
+        def _(group):
+            for t in range(4):
+                out_ref[group * 4 + t] = q_all[group * 4 + t].T
 
     for p in range(1, n_dev):
         whole(me, p, peers[p - 1]).wait_send()
@@ -540,15 +553,9 @@
     )(z, mask, w_qkvg, bias_own, w_out, *pt, *((kv, bias_t) if share else ()))
 
 
-def single_inputs(single, w_qkvg):
-    width = w_qkvg.shape[1] // 4
-    projected = jnp.dot(layer_norm(single), w_qkvg, preferred_element_type=F32)
-    return projected[:, :width].astype(BF16), projected[:, width:3 * width].astype(BF16), jax.nn.sigmoid(projected[:, 3 * width:])
-
-
-def single_kernel(layer, natural, z_ref, s_ref, q_ref, gate_ref, kv_ref, mask_ref, bias_t, w_out, w_in, w_back, out_ref, bias_s, q_s, o_s, merged_s):
+def single_kernel(layer, natural, z_ref, s_ref, proj_ref, kv_ref, mask_ref, bias_t, w_out, w_in, w_back, out_ref, bias_s, q_s, o_s, merged_s):
     heads = bias_t.shape[1]
-    rows, width = q_ref.shape
+    rows, width = s_ref.shape[0], kv_ref.shape[1] // 2
     head_dim = width // heads
     lane = lax.broadcasted_iota(jnp.int32, (heads, width), 1)
     head = lax.broadcasted_iota(jnp.int32, (heads, width), 0)
@@ -561,7 +568,7 @@
             spot = pl.ds(pl.multiple_of(i * heads, heads), heads)
             slab = dot_nt(bias_t[layer], layer_norm(z_ref[i])) if natural else dot_nn(bias_t[layer], layer_norm_t(z_ref[i]))
             bias_s[spot, :] = slab.astype(BF16)
-            q_s[spot, :] = (q_ref[pl.ds(i, 1), :] * own_head).astype(BF16)
+            q_s[spot, :] = (proj_ref[pl.ds(i, 1), :width] * own_head).astype(BF16)
 
     key_bias = (jnp.concatenate([mask_ref[half * LANES:(half + 1) * LANES, :].T[:1, :] for half in range(2)], axis=1) - 1.0) * NEG_BIG
     logits = dot_nt(q_s[...], kv_ref[:, :width]) * head_dim ** -0.5 + bias_s[...].astype(F32) + key_bias
@@ -573,7 +580,7 @@
     def _(i):
         merged_s[pl.ds(i, 1), :] = jnp.sum(o_s[pl.ds(pl.multiple_of(i * heads, heads), heads), :] * own_head, axis=0, keepdims=True)
 
-    merged = (merged_s[...] * gate_ref[...]).astype(BF16)
+    merged = (merged_s[...] * sigmoid(proj_ref[:, 3 * width:])).astype(BF16)
     single = (s_ref[...].astype(F32) + dot_nn(merged, w_out[layer])).astype(BF16)
     normed = layer_norm(single)
     hidden = w_back.shape[1]
@@ -586,14 +593,14 @@
     out_ref[...] = (single.astype(F32) + update).astype(BF16)
 
 
-def single_step(layer, natural, single, query, gate, kv_all, pair, mask, bias_t, w_out, st_in, st_out):
-    rows, width = query.shape
+def single_step(layer, natural, single, projected, kv_all, pair, mask, bias_t, w_out, st_in, st_out):
+    rows, width = single.shape[0], kv_all.shape[1] // 2
     heads = bias_t.shape[1]
     vmem = pl.BlockSpec(memory_space=pltpu.VMEM)
     return pl.pallas_call(
         functools.partial(single_kernel, layer, natural),
         out_shape=jax.ShapeDtypeStruct(single.shape, BF16),
-        in_specs=[vmem] * 10,
+        in_specs=[vmem] * 9,
         out_specs=vmem,
         scratch_shapes=[
             pltpu.VMEM((rows * heads, kv_all.shape[0]), BF16),
@@ -603,7 +610,7 @@
         ],
         compiler_params=pltpu.CompilerParams(vmem_limit_bytes=VMEM_LIMIT),
         name=f'single_step_{layer}',
-    )(pair, single, query.astype(F32), gate, kv_all, mask, bias_t, w_out, st_in, st_out)
+    )(pair, single, projected, kv_all, mask, bias_t, w_out, st_in, st_out)
 
 
 def solution(mesh):
@@ -618,26 +625,23 @@
         mask = jnp.broadcast_to(token_mask.astype(F32)[:, None], (token_mask.shape[0], LANES))
         heads = w['tas_bias'].shape[2]
 
-        def bias_rows(name):
-            swapped = jnp.swapaxes(w[name], 1, 2)
-            return jnp.pad(swapped, ((0, 0), (0, 8 - heads), (0, 0)))
-
-        tas_bias, tae_bias = bias_rows('tas_bias'), bias_rows('tae_bias')
         ap_bias = jnp.swapaxes(w['ap_bias'], 1, 2)
         pair = jnp.swapaxes(pair, 1, 2)
         for b in range(blocks):
             cid = 4 * b
             last = b == blocks - 1
-            query, kv, gate = single_inputs(single, w['ap_qkvg'][b])
+            projected = jnp.dot(layer_norm(single), w['ap_qkvg'][b], preferred_element_type=F32)
+            width = projected.shape[1] // 4
+            kv = projected[:, width:3 * width].astype(BF16)
             out = ('row', b, n_dev, cid, b == 0, pair, mask, w['tmo_proj'], w['tmo_gate'], w['tmo_out'])
             if b == 0:
                 pair, mask = tri_mult(*out)
             else:
                 pair, = tri_mult(*out)
-            pair, bias = tri_mult('col', b, n_dev, cid + 1, False, pair, mask, w['tmi_proj'], w['tmi_gate'], w['tmi_out'], tas_bias, heads)
-            pair, kv_all, bias = tri_att(b, n_dev, cid + 2, False, pair, mask, w['tas_qkvg'], bias, w['tas_out'], (), kv, tae_bias)
+            pair, bias = tri_mult('col', b, n_dev, cid + 1, False, pair, mask, w['tmi_proj'], w['tmi_gate'], w['tmi_out'], w['tas_bias'], heads)
+            pair, kv_all, bias = tri_att(b, n_dev, cid + 2, False, pair, mask, w['tas_qkvg'], bias, w['tas_out'], (), kv, w['tae_bias'])
             pair = tri_att(b, n_dev, cid + 3, last, pair, mask, w['tae_qkvg'], bias, w['tae_out'], (w['pt_in'], w['pt_out']))
-            single = single_step(b, last, single, query, gate, kv_all, pair, mask, ap_bias, w['ap_out'], w['st_in'], w['st_out'])
+            single = single_step(b, last, single, projected, kv_all, pair, mask, ap_bias, w['ap_out'], w['st_in'], w['st_out'])
         return single, pair
 
     return jax.shard_map(local_program, mesh=mesh, in_specs=(single_spec, pair_spec, row_spec) + (P(),) * len(WEIGHT_NAMES), out_specs=(single_spec, pair_spec), check_vma=False)

time: 693 us -> 683 us (0.986)
  Pallas kernels: 677 us -> 669 us
    pallas_call x4, Pallas kernels: 231 us -> 222 us  [tri_att(): pl.pallas_call(functools.partial(tri_att_kernel, layer, n_dev, heads, las...]
where the time goes in v6:
time: 683 us
  Pallas kernels  669 us (98%)
  local copies, waits for them, and re-layouts  8.06 us (1%)
    pallas_call x4, Pallas kernels, tri_mult(): pl.pallas_call(functools.partial(tri_mult_kernel, kind, layer, n_dev, fir...  429 us
    pallas_call x4, Pallas kernels, tri_att(): pl.pallas_call(functools.partial(tri_att_kernel, layer, n_dev, heads, las...  222 us
    pallas_call x2, Pallas kernels, single_step(): pl.pallas_call(functools.partial(single_kernel, layer, natural), out_shap...  17.4 us

profile of v6, /device:TPU:21, one launch (start us, length us, event | category | flops | bytes accessed | tf_op | source)
XLA Modules:
  0.0 682.6 jit_solution(6961373709152986007)
XLA Ops:
  0.6 0.7 convert_element_type.17
  1.3 0.8 convert_reduce_fusion.1
  2.1 0.9 fusion.12
  3.0 0.7 broadcast_in_dim.2.mask_ref
  3.7 1.4 copy.25.rest_0_
  5.1 1.4 copy.26.rest_1_
  6.5 1.6 fusion.2.proj_ref
  8.1 0.0 copy-start.2
  8.1 0.7 slice.31.rest_0_
  8.8 2.3 copy.24
  11.0 113.0 %tri_mult_row_0.1 = (bf16[16,128,256]{2,1,0:T(8,128)(2,1)}, f32[256,128]{1,0:T(8,128)}) custom-call(bf16[16,128,256]{2,1,0:T(8,128)(2,1)} %bitcast.8, f32[16,128]{1,0:T(8,128)} %broadcast_in_dim.2.mask_ref, bf16[2,128,512]{2,1,0:T(8,128)(2,1)} %w_proj.6, bf16[2,128,128]{2,1,0:T(8,128)(2,1)} %w_gate.6, bf16[2,128,128]{2,1,0:T(8,128)(2,1)} %w_out.14), custom_call_target="tpu_custom_call" | custom-call | tf_op jit(solution)/shard_map/tri_mult_row_0/pallas_call | solution.py:306
  124.1 107.1 %tri_mult_col_1.1 = (bf16[16,128,256]{2,1,0:T(8,128)(2,1)}, bf16[4,16,256]{2,1,0:T(8,128)(2,1)}) custom-call(bf16[16,128,256]{2,1,0:T(8,128)(2,1)} %get-tuple-element.14.z_hbm, f32[256,128]{1,0:T(8,128)} %get-tuple-element.15.mask_ref, bf16[2,128,512]{2,1,0:T(8,128)(2,1)} %w_proj.7, bf16[2,128,128]{2,1,0:T(8,128)(2,1)} %w_gate.7, ...), custom_call_target="tpu_custom_call" | custom-call | tf_op jit(solution)/shard_map/tri_mult_col_1/pallas_call | solution.py:306
  231.2 0.0 copy-done.2
  231.2 51.9 %tri_att_2.1 = (bf16[16,128,256]{2,1,0:T(8,128)(2,1)}, bf16[256,768]{1,0:T(8,128)(2,1)}, bf16[4,16,256]{2,1,0:T(8,128)(2,1)}) custom-call(bf16[16,128,256]{2,1,0:T(8,128)(2,1)} %get-tuple-element.16.z_ref, f32[256,128]{1,0:T(8,128)} %get-tuple-element.15.mask_ref, bf16[2,128,512]{2,1,0:T(8,128)(2,1)} %w_qkvg.6, ...), custom_call_target="tpu_custom_call" | custom-call | tf_op jit(solution)/shard_map/tri_att_2/pallas_call | solution.py:545
  283.2 59.9 %tri_att_3.1.z_hbm.z_ref = bf16[16,128,256]{2,1,0:T(8,128)(2,1)} custom-call(bf16[16,128,256]{2,1,0:T(8,128)(2,1)} %get-tuple-element.18.z_ref, f32[256,128]{1,0:T(8,128)} %get-tuple-element.15.mask_ref, bf16[2,128,512]{2,1,0:T(8,128)(2,1)} %w_qkvg.7, bf16[4,16,256]{2,1,0:T(8,128)(2,1)} %get-tuple-element.19.bias_own, bf16[2,128,128]{2,1,0:T(8,128)(2,1)} %w_out.18, ...), custom_call_target="tpu_custom_call" | custom-call | tf_op jit(solution)/shard_map/tri_att_3/pallas_call | solution.py:545
  343.1 8.1 %single_step_0.1.s_ref = bf16[16,384]{1,0:T(8,128)(2,1)} custom-call(bf16[16,128,256]{2,1,0:T(8,128)(2,1)} %tri_att_3.1.z_hbm.z_ref, bf16[16,384]{1,0:T(8,128)(2,1)} %s_ref.1, f32[16,1536]{1,0:T(8,128)} %copy-done.2, bf16[256,768]{1,0:T(8,128)(2,1)} %get-tuple-element.22.kv_ref, f32[256,128]{1,0:T(8,128)} %get-tuple-element.15.mask_ref, ...), custom_call_target="tpu_custom_call" | custom-call | tf_op jit(solution)/shard_map/single_step_0/pallas_call | solution.py:600
  351.2 0.0 copy-start.4
  351.2 0.0 copy-start.1
  351.2 102.6 %tri_mult_row_4.1.z_hbm = bf16[16,128,256]{2,1,0:T(8,128)(2,1)} custom-call(bf16[16,128,256]{2,1,0:T(8,128)(2,1)} %tri_att_3.1.z_hbm.z_ref, f32[256,128]{1,0:T(8,128)} %get-tuple-element.15.mask_ref, bf16[2,128,512]{2,1,0:T(8,128)(2,1)} %w_proj.6, bf16[2,128,128]{2,1,0:T(8,128)(2,1)} %w_gate.6, bf16[2,128,128]{2,1,0:T(8,128)(2,1)} %w_out.14), custom_call_target="tpu_custom_call" | custom-call | tf_op jit(solution)/shard_map/tri_mult_row_4/pallas_call | solution.py:306
  453.8 106.6 %tri_mult_col_5.1 = (bf16[16,128,256]{2,1,0:T(8,128)(2,1)}, bf16[4,16,256]{2,1,0:T(8,128)(2,1)}) custom-call(bf16[16,128,256]{2,1,0:T(8,128)(2,1)} %tri_mult_row_4.1.z_hbm, f32[256,128]{1,0:T(8,128)} %get-tuple-element.15.mask_ref, bf16[2,128,512]{2,1,0:T(8,128)(2,1)} %w_proj.7, bf16[2,128,128]{2,1,0:T(8,128)(2,1)} %w_gate.7, bf16[2,128,128]{2,1,0:T(8,128)(2,1)} %w_out.15, ...), custom_call_target="tpu_custom_call" | custom-call | tf_op jit(solution)/shard_map/tri_mult_col_5/pallas_call | solution.py:306
  560.5 0.0 copy-done.4
  560.5 0.1 convert_reduce_fusion
  560.6 0.2 fusion.10
  560.8 0.0 copy-done.1
  560.8 0.3 fusion.proj_ref
  561.1 0.0 copy-start.3
  561.1 0.6 slice.30.rest_0_
  561.8 51.2 %tri_att_6.1 = (bf16[16,128,256]{2,1,0:T(8,128)(2,1)}, bf16[256,768]{1,0:T(8,128)(2,1)}, bf16[4,16,256]{2,1,0:T(8,128)(2,1)}) custom-call(bf16[16,128,256]{2,1,0:T(8,128)(2,1)} %get-tuple-element.20.z_ref, f32[256,128]{1,0:T(8,128)} %get-tuple-element.15.mask_ref, bf16[2,128,512]{2,1,0:T(8,128)(2,1)} %w_qkvg.6, ...), custom_call_target="tpu_custom_call" | custom-call | tf_op jit(solution)/shard_map/tri_att_6/pallas_call | solution.py:545
  613.0 59.3 %tri_att_7.1.z_ref = bf16[16,256,128]{2,1,0:T(8,128)(2,1)} custom-call(bf16[16,128,256]{2,1,0:T(8,128)(2,1)} %get-tuple-element.23.z_ref, f32[256,128]{1,0:T(8,128)} %get-tuple-element.15.mask_ref, bf16[2,128,512]{2,1,0:T(8,128)(2,1)} %w_qkvg.7, bf16[4,16,256]{2,1,0:T(8,128)(2,1)} %get-tuple-element.24.bias_own, bf16[2,128,128]{2,1,0:T(8,128)(2,1)} %w_out.18, ...), custom_call_target="tpu_custom_call" | custom-call | tf_op jit(solution)/shard_map/tri_att_7/pallas_call | solution.py:545
  672.3 0.0 copy-done.3
  672.3 0.0 copy-start
  672.4 9.3 %single_step_1.1 = bf16[16,384]{1,0:T(8,128)(2,1)} custom-call(bf16[16,256,128]{2,1,0:T(8,128)(2,1)} %tri_att_7.1.z_ref, bf16[16,384]{1,0:T(8,128)(2,1)} %single_step_0.1.s_ref, f32[16,1536]{1,0:T(8,128)} %copy-done.3, bf16[256,768]{1,0:T(8,128)(2,1)} %get-tuple-element.25.kv_ref, f32[256,128]{1,0:T(8,128)} %get-tuple-element.15.mask_ref, ...), custom_call_target="tpu_custom_call" | custom-call | tf_op jit(solution)/shard_map/single_step_1/pallas_call | solution.py:600
  681.6 0.0 copy-done
  681.6 1.0 copy.30
  (4 shorter events, 0.0 us)
Async XLA Ops:
  8.1 223.1 %copy-start.2 = (f32[16,1536]{1,0:T(8,128)}, f32[16,1536]{1,0:T(8,128)S(1)}, u32[]{:S(2)}) copy-start(f32[16,1536]{1,0:T(8,128)S(1)} %fusion.2.proj_ref) | copy-start | bytes 294916
  351.2 209.3 %copy-start.4 = (bf16[16,384]{1,0:T(8,128)(2,1)S(1)}, bf16[16,384]{1,0:T(8,128)(2,1)}, u32[]{:S(2)}) copy-start(bf16[16,384]{1,0:T(8,128)(2,1)} %single_step_0.1.s_ref) | copy-start | bytes 36868
  351.2 209.6 %copy-start.1 = (bf16[2,384,1536]{2,1,0:T(8,128)(2,1)S(1)}, bf16[2,384,1536]{2,1,0:T(8,128)(2,1)}, u32[]{:S(2)}) copy-start(bf16[2,384,1536]{2,1,0:T(8,128)(2,1)} %param.39) | copy-start | bytes 7077892
  561.1 111.2 %copy-start.3 = (f32[16,1536]{1,0:T(8,128)}, f32[16,1536]{1,0:T(8,128)S(1)}, u32[]{:S(2)}) copy-start(f32[16,1536]{1,0:T(8,128)S(1)} %fusion.proj_ref) | copy-start | bytes 294916
  672.3 9.3 %copy-start = (bf16[16,256,128]{2,1,0:T(8,128)(2,1)S(1)}, bf16[16,256,128]{2,1,0:T(8,128)(2,1)}, u32[]{:S(2)}) copy-start(bf16[16,256,128]{2,1,0:T(8,128)(2,1)} %tri_att_7.1.z_ref) | copy-start | bytes 3145732
